TPU v7x, 32 devices: a whole 2x2x4 slice. The times are simulated.
32 devices in a mesh: leaf: 16 (over z, x, core), head: 2 (over y).
Axes of the slice: x: 2, y: 2, z: 4, core: 2. Of those that a mesh axis runs over, the one named last changes fastest.
Arguments:
- queries: bfloat16 [4096, 2048], P(('leaf', 'head')), may hold values from -64 to 64
- keys: bfloat16 [4096, 256], P(('leaf', 'head')), may hold values from -16 to 16
- values: bfloat16 [4096, 256], P(('leaf', 'head')), may hold values from -6 to 6
- output_gradient: bfloat16 [4096, 2048], P('leaf', 'head'), may hold values from -6 to 6
- parents: int32 [16], replicated, may hold values from -1 to 15, as said below
Outputs:
- attended: bfloat16 [4096, 2048], P('leaf', 'head')
- query_gradient: bfloat16 [4096, 2048], P(('leaf', 'head'))
- key_grad: bfloat16 [4096, 256], P(('leaf', 'head'))
- value_grad: bfloat16 [4096, 256], P(('leaf', 'head'))
Inputs may be any that keep to these rules, and one draw needn't show every extreme that they name: Exactly one group has parent -1; every other group's parent is another group, and following parents from any group reaches that root after at most 6 steps; some group is exactly 6 steps from it.
All inputs are finite; a program needn't handle non-finite values.
Results may differ from a plain program's by a relative error of at most 0.035.
Values may be sent and summed in bfloat16 or wider, within the bound.
No kernel may reach another device: no remote copies, remote signals or barrier semaphores. Data moves between devices by JAX's collectives and lax.ppermute only.
A program may use at most 64 MiB of HBM per device.

v0:
```python
import math

import jax
import jax.numpy as jnp
from jax import lax
from jax.sharding import PartitionSpec as P

HEAD_SIZE = 128
NODE_TOKENS = 128
MAX_DEPTH = 6


masked_score = -1e30


def ancestor_slots(parents, my_group, group_count):
    indices = jnp.arange(group_count, dtype=jnp.int32)
    current = jnp.sum(jnp.where(indices == my_group, parents, 0))
    columns = []
    for level in range(MAX_DEPTH):
        columns.append(current)
        following = jnp.sum(jnp.where(indices == current, parents, 0))
        current = jnp.where(current >= 0, following, -1)
    return jnp.stack(columns)


def causal_mask(length):
    positions = jnp.arange(length, dtype=jnp.int32)
    return positions[:, None] >= positions[None, :]


def own_scores(query5, key_block, scaling):
    scores = (
        jnp.einsum("jrcgd,jkcd->jrcgk", query5, key_block, preferred_element_type=jnp.float32)
        * scaling
    )
    causal = causal_mask(key_block.shape[1])
    return jnp.where(causal[None, :, None, None, :], scores, masked_score)


def own_stats(query5, key_block, scaling, row_count):
    scores = own_scores(query5, key_block, scaling)
    top_score = jnp.max(scores, axis=-1)
    weight_sum = jnp.sum(jnp.exp(scores - top_score[..., None]), axis=-1)
    leading = (row_count,) + top_score.shape[2:]
    return (top_score.reshape(leading), weight_sum.reshape(leading))


def trunk_stats(running, query4, trunk_key, scaling):
    top_score, weight_sum = running
    kv_count = query4.shape[1]
    key3 = trunk_key.reshape(-1, kv_count, query4.shape[3])
    scores = (
        jnp.einsum("rcgd,kcd->rcgk", query4, key3, preferred_element_type=jnp.float32) * scaling
    )
    new_top = jnp.maximum(top_score, jnp.max(scores, axis=-1))
    weight_sum = weight_sum * jnp.exp(top_score - new_top) + jnp.sum(
        jnp.exp(scores - new_top[..., None]), axis=-1
    )
    return (new_top, weight_sum)


def return_trunks(parts, slots, key_local, value_local, group_count):
    width = key_local.shape[1]
    guarded_value = jnp.maximum(slots, 0)
    store = jnp.zeros((group_count * NODE_TOKENS, parts.shape[2]), jnp.float32)
    for slot_index in range(MAX_DEPTH):
        segment = lax.dynamic_slice_in_dim(
            store, guarded_value[slot_index] * NODE_TOKENS, NODE_TOKENS, 0
        )
        store = lax.dynamic_update_slice_in_dim(
            store, segment + parts[slot_index], guarded_value[slot_index] * NODE_TOKENS, 0
        )
    back_parts = lax.all_to_all(store, "leaf", split_axis=0, concat_axis=0, tiled=True)
    arriving = jnp.sum(back_parts.reshape(group_count, NODE_TOKENS, -1), axis=0)
    key_total = key_local.at[:NODE_TOKENS].add(arriving[:, :width])
    value_total = value_local.at[:NODE_TOKENS].add(arriving[:, width:])
    return (key_total.astype(jnp.bfloat16), value_total.astype(jnp.bfloat16))


def per_device(queries, keys, values, output_gradient, parents):
    heads_query, heads_key, heads_value = (
        lax.all_to_all(queries, "head", split_axis=1, concat_axis=0, tiled=True),
        lax.all_to_all(keys, "head", split_axis=1, concat_axis=0, tiled=True),
        lax.all_to_all(values, "head", split_axis=1, concat_axis=0, tiled=True),
    )
    row_count = heads_query.shape[0]
    node_count = row_count // NODE_TOKENS
    kv_count = heads_key.shape[1] // HEAD_SIZE
    per_key = heads_query.shape[1] // (kv_count * HEAD_SIZE)
    scaling = 1.0 / math.sqrt(HEAD_SIZE)
    group_count = lax.axis_size("leaf")
    my_group = lax.axis_index("leaf")
    slots = ancestor_slots(parents, my_group, group_count)
    usable = slots >= 0
    guarded_value = jnp.maximum(slots, 0)
    query4 = heads_query.reshape(row_count, kv_count, per_key, HEAD_SIZE)
    grad4 = output_gradient.reshape(row_count, kv_count, per_key, HEAD_SIZE)
    query5 = heads_query.reshape(node_count, NODE_TOKENS, kv_count, per_key, HEAD_SIZE)
    grad5 = output_gradient.reshape(node_count, NODE_TOKENS, kv_count, per_key, HEAD_SIZE)
    key_block = heads_key.reshape(node_count, NODE_TOKENS, kv_count, HEAD_SIZE)
    value_block = heads_value.reshape(node_count, NODE_TOKENS, kv_count, HEAD_SIZE)
    stem_keys = heads_key[:NODE_TOKENS]
    stem_values = heads_value[:NODE_TOKENS]
    start_state = own_stats(query5, key_block, scaling, row_count)
    all_keys, all_values = (
        lax.all_gather(stem_keys, "leaf", axis=0, tiled=True),
        lax.all_gather(stem_values, "leaf", axis=0, tiled=True),
    )
    ancestor_keys = jnp.stack(
        [
            lax.dynamic_slice_in_dim(
                all_keys, guarded_value[slot_index] * NODE_TOKENS, NODE_TOKENS, 0
            )
            for slot_index in range(MAX_DEPTH)
        ]
    )
    ancestor_values = jnp.stack(
        [
            lax.dynamic_slice_in_dim(
                all_values, guarded_value[slot_index] * NODE_TOKENS, NODE_TOKENS, 0
            )
            for slot_index in range(MAX_DEPTH)
        ]
    )

    def stats_step(state, inputs):
        trunk_key, usable_now = inputs
        updated = trunk_stats(state, query4, trunk_key, scaling)
        return (
            jax.tree.map(lambda fresh, stale: jnp.where(usable_now, fresh, stale), updated, state),
            None,
        )

    running, unused = lax.scan(stats_step, start_state, (ancestor_keys, usable))
    top_score, weight_sum = running
    top5 = top_score.reshape(node_count, NODE_TOKENS, kv_count, per_key)
    sum5 = weight_sum.reshape(node_count, NODE_TOKENS, kv_count, per_key)
    scores = own_scores(query5, key_block, scaling)
    weights = jnp.exp(scores - top5[..., None]) / sum5[..., None]
    weights_b = weights.astype(jnp.bfloat16)
    summed_own = jnp.einsum(
        "jrcgk,jkcd->jrcgd", weights_b, value_block, preferred_element_type=jnp.float32
    ).reshape(row_count, kv_count, per_key, HEAD_SIZE)

    def trunk_probs(trunk_key):
        key3 = trunk_key.reshape(-1, kv_count, HEAD_SIZE)
        trunk_scores = (
            jnp.einsum("rcgd,kcd->rcgk", query4, key3, preferred_element_type=jnp.float32) * scaling
        )
        return jnp.exp(trunk_scores - top_score[..., None]) / weight_sum[..., None]

    def value_step(total, inputs):
        trunk_key, trunk_value, usable_now = inputs
        probs_b = trunk_probs(trunk_key).astype(jnp.bfloat16)
        value3 = trunk_value.reshape(-1, kv_count, HEAD_SIZE)
        addition = jnp.einsum("rcgk,kcd->rcgd", probs_b, value3, preferred_element_type=jnp.float32)
        return (total + jnp.where(usable_now, addition, 0.0), None)

    summed, unused = lax.scan(value_step, summed_own, (ancestor_keys, ancestor_values, usable))
    attended4 = summed.astype(jnp.bfloat16)
    attended = attended4.reshape(row_count, -1)
    row_delta = jnp.sum(grad4.astype(jnp.float32) * attended4.astype(jnp.float32), axis=-1)
    delta5 = row_delta.reshape(node_count, NODE_TOKENS, kv_count, per_key)
    prob_grad = jnp.einsum(
        "jrcgd,jkcd->jrcgk", grad5, value_block, preferred_element_type=jnp.float32
    )
    dscore_b = (weights * (prob_grad - delta5[..., None])).astype(jnp.bfloat16)
    query_own = jnp.einsum(
        "jrcgk,jkcd->jrcgd", dscore_b, key_block, preferred_element_type=jnp.float32
    )
    key_local = (
        jnp.einsum("jrcgk,jrcgd->jkcd", dscore_b, query5, preferred_element_type=jnp.float32)
        * scaling
    ).reshape(row_count, -1)
    value_local = jnp.einsum(
        "jrcgk,jrcgd->jkcd", weights_b, grad5, preferred_element_type=jnp.float32
    ).reshape(row_count, -1)

    def backward_step(query_acc, inputs):
        trunk_key, trunk_value, usable_now = inputs
        key3 = trunk_key.reshape(-1, kv_count, HEAD_SIZE)
        value3 = trunk_value.reshape(-1, kv_count, HEAD_SIZE)
        trunk_weights = trunk_probs(trunk_key)
        trunk_weights_b = trunk_weights.astype(jnp.bfloat16)
        trunk_prob_grad = jnp.einsum(
            "rcgd,kcd->rcgk", grad4, value3, preferred_element_type=jnp.float32
        )
        trunk_dscore = (trunk_weights * (trunk_prob_grad - row_delta[..., None])).astype(
            jnp.bfloat16
        )
        addition = jnp.einsum(
            "rcgk,kcd->rcgd", trunk_dscore, key3, preferred_element_type=jnp.float32
        )
        query_acc = query_acc + jnp.where(usable_now, addition, 0.0)
        key_portion = (
            jnp.einsum("rcgk,rcgd->kcd", trunk_dscore, query4, preferred_element_type=jnp.float32)
            * scaling
        )
        value_portion = jnp.einsum(
            "rcgk,rcgd->kcd", trunk_weights_b, grad4, preferred_element_type=jnp.float32
        )
        joined = jnp.concatenate(
            [key_portion.reshape(NODE_TOKENS, -1), value_portion.reshape(NODE_TOKENS, -1)], axis=1
        )
        return (query_acc, jnp.where(usable_now, joined, 0.0))

    query_acc, parts = lax.scan(
        backward_step,
        query_own.reshape(row_count, kv_count, per_key, HEAD_SIZE),
        (ancestor_keys, ancestor_values, usable),
    )
    query_gradient = (query_acc * scaling).astype(jnp.bfloat16).reshape(row_count, -1)
    key_grad, value_grad = return_trunks(parts, slots, key_local, value_local, group_count)
    query_home, key_home, value_home = (
        lax.all_to_all(query_gradient, "head", split_axis=0, concat_axis=1, tiled=True),
        lax.all_to_all(key_grad, "head", split_axis=0, concat_axis=1, tiled=True),
        lax.all_to_all(value_grad, "head", split_axis=0, concat_axis=1, tiled=True),
    )
    return (attended, query_home, key_home, value_home)


def solution(mesh):
    placed = (
        P(("leaf", "head"), None),
        P(("leaf", "head"), None),
        P(("leaf", "head"), None),
        P("leaf", "head"),
        P(),
    )
    return jax.shard_map(
        per_device,
        mesh=mesh,
        in_specs=placed,
        out_specs=(
            P("leaf", "head"),
            P(("leaf", "head"), None),
            P(("leaf", "head"), None),
            P(("leaf", "head"), None),
        ),
        check_vma=False,
    )
```

profile of v0, /device:TPU:10, one launch (start us, length us, event | category | flops | bytes accessed | tf_op | source)
XLA Modules:
  0.0 267.4 jit_solution(7567391121609102019)
XLA Ops:
  2.4 3.3 %all-to-all-start = ((bf16[128,2,128]{2,0,1:T(8,128)(2,1)}), bf16[128,2,128]{2,0,1:T(8,128)(2,1)S(1)}, u32[]{:S(2)}, u32[]{:S(2)}) async-start(bf16[128,2,128]{2,0,1:T(8,128)(2,1)} %copy.134), calls=%async_computation | async-start | bytes 131072 | tf_op jit(solution)/shard_map/all_to_all | solution.py:84
  7.0 1.9 fusion.85
  20.6 3.3 %all-to-all-start.2 = ((bf16[128,2,128]{2,0,1:T(8,128)(2,1)}), bf16[128,2,128]{2,0,1:T(8,128)(2,1)S(1)}, u32[]{:S(2)}, u32[]{:S(2)}) async-start(bf16[128,2,128]{2,0,1:T(8,128)(2,1)} %copy.140), calls=%async_computation.2 | async-start | bytes 131072 | tf_op jit(solution)/shard_map/all_to_all | solution.py:85
  28.3 2.0 copy.135
  31.4 3.5 %all-to-all-start.1 = ((bf16[128,2,1024]{0,2,1:T(8,128)(2,1)}), bf16[128,2,1024]{0,2,1:T(8,128)(2,1)S(1)}, u32[]{:S(2)}, u32[]{:S(2)}) async-start(bf16[128,2,1024]{0,2,1:T(8,128)(2,1)} %bitcast.54), calls=%async_computation.1 | async-start | bytes 1048576 | tf_op jit(solution)/shard_map/all_to_all | solution.py:83
  35.0 16.6 %all-gather.1 = bf16[1,2048,128]{2,1,0:T(8,128)(2,1)S(1)} all-gather(bf16[1,128,128]{2,1,0:T(8,128)(2,1)S(1)} %slice.132), channel_id=3, replica_groups=mesh['leaf'=16,'head'=2] {'leaf'}, dimensions={1}, use_global_device_ids=true | all-gather | bytes 557056 | tf_op jit(solution)/shard_map/all_gather | solution.py:108
  51.5 22.8 %all-gather = bf16[1,2048,128]{2,1,0:T(8,128)(2,1)S(1)} all-gather(bf16[1,128,128]{2,1,0:T(8,128)(2,1)S(1)} %slice.131), channel_id=2, replica_groups=mesh['leaf'=16,'head'=2] {'leaf'}, dimensions={1}, use_global_device_ids=true | all-gather | bytes 557056 | tf_op jit(solution)/shard_map/all_gather | solution.py:107
  82.2 15.2 %while.36 = (s32[]{:T(128)}, f32[256,1,8]{0,2,1:T(8,128)S(1)}, f32[256,1,8]{0,2,1:T(8,128)S(1)}, pred[6]{0:T(512)(128)(4,1)S(1)}, bf16[6,128,128]{2,1,0:T(8,128)...) while((s32[]{:T(128)}, f32[256,1,8]{0,2,1:T(8,128)S(1)}, f32[256,1,8]{0,2,1:T(8,128)S(1)}, ...), condition=%wide.region_11.12_spmd, body=%wide.region_8.11_spmd.sunk | while | flops 68167680 | bytes 2752608 | solution.py:135
  99.4 2.6 copy.143
  102.0 24.4 %while.37 = (s32[]{:T(128)}, f32[256,1,8,128]{0,3,2,1:T(8,128)}, pred[6]{0:T(512)(128)(4,1)S(1)}, bf16[6,128,128]{2,1,0:T(8,128)(2,1)}, bf16[6,128,128]{2,1,0:T(...) while((s32[]{:T(128)}, f32[256,1,8,128]{0,3,2,1:T(8,128)}, ...), condition=%wide.region_13.14_spmd, body=%wide.region_12.13_spmd.sunk | while | flops 135790592 | bytes 2705003 | solution.py:160
  102.6 3.5 %fusion.129 = f32[256,1,8,128]{0,3,2,1:T(8,128)} fusion(f32[256,1,8,128]{0,3,2,1:T(8,128)} %get-tuple-element.552, bf16[256,1,8,128]{3,0,2,1:T(8,128)(2,1)S(1)} %get-tuple-element.565, f32[256,8]{0,1:T(8,128)S(1)} %bitcast.429, f32[256,8]{0,1:T(8,128)S(1)} %bitcast.415, pred[]{:T(512)} %bitcast.378, bf16[6,128,128]{2,1,0:T(8,128)(2,1)} %get-tuple-element.564, ...), kind=kOutput, calls=%fused_computation.16.clone.1 | convolution fusion | flops 135790592 | bytes 2704896 | tf_op jit(solution)/shard_map/while/body/eval_jaxpr/rcgk,kcd->rcgd/dot_general | solution.py:157
  106.6 3.5 %fusion.129 = f32[256,1,8,128]{0,3,2,1:T(8,128)} fusion(f32[256,1,8,128]{0,3,2,1:T(8,128)} %get-tuple-element.552, bf16[256,1,8,128]{3,0,2,1:T(8,128)(2,1)S(1)} %get-tuple-element.565, f32[256,8]{0,1:T(8,128)S(1)} %bitcast.429, f32[256,8]{0,1:T(8,128)S(1)} %bitcast.415, pred[]{:T(512)} %bitcast.378, bf16[6,128,128]{2,1,0:T(8,128)(2,1)} %get-tuple-element.564, ...), kind=kOutput, calls=%fused_computation.16.clone.1 | convolution fusion | flops 135790592 | bytes 2704896 | tf_op jit(solution)/shard_map/while/body/eval_jaxpr/rcgk,kcd->rcgd/dot_general | solution.py:157
  110.7 3.5 %fusion.129 = f32[256,1,8,128]{0,3,2,1:T(8,128)} fusion(f32[256,1,8,128]{0,3,2,1:T(8,128)} %get-tuple-element.552, bf16[256,1,8,128]{3,0,2,1:T(8,128)(2,1)S(1)} %get-tuple-element.565, f32[256,8]{0,1:T(8,128)S(1)} %bitcast.429, f32[256,8]{0,1:T(8,128)S(1)} %bitcast.415, pred[]{:T(512)} %bitcast.378, bf16[6,128,128]{2,1,0:T(8,128)(2,1)} %get-tuple-element.564, ...), kind=kOutput, calls=%fused_computation.16.clone.1 | convolution fusion | flops 135790592 | bytes 2704896 | tf_op jit(solution)/shard_map/while/body/eval_jaxpr/rcgk,kcd->rcgd/dot_general | solution.py:157
  114.7 3.5 %fusion.129 = f32[256,1,8,128]{0,3,2,1:T(8,128)} fusion(f32[256,1,8,128]{0,3,2,1:T(8,128)} %get-tuple-element.552, bf16[256,1,8,128]{3,0,2,1:T(8,128)(2,1)S(1)} %get-tuple-element.565, f32[256,8]{0,1:T(8,128)S(1)} %bitcast.429, f32[256,8]{0,1:T(8,128)S(1)} %bitcast.415, pred[]{:T(512)} %bitcast.378, bf16[6,128,128]{2,1,0:T(8,128)(2,1)} %get-tuple-element.564, ...), kind=kOutput, calls=%fused_computation.16.clone.1 | convolution fusion | flops 135790592 | bytes 2704896 | tf_op jit(solution)/shard_map/while/body/eval_jaxpr/rcgk,kcd->rcgd/dot_general | solution.py:157
  118.8 3.5 %fusion.129 = f32[256,1,8,128]{0,3,2,1:T(8,128)} fusion(f32[256,1,8,128]{0,3,2,1:T(8,128)} %get-tuple-element.552, bf16[256,1,8,128]{3,0,2,1:T(8,128)(2,1)S(1)} %get-tuple-element.565, f32[256,8]{0,1:T(8,128)S(1)} %bitcast.429, f32[256,8]{0,1:T(8,128)S(1)} %bitcast.415, pred[]{:T(512)} %bitcast.378, bf16[6,128,128]{2,1,0:T(8,128)(2,1)} %get-tuple-element.564, ...), kind=kOutput, calls=%fused_computation.16.clone.1 | convolution fusion | flops 135790592 | bytes 2704896 | tf_op jit(solution)/shard_map/while/body/eval_jaxpr/rcgk,kcd->rcgd/dot_general | solution.py:157
  122.9 3.5 %fusion.129 = f32[256,1,8,128]{0,3,2,1:T(8,128)} fusion(f32[256,1,8,128]{0,3,2,1:T(8,128)} %get-tuple-element.552, bf16[256,1,8,128]{3,0,2,1:T(8,128)(2,1)S(1)} %get-tuple-element.565, f32[256,8]{0,1:T(8,128)S(1)} %bitcast.429, f32[256,8]{0,1:T(8,128)S(1)} %bitcast.415, pred[]{:T(512)} %bitcast.378, bf16[6,128,128]{2,1,0:T(8,128)(2,1)} %get-tuple-element.564, ...), kind=kOutput, calls=%fused_computation.16.clone.1 | convolution fusion | flops 135790592 | bytes 2704896 | tf_op jit(solution)/shard_map/while/body/eval_jaxpr/rcgk,kcd->rcgd/dot_general | solution.py:157
  126.3 2.2 multiply_reduce_fusion
  132.4 39.2 %while.38 = (s32[]{:T(128)}, f32[256,1,8,128]{0,3,2,1:T(8,128)S(1)}, f32[6,128,256]{2,1,0:T(8,128)}, pred[6]{0:T(512)(128)(4,1)S(1)}, bf16[6,128,128]{2,1,0:T(8,...) while((s32[]{:T(128)}, ...), condition=%wide.region_16.17_spmd, body=%wide.region_15.16_spmd.sunk | while | flops 337985536 | bytes 9953940 | solution.py:208
  136.6 1.7 fusion.142
  143.1 1.7 fusion.142
  149.6 1.7 fusion.142
  162.7 1.7 fusion.142
  169.2 1.7 fusion.142
  181.6 2.9 %copy.162 = f32[16,128,256]{1,2,0:T(8,128)} copy(f32[16,128,256]{2,1,0:T(8,128)} %bitcast.117) | data formatting | bytes 4194304 | tf_op jit(solution)/shard_map/all_to_all | solution.py:74
  184.5 7.3 %all-to-all-start.4 = ((f32[16,128,256]{1,2,0:T(8,128)}), f32[16,128,256]{1,2,0:T(8,128)}, u32[]{:S(2)}, u32[]{:S(2)}) async-start(f32[16,128,256]{1,2,0:T(8,128)} %copy.162), calls=%async_computation.4 | async-start | bytes 4194304 | tf_op jit(solution)/shard_map/all_to_all | solution.py:74
  194.6 44.5 %all-to-all-done.4 = f32[16,128,256]{1,2,0:T(8,128)} async-done(((f32[16,128,256]{1,2,0:T(8,128)}), f32[16,128,256]{1,2,0:T(8,128)}, u32[]{:S(2)}, u32[]{:S(2)}) %all-to-all-start.4) | async-done | bytes 2097184 | tf_op jit(solution)/shard_map/all_to_all | solution.py:74
  239.1 3.5 %all-to-all-start.3 = ((bf16[2,128,1024]{2,1,0:T(8,128)(2,1)}), bf16[2,128,1024]{2,1,0:T(8,128)(2,1)S(1)}, u32[]{:S(2)}, u32[]{:S(2)}) async-start(bf16[2,128,1024]{2,1,0:T(8,128)(2,1)} %copy.189), calls=%async_computation.3 | async-start | bytes 1048576 | tf_op jit(solution)/shard_map/all_to_all | solution.py:216
  242.6 1.8 reduce_sum.103
  245.2 6.4 %all-to-all-done.3 = bf16[2,128,1024]{2,1,0:T(8,128)(2,1)S(1)} async-done(((bf16[2,128,1024]{2,1,0:T(8,128)(2,1)}), bf16[2,128,1024]{2,1,0:T(8,128)(2,1)S(1)}, u32[]{:S(2)}, u32[]{:S(2)}) %all-to-all-start.3) | async-done | bytes 524320 | tf_op jit(solution)/shard_map/all_to_all | solution.py:216
  251.7 3.3 %all-to-all-start.6 = ((bf16[2,128,128]{2,1,0:T(8,128)(2,1)}), bf16[2,128,128]{2,1,0:T(8,128)(2,1)S(1)}, u32[]{:S(2)}, u32[]{:S(2)}) async-start(bf16[2,128,128]{2,1,0:T(8,128)(2,1)} %bitcast.131), calls=%async_computation.6 | async-start | bytes 131072 | tf_op jit(solution)/shard_map/all_to_all | solution.py:218
  255.6 3.5 %all-to-all-done.6 = bf16[2,128,128]{2,1,0:T(8,128)(2,1)S(1)} async-done(((bf16[2,128,128]{2,1,0:T(8,128)(2,1)}), bf16[2,128,128]{2,1,0:T(8,128)(2,1)S(1)}, u32[]{:S(2)}, u32[]{:S(2)}) %all-to-all-start.6) | async-done | bytes 65568 | tf_op jit(solution)/shard_map/all_to_all | solution.py:218
  259.1 3.3 %all-to-all-start.5 = ((bf16[2,128,128]{2,1,0:T(8,128)(2,1)}), bf16[2,128,128]{2,1,0:T(8,128)(2,1)S(1)}, u32[]{:S(2)}, u32[]{:S(2)}) async-start(bf16[2,128,128]{2,1,0:T(8,128)(2,1)} %bitcast.118), calls=%async_computation.5 | async-start | bytes 131072 | tf_op jit(solution)/shard_map/all_to_all | solution.py:217
  (177 shorter events, 93.9 us)
Async XLA Ops:
  0.6 29.7 %copy-start.4 = (bf16[256,1024]{1,0:T(8,128)(2,1)S(1)}, bf16[256,1024]{1,0:T(8,128)(2,1)}, u32[]{:S(2)}) copy-start(bf16[256,1024]{1,0:T(8,128)(2,1)} %param.18) | copy-start | bytes 1572868
  2.4 18.2 %all-to-all-start = ((bf16[128,2,128]{2,0,1:T(8,128)(2,1)}), bf16[128,2,128]{2,0,1:T(8,128)(2,1)S(1)}, u32[]{:S(2)}, u32[]{:S(2)}) async-start(bf16[128,2,128]{2,0,1:T(8,128)(2,1)} %copy.134), calls=%async_computation | async-start | bytes 131072 | tf_op jit(solution)/shard_map/all_to_all | solution.py:84
  20.6 10.9 %all-to-all-start.2 = ((bf16[128,2,128]{2,0,1:T(8,128)(2,1)}), bf16[128,2,128]{2,0,1:T(8,128)(2,1)S(1)}, u32[]{:S(2)}, u32[]{:S(2)}) async-start(bf16[128,2,128]{2,0,1:T(8,128)(2,1)} %copy.140), calls=%async_computation.2 | async-start | bytes 131072 | tf_op jit(solution)/shard_map/all_to_all | solution.py:85
  31.4 49.6 %all-to-all-start.1 = ((bf16[128,2,1024]{0,2,1:T(8,128)(2,1)}), bf16[128,2,1024]{0,2,1:T(8,128)(2,1)S(1)}, u32[]{:S(2)}, u32[]{:S(2)}) async-start(bf16[128,2,1024]{0,2,1:T(8,128)(2,1)} %bitcast.54), calls=%async_computation.1 | async-start | bytes 1048576 | tf_op jit(solution)/shard_map/all_to_all | solution.py:83
  82.0 46.5 %copy-start = (f32[2,128,1,8,128]{1,4,3,0,2:T(8,128)}, f32[2,128,1,8,128]{1,4,3,0,2:T(8,128)S(1)}, u32[]{:S(2)}) copy-start(f32[2,128,1,8,128]{1,4,3,0,2:T(8,128)S(1)} %get-tuple-element.357) | copy-start | bytes 3145732
  126.3 2.2 copy-start.7
  128.9 2.0 copy-start.2
  171.6 1.4 copy-start.6
  184.5 7.3 %copy-start.1 = (f32[2,128,1,8,128]{1,4,3,0,2:T(8,128)S(1)}, f32[2,128,1,8,128]{1,4,3,0,2:T(8,128)}, u32[]{:S(2)}) copy-start(f32[2,128,1,8,128]{1,4,3,0,2:T(8,128)} %copy-done) | copy-start | bytes 3145732
  184.5 7.3 %copy-start.8 = (bf16[32,8,8,128]{3,2,1,0:T(8,128)(2,1)S(1)}, bf16[32,8,8,128]{3,2,1,0:T(8,128)(2,1)}, u32[]{:S(2)}) copy-start(bf16[32,8,8,128]{3,2,1,0:T(8,128)(2,1)} %copy.200) | copy-start | bytes 1572868
  184.5 54.6 %all-to-all-start.4 = ((f32[16,128,256]{1,2,0:T(8,128)}), f32[16,128,256]{1,2,0:T(8,128)}, u32[]{:S(2)}, u32[]{:S(2)}) async-start(f32[16,128,256]{1,2,0:T(8,128)} %copy.162), calls=%async_computation.4 | async-start | bytes 4194304 | tf_op jit(solution)/shard_map/all_to_all | solution.py:74
  191.9 1.0 copy-start.3
  239.1 12.6 %all-to-all-start.3 = ((bf16[2,128,1024]{2,1,0:T(8,128)(2,1)}), bf16[2,128,1024]{2,1,0:T(8,128)(2,1)S(1)}, u32[]{:S(2)}, u32[]{:S(2)}) async-start(bf16[2,128,1024]{2,1,0:T(8,128)(2,1)} %copy.189), calls=%async_computation.3 | async-start | bytes 1048576 | tf_op jit(solution)/shard_map/all_to_all | solution.py:216
  242.6 19.8 %copy-start.5 = (bf16[256,1,8,128]{0,3,2,1:T(8,128)(2,1)S(1)}, bf16[256,1,8,128]{0,3,2,1:T(8,128)(2,1)}, u32[]{:S(2)}) copy-start(bf16[256,1,8,128]{0,3,2,1:T(8,128)(2,1)} %get-tuple-element.343) | copy-start | bytes 1572868
  251.7 7.4 %all-to-all-start.6 = ((bf16[2,128,128]{2,1,0:T(8,128)(2,1)}), bf16[2,128,128]{2,1,0:T(8,128)(2,1)S(1)}, u32[]{:S(2)}, u32[]{:S(2)}) async-start(bf16[2,128,128]{2,1,0:T(8,128)(2,1)} %bitcast.131), calls=%async_computation.6 | async-start | bytes 131072 | tf_op jit(solution)/shard_map/all_to_all | solution.py:218
  259.1 7.4 %all-to-all-start.5 = ((bf16[2,128,128]{2,1,0:T(8,128)(2,1)}), bf16[2,128,128]{2,1,0:T(8,128)(2,1)S(1)}, u32[]{:S(2)}, u32[]{:S(2)}) async-start(bf16[2,128,128]{2,1,0:T(8,128)(2,1)} %bitcast.118), calls=%async_computation.5 | async-start | bytes 131072 | tf_op jit(solution)/shard_map/all_to_all | solution.py:217
where the time goes:
time: 271 us; the launch traced here: 267 us
  matrix products  56.1 us (21%)
  waiting for transfers between devices  55.4 us (20%)
  local copies, waits for them, and re-layouts  49.1 us (18%)
  blocking collectives  39.4 us (15%)
  other arithmetic  30.8 us (11%)
  starting transfers between devices  27.5 us (10%)
  between operations  8.6 us (3%)
    all_to_all x1, waiting for transfers between devices, return_trunks(): lax.all_to_all(store, 'leaf', split_axis=0, concat_axis=0, tiled=True)  44.5 us
    all_gather x1, blocking collectives, per_device(): lax.all_gather(stem_keys, 'leaf', axis=0, tiled=True)  22.8 us
    dot_general x6, matrix products, value_step(): jnp.einsum('rcgk,kcd->rcgd', probs_b, value3, preferred_element_type=jnp....  20.8 us
    all_gather x1, blocking collectives, per_device(): lax.all_gather(stem_values, 'leaf', axis=0, tiled=True)  16.6 us
    unnamed x40, local copies, waits for them, and re-layouts  14.1 us
    dynamic_slice x18, local copies, waits for them, and re-layouts, per_device(): running, unused = lax.scan(stats_step, start_state, (ancestor_keys, usable))  10.6 us
    dot_general x6, matrix products, backward_step(): jnp.einsum('rcgk,kcd->rcgd', trunk_dscore, key3, preferred_element_type=j...  10.4 us
    dynamic_update_slice x5, other arithmetic, return_trunks(): lax.dynamic_update_slice_in_dim(store, segment + parts[slot_index], guard...  7.86 us
  transfers between devices with their start and end apart: 7, of which 4 were waited for; matrix products, arithmetic and copies ran while one was open for 11% of the time, Pallas kernels for 0%

commit v1 on v0

v1 whole, which is shorter than its diff:
```python
import functools
import math

import jax
import jax.numpy as jnp
from jax import lax
from jax.experimental import pallas as pl
from jax.experimental.pallas import tpu as pltpu
from jax.sharding import PartitionSpec as P

HEAD_SIZE = 128
NODE_TOKENS = 128
MAX_DEPTH = 6

masked_score = -1e30
TILE_HEADS = 2


def exchange_bits(count):
    bits = []
    bit = count // 2
    while bit:
        bits.append(bit)
        bit //= 2
    return bits


def reverse_bits(value, count):
    result = value * 0
    bit, mirrored = 1, count // 2
    while mirrored:
        result = result + jnp.where((value & bit) != 0, mirrored, 0)
        bit, mirrored = bit * 2, mirrored // 2
    return result


def attention_kernel(
    group_count,
    node_count,
    per_key,
    scaling,
    parents_ref,
    place_ref,
    *refs,
):
    query_refs = refs[:node_count]
    own_refs = refs[node_count : 2 * node_count]
    grad_ref, trunk_ref = refs[2 * node_count : 2 * node_count + 2]
    outs = refs[2 * node_count + 2 :]
    attended_ref = outs[0]
    query_grad_refs = outs[1 : 1 + node_count]
    own_grad_ref, part_ref = outs[1 + node_count : 3 + node_count]
    keys_s, values_s, keys_t, values_t, prob_s, prob_b, score_b, key_acc, value_acc = outs[
        3 + node_count :
    ]
    factor = scaling * math.log2(math.e)
    trunk_rows = MAX_DEPTH * NODE_TOKENS
    total_rows = trunk_rows + NODE_TOKENS
    tile_rows = TILE_HEADS * NODE_TOKENS
    me = place_ref[0]
    current = parents_ref[me]
    spots, valids = [], []
    for level in range(MAX_DEPTH):
        valids.append(current >= 0)
        guarded = jnp.maximum(current, 0)
        spots.append(reverse_bits(guarded ^ me, group_count))
        current = jnp.where(current >= 0, parents_ref[guarded], -1)
    penalties = [jnp.where(valid, 0.0, -masked_score).astype(jnp.float32) for valid in valids]
    penalties.append(None)

    def place_block(block, key, value):
        rows = slice(block * NODE_TOKENS, (block + 1) * NODE_TOKENS)
        keys_s[rows, :] = key
        values_s[rows, :] = value
        keys_t[:, rows] = key.T
        values_t[:, rows] = value.T

    for level in range(MAX_DEPTH):
        pair = trunk_ref[spots[level]]
        place_block(level, pair[:NODE_TOKENS], pair[NODE_TOKENS:])
    key_acc[0:trunk_rows] = jnp.zeros((trunk_rows, HEAD_SIZE), jnp.float32)
    value_acc[0:trunk_rows] = jnp.zeros((trunk_rows, HEAD_SIZE), jnp.float32)
    part_ref[...] = jnp.zeros(part_ref.shape, part_ref.dtype)
    positions_k = lax.broadcasted_iota(jnp.int32, (NODE_TOKENS, tile_rows), 0)
    positions_q = lax.broadcasted_iota(jnp.int32, (NODE_TOKENS, tile_rows), 1) % NODE_TOKENS
    causal = positions_k <= positions_q
    contract_minor = (((1,), (1,)), ((), ()))
    plain = (((1,), (0,)), ((), ()))

    def dot(left, right, dims):
        return lax.dot_general(left, right, dims, preferred_element_type=jnp.float32)

    for node in range(node_count):
        own = own_refs[node]
        place_block(MAX_DEPTH, own[:NODE_TOKENS, :], own[NODE_TOKENS:, :])
        key_acc[trunk_rows:total_rows] = jnp.zeros((NODE_TOKENS, HEAD_SIZE), jnp.float32)
        value_acc[trunk_rows:total_rows] = jnp.zeros((NODE_TOKENS, HEAD_SIZE), jnp.float32)
        query_ref = query_refs[node]
        query_grad_ref = query_grad_refs[node]
        first_column = place_ref[2 + 2 * node]
        grad_rows = pl.ds(
            pl.multiple_of(place_ref[1 + 2 * node] * NODE_TOKENS, NODE_TOKENS), NODE_TOKENS
        )

        def tile(step, carry):
            def columns(offset, index):
                return pl.ds(
                    pl.multiple_of(
                        offset + (step * TILE_HEADS + index) * HEAD_SIZE, HEAD_SIZE
                    ),
                    HEAD_SIZE,
                )

            query = jnp.concatenate(
                [query_ref[:, columns(first_column, i)] for i in range(TILE_HEADS)], axis=0
            )
            grad_pieces = [grad_ref[grad_rows, columns(0, i)] for i in range(TILE_HEADS)]
            grad = jnp.concatenate(grad_pieces, axis=0)
            grad_t = jnp.concatenate([piece.T for piece in grad_pieces], axis=1)
            blocks = [
                slice(b * NODE_TOKENS, (b + 1) * NODE_TOKENS) for b in range(MAX_DEPTH + 1)
            ]
            top = None
            for b, rows in enumerate(blocks):
                scores = dot(keys_s[rows, :], query, contract_minor)
                if penalties[b] is None:
                    scores = jnp.where(causal, scores, masked_score)
                prob_s[rows, :] = scores
                peak = jnp.max(scores, axis=0, keepdims=True)
                if penalties[b] is not None:
                    peak = peak - penalties[b]
                top = peak if top is None else jnp.maximum(top, peak)
            weight_sum = None
            for b, rows in enumerate(blocks):
                shift = top if penalties[b] is None else top + penalties[b]
                weight = jnp.exp2((prob_s[rows, :] - shift) * factor)
                prob_s[rows, :] = weight
                addition = jnp.sum(weight, axis=0, keepdims=True)
                weight_sum = addition if weight_sum is None else weight_sum + addition
            inverse = 1.0 / weight_sum
            for rows in blocks:
                probs = prob_s[rows, :] * inverse
                prob_s[rows, :] = probs
                prob_b[rows, :] = probs.astype(jnp.bfloat16)
            attended = dot(values_t[...], prob_b[...], plain).astype(jnp.bfloat16)
            delta = jnp.sum(
                attended.astype(jnp.float32) * grad_t.astype(jnp.float32), axis=0, keepdims=True
            )
            for rows in blocks:
                prob_grad = dot(values_s[rows, :], grad, contract_minor)
                score_b[rows, :] = (prob_s[rows, :] * (prob_grad - delta)).astype(jnp.bfloat16)
            query_grad = (dot(keys_t[...], score_b[...], plain) * scaling).astype(jnp.bfloat16)
            key_acc[...] += dot(score_b[...], query, plain)
            value_acc[...] += dot(prob_b[...], grad, plain)
            for i in range(TILE_HEADS):
                lanes = slice(i * NODE_TOKENS, (i + 1) * NODE_TOKENS)
                attended_ref[grad_rows, columns(0, i)] = attended[:, lanes].T
                query_grad_ref[:, columns(0, i)] = query_grad[:, lanes].T
            return carry

        lax.fori_loop(0, per_key // TILE_HEADS, tile, 0)
        own_grad_ref[node, :NODE_TOKENS, :] = key_acc[trunk_rows:total_rows] * scaling
        own_grad_ref[node, NODE_TOKENS:, :] = value_acc[trunk_rows:total_rows]

    for level in range(MAX_DEPTH):
        rows = slice(level * NODE_TOKENS, (level + 1) * NODE_TOKENS)

        @pl.when(valids[level])
        def store():
            part_ref[spots[level], :NODE_TOKENS, :] = (key_acc[rows] * scaling).astype(
                part_ref.dtype
            )
            part_ref[spots[level], NODE_TOKENS:, :] = value_acc[rows].astype(part_ref.dtype)


def attention(parents, place, queries, owns, grad, trunks, per_key, scaling):
    node_count = len(queries)
    group_count = trunks.shape[0]
    width = per_key * HEAD_SIZE
    total_rows = (MAX_DEPTH + 1) * NODE_TOKENS
    tile_rows = TILE_HEADS * NODE_TOKENS
    bf16, f32 = jnp.bfloat16, jnp.float32
    smem = pl.BlockSpec(memory_space=pltpu.SMEM)
    vmem = pl.BlockSpec(memory_space=pltpu.VMEM)
    out_shape = (
        [jax.ShapeDtypeStruct((node_count * NODE_TOKENS, width), bf16)]
        + [jax.ShapeDtypeStruct((NODE_TOKENS, width), bf16)] * node_count
        + [jax.ShapeDtypeStruct((node_count, 2 * NODE_TOKENS, HEAD_SIZE), f32)]
        + [jax.ShapeDtypeStruct((group_count, 2 * NODE_TOKENS, HEAD_SIZE), bf16)]
    )
    pairs = node_count * per_key * NODE_TOKENS * total_rows
    results = pl.pallas_call(
        functools.partial(attention_kernel, group_count, node_count, per_key, scaling),
        out_shape=out_shape,
        in_specs=[smem, smem] + [vmem] * (2 * node_count + 2),
        out_specs=[vmem] * len(out_shape),
        scratch_shapes=[
            pltpu.VMEM((total_rows, HEAD_SIZE), bf16),
            pltpu.VMEM((total_rows, HEAD_SIZE), bf16),
            pltpu.VMEM((HEAD_SIZE, total_rows), bf16),
            pltpu.VMEM((HEAD_SIZE, total_rows), bf16),
            pltpu.VMEM((total_rows, tile_rows), f32),
            pltpu.VMEM((total_rows, tile_rows), bf16),
            pltpu.VMEM((total_rows, tile_rows), bf16),
            pltpu.VMEM((total_rows, HEAD_SIZE), f32),
            pltpu.VMEM((total_rows, HEAD_SIZE), f32),
        ],
        cost_estimate=pl.CostEstimate(
            flops=12 * pairs * HEAD_SIZE, transcendentals=pairs, bytes_accessed=8 * 2**20
        ),
    )(parents, place, *queries, *owns, grad, trunks)
    attended = results[0]
    query_grads = results[1 : 1 + node_count]
    own_grads, parts = results[1 + node_count :]
    return attended, query_grads, own_grads, parts


def gather_trunks(trunk, group_count):
    held = trunk[None]
    for bit in exchange_bits(group_count):
        pairs = [(i, i ^ bit) for i in range(group_count)]
        held = jnp.concatenate([held, lax.ppermute(held, "leaf", pairs)], axis=0)
    return held


def scatter_parts(parts, group_count):
    held = parts
    for bit in reversed(exchange_bits(group_count)):
        pairs = [(i, i ^ bit) for i in range(group_count)]
        half = held.shape[0] // 2
        arrived = lax.ppermute(held[half:], "leaf", pairs)
        total = held[:half].astype(jnp.float32) + arrived.astype(jnp.float32)
        held = total if half == 1 else total.astype(jnp.bfloat16)
    return held[0]


def per_device(queries, keys, values, output_gradient, parents):
    head_devices = lax.axis_size("head")
    group_count = lax.axis_size("leaf")
    my_head = lax.axis_index("head")
    my_group = lax.axis_index("leaf").astype(jnp.int32)
    row_count = output_gradient.shape[0]
    node_count = row_count // NODE_TOKENS
    width = output_gradient.shape[1]
    per_key = queries.shape[1] // keys.shape[1]
    scaling = 1.0 / math.sqrt(HEAD_SIZE)
    paired = head_devices == 2 and node_count == 2
    if paired:
        other = 1 - my_head
        swap = [(0, 1), (1, 0)]

        def both(array):
            return array[:, :HEAD_SIZE], array[:, HEAD_SIZE:]

        (key0, key1), (value0, value1) = both(keys), both(values)
        pair0 = jnp.concatenate([key0, value0], axis=0)
        pair1 = jnp.concatenate([key1, value1], axis=0)
        first = my_head == 0
        kept = jnp.where(first, pair0, pair1)
        came = lax.ppermute(jnp.where(first, pair1, pair0), "head", swap)
        trunk = jnp.where(first, kept, came)
        query_send = lax.dynamic_slice_in_dim(queries, other * width, width, 1)
        query_nodes = [queries, lax.ppermute(query_send, "head", swap)]
        owns = [kept, came]
        place = jnp.stack([my_group, my_head, my_head * width, other, other * 0])
    else:
        whole = [
            lax.all_to_all(a, "head", split_axis=1, concat_axis=0, tiled=True)
            for a in (queries, keys, values)
        ]
        starts = [node * NODE_TOKENS for node in range(node_count)]
        query_nodes = [whole[0][s : s + NODE_TOKENS] for s in starts]
        owns = [
            jnp.concatenate([whole[1][s : s + NODE_TOKENS], whole[2][s : s + NODE_TOKENS]], axis=0)
            for s in starts
        ]
        trunk = owns[0]
        place = [my_group]
        for node in range(node_count):
            place += [my_group * 0 + node, my_group * 0]
        place = jnp.stack(place)
    trunks = gather_trunks(trunk, group_count)
    attended, query_grads, own_grads, parts = attention(
        parents, place.astype(jnp.int32), query_nodes, owns, output_gradient, trunks, per_key, scaling
    )
    if paired:
        query_came = lax.ppermute(query_grads[1], "head", swap)
        query_home = jnp.concatenate(
            [
                jnp.where(first, query_grads[0], query_came),
                jnp.where(first, query_came, query_grads[0]),
            ],
            axis=1,
        )
        total = scatter_parts(parts, group_count)
        mine = (own_grads[0] + jnp.where(first, total, 0.0)).astype(jnp.bfloat16)
        theirs = (own_grads[1] + jnp.where(first, 0.0, total)).astype(jnp.bfloat16)
        came_back = lax.ppermute(theirs, "head", swap)
        left = jnp.where(first, mine, came_back)
        right = jnp.where(first, came_back, mine)
        key_home = jnp.concatenate([left[:NODE_TOKENS], right[:NODE_TOKENS]], axis=1)
        value_home = jnp.concatenate([left[NODE_TOKENS:], right[NODE_TOKENS:]], axis=1)
    else:
        total = scatter_parts(parts, group_count)
        grads = [own_grads[0] + total] + [own_grads[node] for node in range(1, node_count)]
        key_grad = jnp.concatenate([g[:NODE_TOKENS] for g in grads], axis=0).astype(jnp.bfloat16)
        value_grad = jnp.concatenate([g[NODE_TOKENS:] for g in grads], axis=0).astype(jnp.bfloat16)
        query_gradient = jnp.concatenate(query_grads, axis=0)
        query_home, key_home, value_home = [
            lax.all_to_all(a, "head", split_axis=0, concat_axis=1, tiled=True)
            for a in (query_gradient, key_grad, value_grad)
        ]
    return (attended, query_home, key_home, value_home)


def solution(mesh):
    placed = (
        P(("leaf", "head"), None),
        P(("leaf", "head"), None),
        P(("leaf", "head"), None),
        P("leaf", "head"),
        P(),
    )
    return jax.shard_map(
        per_device,
        mesh=mesh,
        in_specs=placed,
        out_specs=(
            P("leaf", "head"),
            P(("leaf", "head"), None),
            P(("leaf", "head"), None),
            P(("leaf", "head"), None),
        ),
        check_vma=False,
    )
```

time: 271 us -> 77.4 us (0.29)
  matrix products: 56.1 us -> 0 us
  local copies, waits for them, and re-layouts: 49.1 us -> 3.93 us
  blocking collectives: 39.4 us -> 0 us
  other arithmetic: 30.8 us -> 3.26 us
  waiting for transfers between devices: 55.4 us -> 38.5 us
  Pallas kernels: 0 us -> 15.1 us
  starting transfers between devices: 27.5 us -> 14.5 us
  between operations: 8.6 us -> 0.84 us
    dot_general x48 -> x0, matrix products: 56.1 us -> none  [the longest x6 20.8 us: value_step(): jnp.einsum('rcgk,kcd->rcgd', probs_b, value3, preferred_element_type=jnp....]
    all_to_all x7 -> x0, waiting for transfers between devices: 55.4 us -> none  [the longest x1 44.5 us: return_trunks(): lax.all_to_all(store, 'leaf', split_axis=0, concat_axis=0, tiled=True)]
    all_gather x2 -> x0, blocking collectives: 39.4 us -> none  [the longest x1 22.8 us: per_device(): lax.all_gather(stem_keys, 'leaf', axis=0, tiled=True)]
    ppermute x0 -> x12, waiting for transfers between devices: none -> 38.5 us  [the longest x4 14.4 us: scatter_parts(): arrived = lax.ppermute(held[half:], 'leaf', pairs)]
    all_to_all x7 -> x0, starting transfers between devices: 27.5 us -> none  [the longest x1 7.32 us: return_trunks(): lax.all_to_all(store, 'leaf', split_axis=0, concat_axis=0, tiled=True)]
    pallas_call x0 -> x1, Pallas kernels: none -> 15.1 us  [attention(): pl.pallas_call(functools.partial(attention_kernel, group_count, node_coun...]
    ppermute x0 -> x12, starting transfers between devices: none -> 14.5 us  [the longest x4 4.4 us: scatter_parts(): arrived = lax.ppermute(held[half:], 'leaf', pairs)]
    reduce_sum x15 -> x0, other arithmetic: 13.6 us -> none  [the longest x5 7.22 us: ancestor_slots(): following = jnp.sum(jnp.where(indices == current, parents, 0))]
  transfers between devices with their start and end apart: 7 -> 12, of which waited for: 4 -> 11; matrix products, arithmetic and copies ran while one was open for 11% -> 2% of each run, Pallas kernels for 0% -> 0%
where the time goes in v1:
time: 77.4 us; the launch traced here: 76.1 us
  waiting for transfers between devices  38.5 us (50%)
  Pallas kernels  15.1 us (20%)
  starting transfers between devices  14.5 us (19%)
  local copies, waits for them, and re-layouts  3.93 us (5%)
  other arithmetic  3.26 us (4%)
  between operations  0.84 us (1%)
    pallas_call x1, Pallas kernels, attention(): pl.pallas_call(functools.partial(attention_kernel, group_count, node_coun...  15.1 us
    ppermute x4, waiting for transfers between devices, scatter_parts(): arrived = lax.ppermute(held[half:], 'leaf', pairs)  14.4 us
    ppermute x4, waiting for transfers between devices, gather_trunks(): held = jnp.concatenate([held, lax.ppermute(held, 'leaf', pairs)], axis=0)  12.9 us
    ppermute x1, waiting for transfers between devices, per_device(): query_nodes = [queries, lax.ppermute(query_send, 'head', swap)]  6.39 us
    ppermute x4, starting transfers between devices, scatter_parts(): arrived = lax.ppermute(held[half:], 'leaf', pairs)  4.4 us
    ppermute x4, starting transfers between devices, gather_trunks(): held = jnp.concatenate([held, lax.ppermute(held, 'leaf', pairs)], axis=0)  3.77 us
    ppermute x1, waiting for transfers between devices, per_device(): came = lax.ppermute(jnp.where(first, pair1, pair0), 'head', swap)  2.75 us
    ppermute x1, waiting for transfers between devices, per_device(): came_back = lax.ppermute(theirs, 'head', swap)  1.92 us
  transfers between devices with their start and end apart: 12, of which 11 were waited for; matrix products, arithmetic and copies ran while one was open for 2% of the time, Pallas kernels for 0%

profile of v1, /device:TPU:10, one launch (start us, length us, event | category | flops | bytes accessed | tf_op | source)
XLA Modules:
  0.0 76.1 jit_solution(6419294712976016575)
XLA Ops:
  0.6 0.8 %fusion.5 = (bf16[128,128]{1,0:T(8,128)(2,1)S(1)}, bf16[128,128]{1,0:T(8,128)(2,1)S(1)}, bf16[128,128]{1,0:T(8,128)(2,1)S(1)}, bf16[128,128]{1,0:T(8,128)(2,1)S(1)}) fusion(bf16[128,256]{1,0:T(8,128)(2,1)} %param.6, bf16[128,256]{1,0:T(8,128)(2,1)} %param.7), kind=kLoop, calls=%fused_computation.31 | loop fusion | bytes 262144 | tf_op jit(solution)/shard_map/slice | solution.py:253
  1.5 1.6 %collective-permute-start.1 = (bf16[256,128]{1,0:T(8,128)(2,1)S(1)}, bf16[256,128]{1,0:T(8,128)(2,1)S(1)}, u32[]{:S(2)}, u32[]{:S(2)}) collective-permute-start(bf16[256,128]{1,0:T(8,128)(2,1)S(1)} %broadcast_select_fusion.4), channel_id=1, source_target_pairs={{0,1},{1,0},{2,3},{3,2},{4,5},{5,4},{6,7},{7,6},{8,9},{9,8},{10,11... | collective-permute-start | bytes 196616 | tf_op jit(solution)/shard_map/ppermute | solution.py:260
  3.1 2.7 %collective-permute-done.1.refs_3_ = bf16[256,128]{1,0:T(8,128)(2,1)S(1)} collective-permute-done((bf16[256,128]{1,0:T(8,128)(2,1)S(1)}, bf16[256,128]{1,0:T(8,128)(2,1)S(1)}, u32[]{:S(2)}, u32[]{:S(2)}) %collective-permute-start.1) | collective-permute-done | bytes 65568 | tf_op jit(solution)/shard_map/ppermute | solution.py:260
  5.8 0.7 constant_dynamic-update-slice_fusion.4
  6.5 2.6 %collective-permute-start.2 = (bf16[1,256,128]{2,1,0:T(8,128)(2,1)S(1)}, bf16[1,256,128]{2,1,0:T(8,128)(2,1)S(1)}, u32[]{:S(2)}, u32[]{:S(2)}) collective-permute-start(bf16[1,256,128]{2,1,0:T(8,128)(2,1)S(1)} %get-tuple-element.17), channel_id=1, source_target_pairs={{0,16},{2,18},{4,20},{6,22},{8,24},{10,26},{12,28},{14,30},{16,0},... | collective-permute-start | bytes 196616 | tf_op jit(solution)/shard_map/ppermute | solution.py:222
  9.1 2.6 %collective-permute-done.2 = bf16[1,256,128]{2,1,0:T(8,128)(2,1)S(1)} collective-permute-done((bf16[1,256,128]{2,1,0:T(8,128)(2,1)S(1)}, bf16[1,256,128]{2,1,0:T(8,128)(2,1)S(1)}, u32[]{:S(2)}, u32[]{:S(2)}) %collective-permute-start.2) | collective-permute-done | bytes 65568 | tf_op jit(solution)/shard_map/ppermute | solution.py:222
  11.7 0.5 collective-permute-start.3
  12.2 4.5 %collective-permute-done.3 = bf16[2,256,128]{2,1,0:T(8,128)(2,1)S(1)} collective-permute-done((bf16[2,256,128]{2,1,0:T(8,128)(2,1)S(1)}, bf16[2,256,128]{2,1,0:T(8,128)(2,1)S(1)}, u32[]{:S(2)}, u32[]{:S(2)}) %collective-permute-start.3) | collective-permute-done | bytes 131104 | tf_op jit(solution)/shard_map/ppermute | solution.py:222
  16.8 0.6 collective-permute-start.4
  17.4 5.8 %collective-permute-done.4 = bf16[4,256,128]{2,1,0:T(8,128)(2,1)S(1)} collective-permute-done((bf16[4,256,128]{2,1,0:T(8,128)(2,1)S(1)}, bf16[4,256,128]{2,1,0:T(8,128)(2,1)S(1)}, u32[]{:S(2)}, u32[]{:S(2)}) %collective-permute-start.4) | collective-permute-done | bytes 262176 | tf_op jit(solution)/shard_map/ppermute | solution.py:222
  23.4 1.6 %collective-permute-start = (bf16[128,1024]{1,0:T(8,128)(2,1)S(1)}, bf16[128,1024]{1,0:T(8,128)(2,1)S(1)}, u32[]{:S(2)}, u32[]{:S(2)}) collective-permute-start(bf16[128,1024]{1,0:T(8,128)(2,1)S(1)} %constant_dynamic-slice_fusion), channel_id=1, source_target_pairs={{0,1},{1,0},{2,3},{3,2},{4,5},{5,4},{6,7},{7,6},{8,9},{9,8},{10,11... | collective-permute-start | bytes 786440 | tf_op jit(solution)/shard_map/ppermute | solution.py:263
  25.0 0.6 stack.19.place_ref
  25.7 6.4 %collective-permute-done.refs_1_ = bf16[128,1024]{1,0:T(8,128)(2,1)S(1)} collective-permute-done((bf16[128,1024]{1,0:T(8,128)(2,1)S(1)}, bf16[128,1024]{1,0:T(8,128)(2,1)S(1)}, u32[]{:S(2)}, u32[]{:S(2)}) %collective-permute-start) | collective-permute-done | bytes 262176 | tf_op jit(solution)/shard_map/ppermute | solution.py:263
  32.1 0.7 copy-done.7
  32.8 15.1 %shard_map.84 = (bf16[256,1024]{1,0:T(8,128)(2,1)}, bf16[128,1024]{1,0:T(8,128)(2,1)}, bf16[128,1024]{1,0:T(8,128)(2,1)}, f32[2,256,128]{2,1,0:T(8,128)}, bf16[16,256,128]{2,1,0:T(8,128)(2,1)}) custom-call(s32[16]{0:T(128)} %parents_ref.1, s32[5]{0:T(128)} %stack.19.place_ref, bf16[128,2048]{1,0:T(8,128)(2,1)} %refs_0_.1, bf16[128,1024]{1,0:T(8,128)(2,1)} %copy-done.7, ...), custom_call_target="tpu_custom_call" | custom-call | flops 2818572288 | bytes 8388608 | tf_op jit(solution)/shard_map/pallas_call | solution.py:192
  48.0 1.2 %slice.60 = bf16[8,256,128]{2,1,0:T(8,128)(2,1)S(1)} slice(bf16[16,256,128]{2,1,0:T(8,128)(2,1)} %get-tuple-element.13), slice={[8:16], [0:256], [0:128]} | slice | bytes 1048576 | tf_op jit(solution)/shard_map/slice | solution.py:231
  49.2 1.9 %collective-permute-done.7 = bf16[8,256,128]{2,1,0:T(8,128)(2,1)S(1)} collective-permute-done((bf16[8,256,128]{2,1,0:T(8,128)(2,1)S(1)}, bf16[8,256,128]{2,1,0:T(8,128)(2,1)S(1)}, u32[]{:S(2)}, u32[]{:S(2)}) %collective-permute-start.7) | collective-permute-done | bytes 524320 | tf_op jit(solution)/shard_map/ppermute | solution.py:231
  51.1 0.1 add_convert_fusion
  51.3 0.6 collective-permute-start.8
  51.9 7.8 %collective-permute-done.8 = bf16[4,256,128]{2,1,0:T(8,128)(2,1)S(1)} collective-permute-done((bf16[4,256,128]{2,1,0:T(8,128)(2,1)S(1)}, bf16[4,256,128]{2,1,0:T(8,128)(2,1)S(1)}, u32[]{:S(2)}, u32[]{:S(2)}) %collective-permute-start.8) | collective-permute-done | bytes 262176 | tf_op jit(solution)/shard_map/ppermute | solution.py:231
  59.8 0.5 collective-permute-start.9
  60.3 0.4 copy-done.6
  60.7 1.5 %collective-permute-start.6 = (bf16[128,1024]{1,0:T(8,128)(2,1)S(1)}, bf16[128,1024]{1,0:T(8,128)(2,1)S(1)}, u32[]{:S(2)}, u32[]{:S(2)}) collective-permute-start(bf16[128,1024]{1,0:T(8,128)(2,1)S(1)} %copy-done.6), channel_id=1, source_target_pairs={{0,1},{1,0},{2,3},{3,2},{4,5},{5,4},{6,7},{7,6},{8,9},{9,8},{10,11... | collective-permute-start | bytes 786440 | tf_op jit(solution)/shard_map/ppermute | solution.py:287
  62.2 2.6 %collective-permute-done.9 = bf16[2,256,128]{2,1,0:T(8,128)(2,1)S(1)} collective-permute-done((bf16[2,256,128]{2,1,0:T(8,128)(2,1)S(1)}, bf16[2,256,128]{2,1,0:T(8,128)(2,1)S(1)}, u32[]{:S(2)}, u32[]{:S(2)}) %collective-permute-start.9) | collective-permute-done | bytes 131104 | tf_op jit(solution)/shard_map/ppermute | solution.py:231
  64.9 3.2 %collective-permute-start.10 = (bf16[1,256,128]{2,1,0:T(8,128)(2,1)S(1)}, bf16[1,256,128]{2,1,0:T(8,128)(2,1)S(1)}, u32[]{:S(2)}, u32[]{:S(2)}) collective-permute-start(bf16[1,256,128]{2,1,0:T(8,128)(2,1)S(1)} %slice.77), channel_id=1, source_target_pairs={{0,16},{2,18},{4,20},{6,22},{8,24},{10,26},{12,28},{14,30},{16,0},... | collective-permute-start | bytes 196616 | tf_op jit(solution)/shard_map/ppermute | solution.py:231
  68.1 0.1 collective-permute-done.6
  68.3 2.1 %collective-permute-done.10 = bf16[1,256,128]{2,1,0:T(8,128)(2,1)S(1)} collective-permute-done((bf16[1,256,128]{2,1,0:T(8,128)(2,1)S(1)}, bf16[1,256,128]{2,1,0:T(8,128)(2,1)S(1)}, u32[]{:S(2)}, u32[]{:S(2)}) %collective-permute-start.10) | collective-permute-done | bytes 65568 | tf_op jit(solution)/shard_map/ppermute | solution.py:231
  70.4 1.6 %collective-permute-start.11 = (bf16[256,128]{1,0:T(8,128)(2,1)S(1)}, bf16[256,128]{1,0:T(8,128)(2,1)S(1)}, u32[]{:S(2)}, u32[]{:S(2)}) collective-permute-start(bf16[256,128]{1,0:T(8,128)(2,1)S(1)} %fusion.1), channel_id=1, source_target_pairs={{0,1},{1,0},{2,3},{3,2},{4,5},{5,4},{6,7},{7,6},{8,9},{9,8},{10,11... | collective-permute-start | bytes 196616 | tf_op jit(solution)/shard_map/ppermute | solution.py:298
  72.0 0.8 %pad_maximum_fusion.1 = bf16[128,2048]{1,0:T(8,128)(2,1)} fusion(bf16[128,1024]{1,0:T(8,128)(2,1)S(1)} %get-tuple-element.20, bf16[128,1024]{1,0:T(8,128)(2,1)S(1)} %get-tuple-element.19), kind=kLoop, calls=%fused_computation.2 | loop fusion | flops 1048576 | bytes 1048576 | tf_op jit(solution)/shard_map/concatenate | solution.py:288
  72.8 1.9 %collective-permute-done.11 = bf16[256,128]{1,0:T(8,128)(2,1)S(1)} collective-permute-done((bf16[256,128]{1,0:T(8,128)(2,1)S(1)}, bf16[256,128]{1,0:T(8,128)(2,1)S(1)}, u32[]{:S(2)}, u32[]{:S(2)}) %collective-permute-start.11) | collective-permute-done | bytes 65568 | tf_op jit(solution)/shard_map/ppermute | solution.py:298
  74.8 0.6 pad_maximum_fusion.7
  75.5 0.6 pad_maximum_fusion.6
  (37 shorter events, 0.7 us)
Async XLA Ops:
  1.5 4.3 %collective-permute-start.1 = (bf16[256,128]{1,0:T(8,128)(2,1)S(1)}, bf16[256,128]{1,0:T(8,128)(2,1)S(1)}, u32[]{:S(2)}, u32[]{:S(2)}) collective-permute-start(bf16[256,128]{1,0:T(8,128)(2,1)S(1)} %broadcast_select_fusion.4), channel_id=1, source_target_pairs={{0,1},{1,0},{2,3},{3,2},{4,5},{5,4},{6,7},{7,6},{8,9},{9,8},{10,11... | collective-permute-start | bytes 196616 | tf_op jit(solution)/shard_map/ppermute | solution.py:260
  5.8 0.7 copy-start.4
  6.5 5.2 %collective-permute-start.2 = (bf16[1,256,128]{2,1,0:T(8,128)(2,1)S(1)}, bf16[1,256,128]{2,1,0:T(8,128)(2,1)S(1)}, u32[]{:S(2)}, u32[]{:S(2)}) collective-permute-start(bf16[1,256,128]{2,1,0:T(8,128)(2,1)S(1)} %get-tuple-element.17), channel_id=1, source_target_pairs={{0,16},{2,18},{4,20},{6,22},{8,24},{10,26},{12,28},{14,30},{16,0},... | collective-permute-start | bytes 196616 | tf_op jit(solution)/shard_map/ppermute | solution.py:222
  11.7 5.0 %collective-permute-start.3 = (bf16[2,256,128]{2,1,0:T(8,128)(2,1)S(1)}, bf16[2,256,128]{2,1,0:T(8,128)(2,1)S(1)}, u32[]{:S(2)}, u32[]{:S(2)}) collective-permute-start(bf16[2,256,128]{2,1,0:T(8,128)(2,1)S(1)} %pad_maximum_fusion.3), channel_id=1, source_target_pairs={{0,8},{2,10},{4,12},{6,14},{8,0},{10,2},{12,4},{14,6},{16,24},{18,... | collective-permute-start | bytes 393224 | tf_op jit(solution)/shard_map/ppermute | solution.py:222
  16.7 6.6 %copy-start.3 = (bf16[128,2048]{1,0:T(8,128)(2,1)S(1)}, bf16[128,2048]{1,0:T(8,128)(2,1)}, u32[]{:S(2)}) copy-start(bf16[128,2048]{1,0:T(8,128)(2,1)} %refs_0_.1) | copy-start | bytes 1572868
  16.8 6.4 %collective-permute-start.4 = (bf16[4,256,128]{2,1,0:T(8,128)(2,1)S(1)}, bf16[4,256,128]{2,1,0:T(8,128)(2,1)S(1)}, u32[]{:S(2)}, u32[]{:S(2)}) collective-permute-start(bf16[4,256,128]{2,1,0:T(8,128)(2,1)S(1)} %pad_maximum_fusion.2), channel_id=1, source_target_pairs={{0,4},{2,6},{4,0},{6,2},{8,12},{10,14},{12,8},{14,10},{16,20},{18,... | collective-permute-start | bytes 786440 | tf_op jit(solution)/shard_map/ppermute | solution.py:222
  23.2 2.4 %collective-permute-start.5 = (bf16[8,256,128]{2,1,0:T(8,128)(2,1)S(1)}, bf16[8,256,128]{2,1,0:T(8,128)(2,1)S(1)}, u32[]{:S(2)}, u32[]{:S(2)}) collective-permute-start(bf16[8,256,128]{2,1,0:T(8,128)(2,1)S(1)} %pad_maximum_fusion), channel_id=1, source_target_pairs={{0,2},{2,0},{4,6},{6,4},{8,10},{10,8},{12,14},{14,12},{16,18},{18,... | collective-permute-start | bytes 1572872 | tf_op jit(solution)/shard_map/ppermute | solution.py:222
  23.4 8.8 %collective-permute-start = (bf16[128,1024]{1,0:T(8,128)(2,1)S(1)}, bf16[128,1024]{1,0:T(8,128)(2,1)S(1)}, u32[]{:S(2)}, u32[]{:S(2)}) collective-permute-start(bf16[128,1024]{1,0:T(8,128)(2,1)S(1)} %constant_dynamic-slice_fusion), channel_id=1, source_target_pairs={{0,1},{1,0},{2,3},{3,2},{4,5},{5,4},{6,7},{7,6},{8,9},{9,8},{10,11... | collective-permute-start | bytes 786440 | tf_op jit(solution)/shard_map/ppermute | solution.py:263
  25.7 6.4 %copy-start.5 = (bf16[16,256,128]{2,1,0:T(8,128)(2,1)}, bf16[16,256,128]{2,1,0:T(8,128)(2,1)S(1)}, u32[]{:S(2)}) copy-start(bf16[16,256,128]{2,1,0:T(8,128)(2,1)S(1)} %constant_dynamic-update-slice_fusion.refs_5_) | copy-start | bytes 3145732
  32.1 0.7 copy-start.7
  48.0 3.1 %copy-start = (bf16[16,256,128]{2,1,0:T(8,128)(2,1)S(1)}, bf16[16,256,128]{2,1,0:T(8,128)(2,1)}, u32[]{:S(2)}) copy-start(bf16[16,256,128]{2,1,0:T(8,128)(2,1)} %get-tuple-element.13) | copy-start | bytes 3145732
  49.1 2.0 %collective-permute-start.7 = (bf16[8,256,128]{2,1,0:T(8,128)(2,1)S(1)}, bf16[8,256,128]{2,1,0:T(8,128)(2,1)S(1)}, u32[]{:S(2)}, u32[]{:S(2)}) collective-permute-start(bf16[8,256,128]{2,1,0:T(8,128)(2,1)S(1)} %slice.60), channel_id=1, source_target_pairs={{0,2},{2,0},{4,6},{6,4},{8,10},{10,8},{12,14},{14,12},{16,18},{18,... | collective-permute-start | bytes 1572872 | tf_op jit(solution)/shard_map/ppermute | solution.py:231
  51.3 8.4 %collective-permute-start.8 = (bf16[4,256,128]{2,1,0:T(8,128)(2,1)S(1)}, bf16[4,256,128]{2,1,0:T(8,128)(2,1)S(1)}, u32[]{:S(2)}, u32[]{:S(2)}) collective-permute-start(bf16[4,256,128]{2,1,0:T(8,128)(2,1)S(1)} %slice.73), channel_id=1, source_target_pairs={{0,4},{2,6},{4,0},{6,2},{8,12},{10,14},{12,8},{14,10},{16,20},{18,... | collective-permute-start | bytes 786440 | tf_op jit(solution)/shard_map/ppermute | solution.py:231
  59.8 1.0 %copy-start.6 = (bf16[128,1024]{1,0:T(8,128)(2,1)S(1)}, bf16[128,1024]{1,0:T(8,128)(2,1)}, u32[]{:S(2)}) copy-start(bf16[128,1024]{1,0:T(8,128)(2,1)} %get-tuple-element.11) | copy-start | bytes 786436
  59.8 5.0 %collective-permute-start.9 = (bf16[2,256,128]{2,1,0:T(8,128)(2,1)S(1)}, bf16[2,256,128]{2,1,0:T(8,128)(2,1)S(1)}, u32[]{:S(2)}, u32[]{:S(2)}) collective-permute-start(bf16[2,256,128]{2,1,0:T(8,128)(2,1)S(1)} %slice.75), channel_id=1, source_target_pairs={{0,8},{2,10},{4,12},{6,14},{8,0},{10,2},{12,4},{14,6},{16,24},{18,... | collective-permute-start | bytes 393224 | tf_op jit(solution)/shard_map/ppermute | solution.py:231
  60.7 7.5 %copy-start.2 = (bf16[128,1024]{1,0:T(8,128)(2,1)S(1)}, bf16[128,1024]{1,0:T(8,128)(2,1)}, u32[]{:S(2)}) copy-start(bf16[128,1024]{1,0:T(8,128)(2,1)} %get-tuple-element.10) | copy-start | bytes 786436
  60.7 7.5 %collective-permute-start.6 = (bf16[128,1024]{1,0:T(8,128)(2,1)S(1)}, bf16[128,1024]{1,0:T(8,128)(2,1)S(1)}, u32[]{:S(2)}, u32[]{:S(2)}) collective-permute-start(bf16[128,1024]{1,0:T(8,128)(2,1)S(1)} %copy-done.6), channel_id=1, source_target_pairs={{0,1},{1,0},{2,3},{3,2},{4,5},{5,4},{6,7},{7,6},{8,9},{9,8},{10,11... | collective-permute-start | bytes 786440 | tf_op jit(solution)/shard_map/ppermute | solution.py:287
  64.9 5.5 %collective-permute-start.10 = (bf16[1,256,128]{2,1,0:T(8,128)(2,1)S(1)}, bf16[1,256,128]{2,1,0:T(8,128)(2,1)S(1)}, u32[]{:S(2)}, u32[]{:S(2)}) collective-permute-start(bf16[1,256,128]{2,1,0:T(8,128)(2,1)S(1)} %slice.77), channel_id=1, source_target_pairs={{0,16},{2,18},{4,20},{6,22},{8,24},{10,26},{12,28},{14,30},{16,0},... | collective-permute-start | bytes 196616 | tf_op jit(solution)/shard_map/ppermute | solution.py:231
  68.2 2.1 %copy-start.1 = (f32[2,256,128]{2,1,0:T(8,128)S(1)}, f32[2,256,128]{2,1,0:T(8,128)}, u32[]{:S(2)}) copy-start(f32[2,256,128]{2,1,0:T(8,128)} %get-tuple-element.12) | copy-start | bytes 786436
  70.4 4.3 %collective-permute-start.11 = (bf16[256,128]{1,0:T(8,128)(2,1)S(1)}, bf16[256,128]{1,0:T(8,128)(2,1)S(1)}, u32[]{:S(2)}, u32[]{:S(2)}) collective-permute-start(bf16[256,128]{1,0:T(8,128)(2,1)S(1)} %fusion.1), channel_id=1, source_target_pairs={{0,1},{1,0},{2,3},{3,2},{4,5},{5,4},{6,7},{7,6},{8,9},{9,8},{10,11... | collective-permute-start | bytes 196616 | tf_op jit(solution)/shard_map/ppermute | solution.py:298

commit v2 on v1

v2 whole, which is shorter than its diff:
```python
import functools
import math

import jax
import jax.numpy as jnp
from jax import lax
from jax.experimental import pallas as pl
from jax.experimental.pallas import tpu as pltpu
from jax.sharding import PartitionSpec as P


HEAD_SIZE = 128
NODE_TOKENS = 128
MAX_DEPTH = 6

masked_score = -1e30
TILE_HEADS = 2


def exchange_bits(count):
    bits = []
    bit = count // 2
    while bit:
        bits.append(bit)
        bit //= 2
    return bits


def reverse_bits(value, count):
    result = value * 0
    bit, mirrored = 1, count // 2
    while mirrored:
        result = result + jnp.where((value & bit) != 0, mirrored, 0)
        bit, mirrored = bit * 2, mirrored // 2
    return result


def attention_kernel(
    group_count,
    node_count,
    per_key,
    scaling,
    parents_ref,
    place_ref,
    *refs,
):
    query_refs = refs[:node_count]
    own_refs = refs[node_count : 2 * node_count]
    grad_ref, trunk_ref = refs[2 * node_count : 2 * node_count + 2]
    outs = refs[2 * node_count + 2 :]
    attended_ref = outs[0]
    query_grad_refs = outs[1 : 1 + node_count]
    own_grad_ref, near_ref, far_ref = outs[1 + node_count : 4 + node_count]
    keys_s, values_s, keys_t, values_t, weight_f, weight_b, score_b, key_acc, value_acc = outs[
        4 + node_count :
    ]
    factor = scaling * math.log2(math.e)
    trunk_rows = MAX_DEPTH * NODE_TOKENS
    half = group_count // 2
    tile_rows = TILE_HEADS * NODE_TOKENS
    me = place_ref[0]
    current = parents_ref[me]
    spots, valids = [], []
    for _ in range(MAX_DEPTH):
        valids.append(current >= 0)
        guarded = jnp.maximum(current, 0)
        spots.append(reverse_bits(guarded ^ me, group_count))
        current = jnp.where(current >= 0, parents_ref[guarded], -1)
    penalties = [jnp.where(valid, 0.0, -masked_score).astype(jnp.float32) for valid in valids]
    penalties.append(None)
    contract_minor = (((1,), (1,)), ((), ()))
    plain = (((1,), (0,)), ((), ()))

    def dot(left, right, dims):
        return lax.dot_general(left, right, dims, preferred_element_type=jnp.float32)

    def place_block(block, key, value):
        rows = slice(block * NODE_TOKENS, (block + 1) * NODE_TOKENS)
        keys_s[rows, :] = key
        values_s[rows, :] = value
        keys_t[:, rows] = key.T
        values_t[:, rows] = value.T

    for level in range(MAX_DEPTH):
        pair = trunk_ref[spots[level]]
        place_block(level, pair[:NODE_TOKENS], pair[NODE_TOKENS:])
    for node in range(node_count):
        own = own_refs[node]
        place_block(MAX_DEPTH + node, own[:NODE_TOKENS, :], own[NODE_TOKENS:, :])
    positions_k = lax.broadcasted_iota(jnp.int32, (NODE_TOKENS, tile_rows), 0)
    positions_q = lax.broadcasted_iota(jnp.int32, (NODE_TOKENS, tile_rows), 1) % NODE_TOKENS
    causal = positions_k <= positions_q
    started = set()

    def block_rows(block):
        return slice(block * NODE_TOKENS, (block + 1) * NODE_TOKENS)

    class Tile:
        def __init__(self, index, node, first_head):
            self.slot = index % 2
            self.node = node
            self.first_head = first_head
            self.blocks = list(range(MAX_DEPTH)) + [MAX_DEPTH + node]
            self.grad_rows = pl.ds(
                pl.multiple_of(place_ref[1 + 2 * node] * NODE_TOKENS, NODE_TOKENS), NODE_TOKENS
            )

        def columns(self, offset, i):
            start = (self.first_head + i) * HEAD_SIZE
            if offset is None:
                return slice(start, start + HEAD_SIZE)
            return pl.ds(pl.multiple_of(offset + start, HEAD_SIZE), HEAD_SIZE)

        def query(self):
            offset = place_ref[2 + 2 * self.node]
            pieces = [
                query_refs[self.node][:, self.columns(offset, i)] for i in range(TILE_HEADS)
            ]
            return jnp.concatenate(pieces, axis=0)

        def forward(self):
            query = self.query()
            top = None
            for b, block in enumerate(self.blocks):
                scores = dot(keys_s[block_rows(block), :], query, contract_minor)
                if b == MAX_DEPTH:
                    scores = jnp.where(causal, scores, masked_score)
                weight_f[self.slot, block_rows(b), :] = scores
                peak = jnp.max(scores, axis=0, keepdims=True)
                if b < MAX_DEPTH:
                    peak = peak - penalties[b]
                top = peak if top is None else jnp.maximum(top, peak)
                yield
            weight_sum = None
            for b in range(MAX_DEPTH + 1):
                shift = top if b == MAX_DEPTH else top + penalties[b]
                weight = jnp.exp2((weight_f[self.slot, block_rows(b), :] - shift) * factor)
                weight_f[self.slot, block_rows(b), :] = weight
                weight_b[self.slot, block_rows(b), :] = weight.astype(jnp.bfloat16)
                addition = jnp.sum(weight, axis=0, keepdims=True)
                weight_sum = addition if weight_sum is None else weight_sum + addition
                yield
            self.inverse = 1.0 / weight_sum

        def backward(self):
            grad_t = jnp.concatenate(
                [grad_ref[self.grad_rows, self.columns(None, i)].T for i in range(TILE_HEADS)],
                axis=1,
            )
            scaled_t = (grad_t.astype(jnp.float32) * self.inverse).astype(jnp.bfloat16)
            trunk = slice(0, trunk_rows)
            own_block = self.blocks[-1]
            attended = dot(values_t[:, trunk], weight_b[self.slot, trunk, :], plain)
            attended += dot(
                values_t[:, block_rows(own_block)],
                weight_b[self.slot, block_rows(MAX_DEPTH), :],
                plain,
            )
            attended = (attended * self.inverse).astype(jnp.bfloat16)
            delta = jnp.sum(
                attended.astype(jnp.float32) * scaled_t.astype(jnp.float32),
                axis=0,
                keepdims=True,
            )
            for i in range(TILE_HEADS):
                attended_ref[self.grad_rows, self.columns(None, i)] = attended[
                    :, block_rows(i)
                ].T
            yield
            for b, block in enumerate(self.blocks):
                prob_grad = dot(values_s[block_rows(block), :], scaled_t, plain)
                weight = weight_f[self.slot, block_rows(b), :]
                score_b[self.slot, block_rows(b), :] = (weight * (prob_grad - delta)).astype(
                    jnp.bfloat16
                )
                yield
            query = self.query()
            for b, block in enumerate(self.blocks):
                key_part = dot(score_b[self.slot, block_rows(b), :], query, plain)
                value_part = dot(weight_b[self.slot, block_rows(b), :], scaled_t, contract_minor)
                if block in started:
                    key_acc[block_rows(block), :] += key_part
                    value_acc[block_rows(block), :] += value_part
                else:
                    key_acc[block_rows(block), :] = key_part
                    value_acc[block_rows(block), :] = value_part
                    started.add(block)
                yield
            query_grad = dot(keys_t[:, trunk], score_b[self.slot, trunk, :], plain)
            query_grad += dot(
                keys_t[:, block_rows(own_block)],
                score_b[self.slot, block_rows(MAX_DEPTH), :],
                plain,
            )
            query_grad = (query_grad * scaling).astype(jnp.bfloat16)
            for i in range(TILE_HEADS):
                query_grad_refs[self.node][:, self.columns(None, i)] = query_grad[
                    :, block_rows(i)
                ].T
            yield

    tiles = []
    for node in range(node_count):
        for first_head in range(0, per_key, TILE_HEADS):
            tiles.append(Tile(len(tiles), node, first_head))
    before = iter(())
    for tile in tiles + [None]:
        running = [before] + ([tile.forward()] if tile is not None else [])
        while running:
            for stream in list(running):
                if next(stream, running) is running:
                    running.remove(stream)
        before = tile.backward() if tile is not None else iter(())

    for node in range(node_count):
        rows = block_rows(MAX_DEPTH + node)
        own_grad_ref[node, :NODE_TOKENS, :] = key_acc[rows, :] * scaling
        own_grad_ref[node, NODE_TOKENS:, :] = value_acc[rows, :]
    near_ref[...] = jnp.zeros(near_ref.shape, near_ref.dtype)
    far_ref[...] = jnp.zeros(far_ref.shape, far_ref.dtype)
    for level in range(MAX_DEPTH):

        def store(part_ref, spot, rows=block_rows(level)):
            part_ref[spot, :NODE_TOKENS, :] = (key_acc[rows, :] * scaling).astype(part_ref.dtype)
            part_ref[spot, NODE_TOKENS:, :] = value_acc[rows, :].astype(part_ref.dtype)

        spot = spots[level]
        pl.when(valids[level] & (spot < half))(functools.partial(store, near_ref, spot))
        pl.when(valids[level] & (spot >= half))(functools.partial(store, far_ref, spot - half))


def attention(parents, place, queries, owns, grad, trunks, per_key, scaling):
    node_count = len(queries)
    group_count = trunks.shape[0]
    width = per_key * HEAD_SIZE
    block_count = MAX_DEPTH + node_count
    held_rows = block_count * NODE_TOKENS
    seen_rows = (MAX_DEPTH + 1) * NODE_TOKENS
    tile_rows = TILE_HEADS * NODE_TOKENS
    bf16, f32 = jnp.bfloat16, jnp.float32
    smem = pl.BlockSpec(memory_space=pltpu.SMEM)
    vmem = pl.BlockSpec(memory_space=pltpu.VMEM)
    half_shape = jax.ShapeDtypeStruct((group_count // 2, 2 * NODE_TOKENS, HEAD_SIZE), bf16)
    out_shape = (
        [jax.ShapeDtypeStruct((node_count * NODE_TOKENS, width), bf16)]
        + [jax.ShapeDtypeStruct((NODE_TOKENS, width), bf16)] * node_count
        + [jax.ShapeDtypeStruct((node_count, 2 * NODE_TOKENS, HEAD_SIZE), f32)]
        + [half_shape, half_shape]
    )
    pairs = node_count * per_key * NODE_TOKENS * seen_rows
    results = pl.pallas_call(
        functools.partial(attention_kernel, group_count, node_count, per_key, scaling),
        out_shape=out_shape,
        in_specs=[smem, smem] + [vmem] * (2 * node_count + 2),
        out_specs=[vmem] * len(out_shape),
        scratch_shapes=[
            pltpu.VMEM((held_rows, HEAD_SIZE), bf16),
            pltpu.VMEM((held_rows, HEAD_SIZE), bf16),
            pltpu.VMEM((HEAD_SIZE, held_rows), bf16),
            pltpu.VMEM((HEAD_SIZE, held_rows), bf16),
            pltpu.VMEM((2, seen_rows, tile_rows), f32),
            pltpu.VMEM((2, seen_rows, tile_rows), bf16),
            pltpu.VMEM((2, seen_rows, tile_rows), bf16),
            pltpu.VMEM((held_rows, HEAD_SIZE), f32),
            pltpu.VMEM((held_rows, HEAD_SIZE), f32),
        ],
        cost_estimate=pl.CostEstimate(
            flops=12 * pairs * HEAD_SIZE, transcendentals=pairs, bytes_accessed=8 * 2**20
        ),
    )(parents, place, *queries, *owns, grad, trunks)
    attended = results[0]
    query_grads = results[1 : 1 + node_count]
    own_grads = results[1 + node_count]
    parts = results[2 + node_count :]
    return attended, query_grads, own_grads, parts


def partner_pairs(count, bit):
    return [(i, i ^ bit) for i in range(count)]


def widen_trunks(held, bits, group_count):
    for bit in bits:
        arrived = lax.ppermute(held, "leaf", partner_pairs(group_count, bit))
        held = jnp.concatenate([held, arrived], axis=0)
    return held


def narrow_parts(near, far, bits, group_count):
    for bit in bits:
        arrived = lax.ppermute(far, "leaf", partner_pairs(group_count, bit))
        total = near.astype(jnp.float32) + arrived.astype(jnp.float32)
        half = near.shape[0] // 2
        total = total.astype(jnp.bfloat16)
        near, far = total[:half], total[half:]
    return near, far


def pair_of(arrays, columns):
    return jnp.concatenate([array[:, columns] for array in arrays], axis=0)


def paired_device(queries, keys, values, output_gradient, parents, per_key, scaling):
    group_count = lax.axis_size("leaf")
    my_head = lax.axis_index("head")
    my_group = lax.axis_index("leaf").astype(jnp.int32)
    width = output_gradient.shape[1]
    swap = [(0, 1), (1, 0)]
    bits = exchange_bits(group_count)
    far_bit = bits[0]
    both = ("leaf", "head")
    straight = [(2 * g, 2 * (g ^ far_bit)) for g in range(group_count)]
    across = [(2 * g, 2 * (g ^ far_bit) + 1) for g in range(group_count)]
    gathered = [(2 * g + 1, 2 * (g ^ far_bit)) for g in range(group_count)]
    first = my_head == 0
    other = 1 - my_head
    pair0 = pair_of((keys, values), slice(0, HEAD_SIZE))
    pair1 = pair_of((keys, values), slice(HEAD_SIZE, 2 * HEAD_SIZE))
    kept = jnp.where(first, pair0, pair1)
    came = lax.ppermute(jnp.where(first, pair1, pair0), "head", swap)
    far0 = lax.ppermute(pair0, both, straight)
    far1 = lax.ppermute(pair1, both, across)
    query_send = lax.dynamic_slice_in_dim(queries, other * width, width, 1)
    query_came = lax.ppermute(query_send, "head", swap)
    held = jnp.stack([jnp.where(first, kept, came), jnp.where(first, far0, far1)])
    trunks = widen_trunks(held, bits[1:], group_count)
    place = jnp.stack([my_group, my_head, my_head * width, other, other * 0]).astype(jnp.int32)
    attended, query_grads, own_grads, (near, far) = attention(
        parents,
        place,
        [queries, query_came],
        [kept, came],
        output_gradient,
        trunks,
        per_key,
        scaling,
    )
    near, far = narrow_parts(near, far, bits[:0:-1], group_count)
    query_back = lax.ppermute(query_grads[1], "head", swap)
    near, far = near[0].astype(jnp.float32), far[0]
    nothing = jnp.zeros_like(near)
    theirs = (own_grads[1] + jnp.where(first, nothing, near)).astype(jnp.bfloat16)
    far1 = lax.ppermute(far, both, gathered)
    came_back = lax.ppermute(theirs, "head", swap)
    far0 = lax.ppermute(far, both, straight)
    f32 = jnp.float32
    mine = own_grads[0] + jnp.where(first, near + far0.astype(f32), nothing)
    cross = came_back.astype(f32) + jnp.where(first, far1.astype(f32), nothing)
    left = jnp.where(first, mine, cross).astype(jnp.bfloat16)
    right = jnp.where(first, cross, mine).astype(jnp.bfloat16)
    key_home = jnp.concatenate([left[:NODE_TOKENS], right[:NODE_TOKENS]], axis=1)
    value_home = jnp.concatenate([left[NODE_TOKENS:], right[NODE_TOKENS:]], axis=1)
    query_home = jnp.concatenate(
        [
            jnp.where(first, query_grads[0], query_back),
            jnp.where(first, query_back, query_grads[0]),
        ],
        axis=1,
    )
    return (attended, query_home, key_home, value_home)


def general_device(queries, keys, values, output_gradient, parents, per_key, scaling):
    group_count = lax.axis_size("leaf")
    my_group = lax.axis_index("leaf").astype(jnp.int32)
    node_count = output_gradient.shape[0] // NODE_TOKENS
    bits = exchange_bits(group_count)
    query_all, key_all, value_all = [
        lax.all_to_all(a, "head", split_axis=1, concat_axis=0, tiled=True)
        for a in (queries, keys, values)
    ]
    spans = [slice(n * NODE_TOKENS, (n + 1) * NODE_TOKENS) for n in range(node_count)]
    owns = [jnp.concatenate([key_all[s], value_all[s]], axis=0) for s in spans]
    trunks = widen_trunks(owns[0][None], bits, group_count)
    zero = my_group * 0
    place = [my_group]
    for node in range(node_count):
        place += [zero + node, zero]
    attended, query_grads, own_grads, (near, far) = attention(
        parents,
        jnp.stack(place),
        [query_all[s] for s in spans],
        owns,
        output_gradient,
        trunks,
        per_key,
        scaling,
    )
    near, far = narrow_parts(near, far, bits[:0:-1], group_count)
    arrived = lax.ppermute(far, "leaf", partner_pairs(group_count, bits[0]))
    total = near[0].astype(jnp.float32) + arrived[0].astype(jnp.float32)
    grads = [own_grads[0] + total] + [own_grads[node] for node in range(1, node_count)]
    key_grad = jnp.concatenate([g[:NODE_TOKENS] for g in grads], axis=0).astype(jnp.bfloat16)
    value_grad = jnp.concatenate([g[NODE_TOKENS:] for g in grads], axis=0).astype(jnp.bfloat16)
    query_gradient = jnp.concatenate(query_grads, axis=0)
    query_home, key_home, value_home = [
        lax.all_to_all(a, "head", split_axis=0, concat_axis=1, tiled=True)
        for a in (query_gradient, key_grad, value_grad)
    ]
    return (attended, query_home, key_home, value_home)


def per_device(queries, keys, values, output_gradient, parents):
    node_count = output_gradient.shape[0] // NODE_TOKENS
    per_key = queries.shape[1] // keys.shape[1]
    scaling = 1.0 / math.sqrt(HEAD_SIZE)
    paired = lax.axis_size("head") == 2 and node_count == 2
    body = paired_device if paired else general_device
    return body(queries, keys, values, output_gradient, parents, per_key, scaling)


def solution(mesh):
    placed = (
        P(("leaf", "head"), None),
        P(("leaf", "head"), None),
        P(("leaf", "head"), None),
        P("leaf", "head"),
        P(),
    )
    return jax.shard_map(
        per_device,
        mesh=mesh,
        in_specs=placed,
        out_specs=(
            P("leaf", "head"),
            P(("leaf", "head"), None),
            P(("leaf", "head"), None),
            P(("leaf", "head"), None),
        ),
        check_vma=False,
    )
```

time: 77.4 us -> 74.6 us (0.964)
  the two profiles are of different devices: /device:TPU:10 before, /device:TPU:0 now
where the time goes in v2:
time: 74.6 us; the launch traced here: 74.3 us
  waiting for transfers between devices  35.2 us (47%)
  starting transfers between devices  22.2 us (30%)
  Pallas kernels  9.1 us (12%)
  other arithmetic  4.35 us (6%)
  local copies, waits for them, and re-layouts  2.45 us (3%)
  between operations  0.9 us (1%)
    ppermute x3, waiting for transfers between devices, narrow_parts(): arrived = lax.ppermute(far, 'leaf', partner_pairs(group_count, bit))  12 us
    ppermute x3, waiting for transfers between devices, widen_trunks(): arrived = lax.ppermute(held, 'leaf', partner_pairs(group_count, bit))  9.31 us
    pallas_call x1, Pallas kernels, attention(): pl.pallas_call(functools.partial(attention_kernel, group_count, node_coun...  9.1 us
    ppermute x1, waiting for transfers between devices, paired_device(): query_came = lax.ppermute(query_send, 'head', swap)  6.82 us
    ppermute x1, waiting for transfers between devices, paired_device(): far0 = lax.ppermute(pair0, both, straight)  4.46 us
    ppermute x1, starting transfers between devices, paired_device(): far1 = lax.ppermute(pair1, both, across)  4.43 us
    ppermute x1, starting transfers between devices, paired_device(): far0 = lax.ppermute(far, both, straight)  3.84 us
    ppermute x3, starting transfers between devices, widen_trunks(): arrived = lax.ppermute(held, 'leaf', partner_pairs(group_count, bit))  3.25 us
  transfers between devices with their start and end apart: 14, of which 9 were waited for; matrix products, arithmetic and copies ran while one was open for 3% of the time, Pallas kernels for 0%

profile of v2, /device:TPU:0, one launch (start us, length us, event | category | flops | bytes accessed | tf_op | source)
XLA Modules:
  0.0 74.3 jit_solution(12078360911422843344)
XLA Ops:
  0.6 0.8 %fusion.6 = (bf16[128,128]{1,0:T(8,128)(2,1)S(1)}, bf16[128,128]{1,0:T(8,128)(2,1)S(1)}, bf16[128,128]{1,0:T(8,128)(2,1)S(1)}, bf16[128,128]{1,0:T(8,128)(2,1)S(1)}) fusion(bf16[128,256]{1,0:T(8,128)(2,1)} %param.6, bf16[128,256]{1,0:T(8,128)(2,1)} %param.7), kind=kLoop, calls=%fused_computation.36 | loop fusion | bytes 262144 | tf_op jit(solution)/shard_map/slice | solution.py:300
  1.5 3.1 %collective-permute-start.1 = (bf16[256,128]{1,0:T(8,128)(2,1)S(1)}, bf16[256,128]{1,0:T(8,128)(2,1)S(1)}, u32[]{:S(2)}, u32[]{:S(2)}) collective-permute-start(bf16[256,128]{1,0:T(8,128)(2,1)S(1)} %get-tuple-element.30), channel_id=1, source_target_pairs={{0,1},{1,0},{2,3},{3,2},{4,5},{5,4},{6,7},{7,6},{8,9},{9,8},{10,11... | collective-permute-start | bytes 196616 | tf_op jit(solution)/shard_map/ppermute | solution.py:320
  4.6 4.4 %collective-permute-start.3 = (bf16[256,128]{1,0:T(8,128)(2,1)S(1)}, bf16[256,128]{1,0:T(8,128)(2,1)S(1)}, u32[]{:S(2)}, u32[]{:S(2)}) collective-permute-start(bf16[256,128]{1,0:T(8,128)(2,1)S(1)} %get-tuple-element.29), channel_id=1, source_target_pairs={{0,17},{2,19},{4,21},{6,23},{8,25},{10,27},{12,29},{14,31},{16,1},... | collective-permute-start | bytes 196616 | tf_op jit(solution)/shard_map/ppermute | solution.py:322
  9.0 1.9 %collective-permute-start.2 = (bf16[256,128]{1,0:T(8,128)(2,1)S(1)}, bf16[256,128]{1,0:T(8,128)(2,1)S(1)}, u32[]{:S(2)}, u32[]{:S(2)}) collective-permute-start(bf16[256,128]{1,0:T(8,128)(2,1)S(1)} %get-tuple-element.31), channel_id=1, source_target_pairs={{0,16},{2,18},{4,20},{6,22},{8,24},{10,26},{12,28},{14,30},{16,0},... | collective-permute-start | bytes 196616 | tf_op jit(solution)/shard_map/ppermute | solution.py:321
  10.9 0.7 constant_dynamic-update-slice_fusion.4
  11.6 4.5 %collective-permute-done.2 = bf16[256,128]{1,0:T(8,128)(2,1)S(1)} collective-permute-done((bf16[256,128]{1,0:T(8,128)(2,1)S(1)}, bf16[256,128]{1,0:T(8,128)(2,1)S(1)}, u32[]{:S(2)}, u32[]{:S(2)}) %collective-permute-start.2) | collective-permute-done | bytes 65568 | tf_op jit(solution)/shard_map/ppermute | solution.py:321
  16.1 1.6 %collective-permute-start.4 = (bf16[2,256,128]{2,1,0:T(8,128)(2,1)S(1)}, bf16[2,256,128]{2,1,0:T(8,128)(2,1)S(1)}, u32[]{:S(2)}, u32[]{:S(2)}) collective-permute-start(bf16[2,256,128]{2,1,0:T(8,128)(2,1)S(1)} %pad_maximum_fusion.3), channel_id=1, source_target_pairs={{0,8},{2,10},{4,12},{6,14},{8,0},{10,2},{12,4},{14,6},{16,24},{18,... | collective-permute-start | bytes 393224 | tf_op jit(solution)/shard_map/ppermute | solution.py:284
  17.8 3.4 %collective-permute-done.4 = bf16[2,256,128]{2,1,0:T(8,128)(2,1)S(1)} collective-permute-done((bf16[2,256,128]{2,1,0:T(8,128)(2,1)S(1)}, bf16[2,256,128]{2,1,0:T(8,128)(2,1)S(1)}, u32[]{:S(2)}, u32[]{:S(2)}) %collective-permute-start.4) | collective-permute-done | bytes 131104 | tf_op jit(solution)/shard_map/ppermute | solution.py:284
  21.2 1.6 %collective-permute-start.5 = (bf16[4,256,128]{2,1,0:T(8,128)(2,1)S(1)}, bf16[4,256,128]{2,1,0:T(8,128)(2,1)S(1)}, u32[]{:S(2)}, u32[]{:S(2)}) collective-permute-start(bf16[4,256,128]{2,1,0:T(8,128)(2,1)S(1)} %pad_maximum_fusion.2), channel_id=1, source_target_pairs={{0,4},{2,6},{4,0},{6,2},{8,12},{10,14},{12,8},{14,10},{16,20},{18,... | collective-permute-start | bytes 786440 | tf_op jit(solution)/shard_map/ppermute | solution.py:284
  22.8 4.9 %collective-permute-done.5 = bf16[4,256,128]{2,1,0:T(8,128)(2,1)S(1)} collective-permute-done((bf16[4,256,128]{2,1,0:T(8,128)(2,1)S(1)}, bf16[4,256,128]{2,1,0:T(8,128)(2,1)S(1)}, u32[]{:S(2)}, u32[]{:S(2)}) %collective-permute-start.5) | collective-permute-done | bytes 262176 | tf_op jit(solution)/shard_map/ppermute | solution.py:284
  27.7 0.1 collective-permute-start.6
  27.8 0.1 collective-permute-start
  27.9 0.7 stack.28.place_ref
  28.7 1.0 %collective-permute-done.6 = bf16[8,256,128]{2,1,0:T(8,128)(2,1)S(1)} collective-permute-done((bf16[8,256,128]{2,1,0:T(8,128)(2,1)S(1)}, bf16[8,256,128]{2,1,0:T(8,128)(2,1)S(1)}, u32[]{:S(2)}, u32[]{:S(2)}) %collective-permute-start.6) | collective-permute-done | bytes 524320 | tf_op jit(solution)/shard_map/ppermute | solution.py:284
  29.8 6.8 %collective-permute-done.refs_1_ = bf16[128,1024]{1,0:T(8,128)(2,1)S(1)} collective-permute-done((bf16[128,1024]{1,0:T(8,128)(2,1)S(1)}, bf16[128,1024]{1,0:T(8,128)(2,1)S(1)}, u32[]{:S(2)}, u32[]{:S(2)}) %collective-permute-start) | collective-permute-done | bytes 262176 | tf_op jit(solution)/shard_map/ppermute | solution.py:324
  36.6 0.7 copy-done.5
  37.3 9.1 %shard_map.84 = (bf16[256,1024]{1,0:T(8,128)(2,1)}, bf16[128,1024]{1,0:T(8,128)(2,1)}, bf16[128,1024]{1,0:T(8,128)(2,1)}, f32[2,256,128]{2,1,0:T(8,128)}, bf16[8...) custom-call(s32[16]{0:T(128)} %parents_ref.1, s32[5]{0:T(128)} %stack.28.place_ref, bf16[128,2048]{1,0:T(8,128)(2,1)} %refs_0_.1, ...), custom_call_target="tpu_custom_call" | custom-call | flops 2818572288 | bytes 8388608 | tf_op jit(solution)/shard_map/pallas_call | solution.py:251
  46.4 2.1 %collective-permute-done.8 = bf16[8,256,128]{2,1,0:T(8,128)(2,1)S(1)} collective-permute-done((bf16[8,256,128]{2,1,0:T(8,128)(2,1)}, bf16[8,256,128]{2,1,0:T(8,128)(2,1)S(1)}, u32[]{:S(2)}, u32[]{:S(2)}) %collective-permute-start.8) | collective-permute-done | bytes 524320 | tf_op jit(solution)/shard_map/ppermute | solution.py:291
  48.5 1.2 %add_convert_fusion = bf16[8,256,128]{2,1,0:T(8,128)(2,1)S(1)} fusion(bf16[8,256,128]{2,1,0:T(8,128)(2,1)S(1)} %collective-permute-done.8, bf16[8,256,128]{2,1,0:T(8,128)(2,1)} %get-tuple-element.14), kind=kLoop, calls=%fused_computation | loop fusion | flops 1048576 | bytes 1572864 | tf_op jit(solution)/shard_map/convert_element_type | solution.py:294
  49.8 1.6 %collective-permute-start.9 = (bf16[4,256,128]{2,1,0:T(8,128)(2,1)S(1)}, bf16[4,256,128]{2,1,0:T(8,128)(2,1)S(1)}, u32[]{:S(2)}, u32[]{:S(2)}) collective-permute-start(bf16[4,256,128]{2,1,0:T(8,128)(2,1)S(1)} %slice.65), channel_id=1, source_target_pairs={{0,4},{2,6},{4,0},{6,2},{8,12},{10,14},{12,8},{14,10},{16,20},{18,... | collective-permute-start | bytes 786440 | tf_op jit(solution)/shard_map/ppermute | solution.py:291
  51.3 0.3 collective-permute-start.7
  51.6 6.6 %collective-permute-done.9 = bf16[4,256,128]{2,1,0:T(8,128)(2,1)S(1)} collective-permute-done((bf16[4,256,128]{2,1,0:T(8,128)(2,1)S(1)}, bf16[4,256,128]{2,1,0:T(8,128)(2,1)S(1)}, u32[]{:S(2)}, u32[]{:S(2)}) %collective-permute-start.9) | collective-permute-done | bytes 262176 | tf_op jit(solution)/shard_map/ppermute | solution.py:291
  58.2 0.1 add_convert_fusion.1
  58.3 1.6 %collective-permute-start.10 = (bf16[2,256,128]{2,1,0:T(8,128)(2,1)S(1)}, bf16[2,256,128]{2,1,0:T(8,128)(2,1)S(1)}, u32[]{:S(2)}, u32[]{:S(2)}) collective-permute-start(bf16[2,256,128]{2,1,0:T(8,128)(2,1)S(1)} %slice.67), channel_id=1, source_target_pairs={{0,8},{2,10},{4,12},{6,14},{8,0},{10,2},{12,4},{14,6},{16,24},{18,... | collective-permute-start | bytes 393224 | tf_op jit(solution)/shard_map/ppermute | solution.py:291
  59.9 3.4 %collective-permute-done.10 = bf16[2,256,128]{2,1,0:T(8,128)(2,1)S(1)} collective-permute-done((bf16[2,256,128]{2,1,0:T(8,128)(2,1)S(1)}, bf16[2,256,128]{2,1,0:T(8,128)(2,1)S(1)}, u32[]{:S(2)}, u32[]{:S(2)}) %collective-permute-start.10) | collective-permute-done | bytes 131104 | tf_op jit(solution)/shard_map/ppermute | solution.py:291
  63.4 1.3 %collective-permute-start.13 = (bf16[256,128]{1,0:T(8,128)(2,1)S(1)}, bf16[256,128]{1,0:T(8,128)(2,1)S(1)}, u32[]{:S(2)}, u32[]{:S(2)}) collective-permute-start(bf16[256,128]{1,0:T(8,128)(2,1)S(1)} %slice_bitcast_fusion), channel_id=1, source_target_pairs={{1,16},{3,18},{5,20},{7,22},{9,24},{11,26},{13,28},{15,30},{17,0},... | collective-permute-start | bytes 196616 | tf_op jit(solution)/shard_map/ppermute | solution.py:343
  64.7 3.8 %collective-permute-start.11 = (bf16[256,128]{1,0:T(8,128)(2,1)S(1)}, bf16[256,128]{1,0:T(8,128)(2,1)S(1)}, u32[]{:S(2)}, u32[]{:S(2)}) collective-permute-start(bf16[256,128]{1,0:T(8,128)(2,1)S(1)} %slice_bitcast_fusion), channel_id=1, source_target_pairs={{0,16},{2,18},{4,20},{6,22},{8,24},{10,26},{12,28},{14,30},{16,0},... | collective-permute-start | bytes 196616 | tf_op jit(solution)/shard_map/ppermute | solution.py:345
  68.6 0.9 %collective-permute-start.12 = (bf16[256,128]{1,0:T(8,128)(2,1)S(1)}, bf16[256,128]{1,0:T(8,128)(2,1)S(1)}, u32[]{:S(2)}, u32[]{:S(2)}) collective-permute-start(bf16[256,128]{1,0:T(8,128)(2,1)S(1)} %fusion.3), channel_id=1, source_target_pairs={{0,1},{1,0},{2,3},{3,2},{4,5},{5,4},{6,7},{7,6},{8,9},{9,8},{10,11... | collective-permute-start | bytes 196616 | tf_op jit(solution)/shard_map/ppermute | solution.py:344
  69.5 0.8 %pad_maximum_fusion.1 = bf16[128,2048]{1,0:T(8,128)(2,1)} fusion(bf16[128,1024]{1,0:T(8,128)(2,1)S(1)} %get-tuple-element.24, bf16[128,1024]{1,0:T(8,128)(2,1)S(1)} %get-tuple-element.23), kind=kLoop, calls=%fused_computation.2 | loop fusion | flops 1048576 | bytes 1048576 | tf_op jit(solution)/shard_map/concatenate | solution.py:353
  70.3 2.6 %collective-permute-done.12 = bf16[256,128]{1,0:T(8,128)(2,1)S(1)} collective-permute-done((bf16[256,128]{1,0:T(8,128)(2,1)S(1)}, bf16[256,128]{1,0:T(8,128)(2,1)S(1)}, u32[]{:S(2)}, u32[]{:S(2)}) %collective-permute-start.12) | collective-permute-done | bytes 65568 | tf_op jit(solution)/shard_map/ppermute | solution.py:344
  73.0 0.6 pad_maximum_fusion.7
  73.6 0.6 pad_maximum_fusion.6
  (37 shorter events, 0.6 us)
Async XLA Ops:
  1.5 9.4 %collective-permute-start.1 = (bf16[256,128]{1,0:T(8,128)(2,1)S(1)}, bf16[256,128]{1,0:T(8,128)(2,1)S(1)}, u32[]{:S(2)}, u32[]{:S(2)}) collective-permute-start(bf16[256,128]{1,0:T(8,128)(2,1)S(1)} %get-tuple-element.30), channel_id=1, source_target_pairs={{0,1},{1,0},{2,3},{3,2},{4,5},{5,4},{6,7},{7,6},{8,9},{9,8},{10,11... | collective-permute-start | bytes 196616 | tf_op jit(solution)/shard_map/ppermute | solution.py:320
  4.6 7.1 %collective-permute-start.3 = (bf16[256,128]{1,0:T(8,128)(2,1)S(1)}, bf16[256,128]{1,0:T(8,128)(2,1)S(1)}, u32[]{:S(2)}, u32[]{:S(2)}) collective-permute-start(bf16[256,128]{1,0:T(8,128)(2,1)S(1)} %get-tuple-element.29), channel_id=1, source_target_pairs={{0,17},{2,19},{4,21},{6,23},{8,25},{10,27},{12,29},{14,31},{16,1},... | collective-permute-start | bytes 196616 | tf_op jit(solution)/shard_map/ppermute | solution.py:322
  9.0 7.1 %collective-permute-start.2 = (bf16[256,128]{1,0:T(8,128)(2,1)S(1)}, bf16[256,128]{1,0:T(8,128)(2,1)S(1)}, u32[]{:S(2)}, u32[]{:S(2)}) collective-permute-start(bf16[256,128]{1,0:T(8,128)(2,1)S(1)} %get-tuple-element.31), channel_id=1, source_target_pairs={{0,16},{2,18},{4,20},{6,22},{8,24},{10,26},{12,28},{14,30},{16,0},... | collective-permute-start | bytes 196616 | tf_op jit(solution)/shard_map/ppermute | solution.py:321
  10.9 0.7 copy-start.3
  16.1 5.0 %collective-permute-start.4 = (bf16[2,256,128]{2,1,0:T(8,128)(2,1)S(1)}, bf16[2,256,128]{2,1,0:T(8,128)(2,1)S(1)}, u32[]{:S(2)}, u32[]{:S(2)}) collective-permute-start(bf16[2,256,128]{2,1,0:T(8,128)(2,1)S(1)} %pad_maximum_fusion.3), channel_id=1, source_target_pairs={{0,8},{2,10},{4,12},{6,14},{8,0},{10,2},{12,4},{14,6},{16,24},{18,... | collective-permute-start | bytes 393224 | tf_op jit(solution)/shard_map/ppermute | solution.py:284
  21.2 6.6 %copy-start.2 = (bf16[128,2048]{1,0:T(8,128)(2,1)S(1)}, bf16[128,2048]{1,0:T(8,128)(2,1)}, u32[]{:S(2)}) copy-start(bf16[128,2048]{1,0:T(8,128)(2,1)} %refs_0_.1) | copy-start | bytes 1572868
  21.2 6.4 %collective-permute-start.5 = (bf16[4,256,128]{2,1,0:T(8,128)(2,1)S(1)}, bf16[4,256,128]{2,1,0:T(8,128)(2,1)S(1)}, u32[]{:S(2)}, u32[]{:S(2)}) collective-permute-start(bf16[4,256,128]{2,1,0:T(8,128)(2,1)S(1)} %pad_maximum_fusion.2), channel_id=1, source_target_pairs={{0,4},{2,6},{4,0},{6,2},{8,12},{10,14},{12,8},{14,10},{16,20},{18,... | collective-permute-start | bytes 786440 | tf_op jit(solution)/shard_map/ppermute | solution.py:284
  27.7 2.0 %collective-permute-start.6 = (bf16[8,256,128]{2,1,0:T(8,128)(2,1)S(1)}, bf16[8,256,128]{2,1,0:T(8,128)(2,1)S(1)}, u32[]{:S(2)}, u32[]{:S(2)}) collective-permute-start(bf16[8,256,128]{2,1,0:T(8,128)(2,1)S(1)} %pad_maximum_fusion), channel_id=1, source_target_pairs={{0,2},{2,0},{4,6},{6,4},{8,10},{10,8},{12,14},{14,12},{16,18},{18,... | collective-permute-start | bytes 1572872 | tf_op jit(solution)/shard_map/ppermute | solution.py:284
  27.8 8.8 %collective-permute-start = (bf16[128,1024]{1,0:T(8,128)(2,1)S(1)}, bf16[128,1024]{1,0:T(8,128)(2,1)S(1)}, u32[]{:S(2)}, u32[]{:S(2)}) collective-permute-start(bf16[128,1024]{1,0:T(8,128)(2,1)S(1)} %constant_dynamic-slice_fusion), channel_id=1, source_target_pairs={{0,1},{1,0},{2,3},{3,2},{4,5},{5,4},{6,7},{7,6},{8,9},{9,8},{10,11... | collective-permute-start | bytes 786440 | tf_op jit(solution)/shard_map/ppermute | solution.py:324
  29.8 6.8 %copy-start.4 = (bf16[16,256,128]{2,1,0:T(8,128)(2,1)}, bf16[16,256,128]{2,1,0:T(8,128)(2,1)S(1)}, u32[]{:S(2)}) copy-start(bf16[16,256,128]{2,1,0:T(8,128)(2,1)S(1)} %constant_dynamic-update-slice_fusion.refs_5_) | copy-start | bytes 3145732
  36.6 0.7 copy-start.5
  46.4 2.1 %collective-permute-start.8 = (bf16[8,256,128]{2,1,0:T(8,128)(2,1)}, bf16[8,256,128]{2,1,0:T(8,128)(2,1)S(1)}, u32[]{:S(2)}, u32[]{:S(2)}) collective-permute-start(bf16[8,256,128]{2,1,0:T(8,128)(2,1)} %get-tuple-element.15), channel_id=1, source_target_pairs={{0,2},{2,0},{4,6},{6,4},{8,10},{10,8},{12,14},{14,12},{16,18},{18,... | collective-permute-start | bytes 1572872 | tf_op jit(solution)/shard_map/ppermute | solution.py:291
  49.7 1.6 %copy-start.6 = (bf16[128,1024]{1,0:T(8,128)(2,1)S(1)}, bf16[128,1024]{1,0:T(8,128)(2,1)}, u32[]{:S(2)}) copy-start(bf16[128,1024]{1,0:T(8,128)(2,1)} %get-tuple-element.12) | copy-start | bytes 786436
  49.8 8.4 %collective-permute-start.9 = (bf16[4,256,128]{2,1,0:T(8,128)(2,1)S(1)}, bf16[4,256,128]{2,1,0:T(8,128)(2,1)S(1)}, u32[]{:S(2)}, u32[]{:S(2)}) collective-permute-start(bf16[4,256,128]{2,1,0:T(8,128)(2,1)S(1)} %slice.65), channel_id=1, source_target_pairs={{0,4},{2,6},{4,0},{6,2},{8,12},{10,14},{12,8},{14,10},{16,20},{18,... | collective-permute-start | bytes 786440 | tf_op jit(solution)/shard_map/ppermute | solution.py:291
  51.3 8.6 %collective-permute-start.7 = (bf16[128,1024]{1,0:T(8,128)(2,1)S(1)}, bf16[128,1024]{1,0:T(8,128)(2,1)S(1)}, u32[]{:S(2)}, u32[]{:S(2)}) collective-permute-start(bf16[128,1024]{1,0:T(8,128)(2,1)S(1)} %copy-done.6), channel_id=1, source_target_pairs={{0,1},{1,0},{2,3},{3,2},{4,5},{5,4},{6,7},{7,6},{8,9},{9,8},{10,11... | collective-permute-start | bytes 786440 | tf_op jit(solution)/shard_map/ppermute | solution.py:339
  58.2 1.6 %copy-start.1 = (bf16[128,1024]{1,0:T(8,128)(2,1)S(1)}, bf16[128,1024]{1,0:T(8,128)(2,1)}, u32[]{:S(2)}) copy-start(bf16[128,1024]{1,0:T(8,128)(2,1)} %get-tuple-element.11) | copy-start | bytes 786436
  58.3 5.0 %collective-permute-start.10 = (bf16[2,256,128]{2,1,0:T(8,128)(2,1)S(1)}, bf16[2,256,128]{2,1,0:T(8,128)(2,1)S(1)}, u32[]{:S(2)}, u32[]{:S(2)}) collective-permute-start(bf16[2,256,128]{2,1,0:T(8,128)(2,1)S(1)} %slice.67), channel_id=1, source_target_pairs={{0,8},{2,10},{4,12},{6,14},{8,0},{10,2},{12,4},{14,6},{16,24},{18,... | collective-permute-start | bytes 393224 | tf_op jit(solution)/shard_map/ppermute | solution.py:291
  59.9 8.6 %copy-start = (f32[2,256,128]{2,1,0:T(8,128)S(1)}, f32[2,256,128]{2,1,0:T(8,128)}, u32[]{:S(2)}) copy-start(f32[2,256,128]{2,1,0:T(8,128)} %get-tuple-element.13) | copy-start | bytes 786436
  63.4 9.5 %collective-permute-start.13 = (bf16[256,128]{1,0:T(8,128)(2,1)S(1)}, bf16[256,128]{1,0:T(8,128)(2,1)S(1)}, u32[]{:S(2)}, u32[]{:S(2)}) collective-permute-start(bf16[256,128]{1,0:T(8,128)(2,1)S(1)} %slice_bitcast_fusion), channel_id=1, source_target_pairs={{1,16},{3,18},{5,20},{7,22},{9,24},{11,26},{13,28},{15,30},{17,0},... | collective-permute-start | bytes 196616 | tf_op jit(solution)/shard_map/ppermute | solution.py:343
  64.7 8.2 %collective-permute-start.11 = (bf16[256,128]{1,0:T(8,128)(2,1)S(1)}, bf16[256,128]{1,0:T(8,128)(2,1)S(1)}, u32[]{:S(2)}, u32[]{:S(2)}) collective-permute-start(bf16[256,128]{1,0:T(8,128)(2,1)S(1)} %slice_bitcast_fusion), channel_id=1, source_target_pairs={{0,16},{2,18},{4,20},{6,22},{8,24},{10,26},{12,28},{14,30},{16,0},... | collective-permute-start | bytes 196616 | tf_op jit(solution)/shard_map/ppermute | solution.py:345
  68.6 4.3 %collective-permute-start.12 = (bf16[256,128]{1,0:T(8,128)(2,1)S(1)}, bf16[256,128]{1,0:T(8,128)(2,1)S(1)}, u32[]{:S(2)}, u32[]{:S(2)}) collective-permute-start(bf16[256,128]{1,0:T(8,128)(2,1)S(1)} %fusion.3), channel_id=1, source_target_pairs={{0,1},{1,0},{2,3},{3,2},{4,5},{5,4},{6,7},{7,6},{8,9},{9,8},{10,11... | collective-permute-start | bytes 196616 | tf_op jit(solution)/shard_map/ppermute | solution.py:344

commit v3 on v2

--- a/solution.py
+++ b/solution.py
@@ -15,6 +15,7 @@
 
 masked_score = -1e30
 TILE_HEADS = 2
+KERNEL_BYTES = 24 * 2**20
 
 
 def exchange_bits(count):
@@ -33,6 +34,20 @@
         result = result + jnp.where((value & bit) != 0, mirrored, 0)
         bit, mirrored = bit * 2, mirrored // 2
     return result
+
+
+def ring_size(group_count):
+    return 4 if group_count % 4 == 0 else 1
+
+
+def relative_spots(me, target, group_count):
+    ring = ring_size(group_count)
+    inner = group_count // ring
+    me_ring, target_ring = me // inner, target // inner
+    block = ring * reverse_bits((me % inner) ^ (target % inner), inner)
+    gathered = block + (me_ring - target_ring + ring) % ring
+    returned = block + (target_ring - me_ring + ring) % ring
+    return gathered, returned
 
 
 def attention_kernel(
@@ -60,11 +75,13 @@
     tile_rows = TILE_HEADS * NODE_TOKENS
     me = place_ref[0]
     current = parents_ref[me]
-    spots, valids = [], []
+    spots, back_spots, valids = [], [], []
     for _ in range(MAX_DEPTH):
         valids.append(current >= 0)
         guarded = jnp.maximum(current, 0)
-        spots.append(reverse_bits(guarded ^ me, group_count))
+        gathered, returned = relative_spots(me, guarded, group_count)
+        spots.append(gathered)
+        back_spots.append(returned)
         current = jnp.where(current >= 0, parents_ref[guarded], -1)
     penalties = [jnp.where(valid, 0.0, -masked_score).astype(jnp.float32) for valid in valids]
     penalties.append(None)
@@ -224,9 +241,13 @@
             part_ref[spot, :NODE_TOKENS, :] = (key_acc[rows, :] * scaling).astype(part_ref.dtype)
             part_ref[spot, NODE_TOKENS:, :] = value_acc[rows, :].astype(part_ref.dtype)
 
-        spot = spots[level]
+        spot = back_spots[level]
         pl.when(valids[level] & (spot < half))(functools.partial(store, near_ref, spot))
         pl.when(valids[level] & (spot >= half))(functools.partial(store, far_ref, spot - half))
+
+
+def on_chip(array):
+    return pltpu.with_memory_space_constraint(array, pltpu.VMEM)
 
 
 def attention(parents, place, queries, owns, grad, trunks, per_key, scaling):
@@ -240,11 +261,11 @@
     bf16, f32 = jnp.bfloat16, jnp.float32
     smem = pl.BlockSpec(memory_space=pltpu.SMEM)
     vmem = pl.BlockSpec(memory_space=pltpu.VMEM)
-    half_shape = jax.ShapeDtypeStruct((group_count // 2, 2 * NODE_TOKENS, HEAD_SIZE), bf16)
+    half_shape = pltpu.VMEM((group_count // 2, 2 * NODE_TOKENS, HEAD_SIZE), bf16)
     out_shape = (
-        [jax.ShapeDtypeStruct((node_count * NODE_TOKENS, width), bf16)]
-        + [jax.ShapeDtypeStruct((NODE_TOKENS, width), bf16)] * node_count
-        + [jax.ShapeDtypeStruct((node_count, 2 * NODE_TOKENS, HEAD_SIZE), f32)]
+        [pltpu.VMEM((node_count * NODE_TOKENS, width), bf16)]
+        + [pltpu.VMEM((NODE_TOKENS, width), bf16)] * node_count
+        + [pltpu.VMEM((node_count, 2 * NODE_TOKENS, HEAD_SIZE), f32)]
         + [half_shape, half_shape]
     )
     pairs = node_count * per_key * NODE_TOKENS * seen_rows
@@ -264,10 +285,15 @@
             pltpu.VMEM((held_rows, HEAD_SIZE), f32),
             pltpu.VMEM((held_rows, HEAD_SIZE), f32),
         ],
+        compiler_params=pltpu.CompilerParams(vmem_limit_bytes=KERNEL_BYTES),
         cost_estimate=pl.CostEstimate(
             flops=12 * pairs * HEAD_SIZE, transcendentals=pairs, bytes_accessed=8 * 2**20
         ),
-    )(parents, place, *queries, *owns, grad, trunks)
+    )(
+        parents,
+        place,
+        *[on_chip(a) for a in (*queries, *owns, grad, trunks)],
+    )
     attended = results[0]
     query_grads = results[1 : 1 + node_count]
     own_grads = results[1 + node_count]
@@ -279,21 +305,37 @@
     return [(i, i ^ bit) for i in range(count)]
 
 
-def widen_trunks(held, bits, group_count):
-    for bit in bits:
+def ring_pairs(count, shift):
+    ring = ring_size(count)
+    inner = count // ring
+    return [(i, (i // inner + shift) % ring * inner + i % inner) for i in range(count)]
+
+
+def gather_trunks(trunk, group_count):
+    ring = ring_size(group_count)
+    pieces = [trunk]
+    for shift in range(1, ring):
+        pieces.append(lax.ppermute(trunk, "leaf", ring_pairs(group_count, shift)))
+    held = jnp.stack(pieces)
+    for bit in exchange_bits(group_count // ring):
         arrived = lax.ppermute(held, "leaf", partner_pairs(group_count, bit))
         held = jnp.concatenate([held, arrived], axis=0)
     return held
 
 
-def narrow_parts(near, far, bits, group_count):
-    for bit in bits:
+def return_parts(near, far, group_count):
+    ring = ring_size(group_count)
+    for bit in reversed(exchange_bits(group_count // ring)):
         arrived = lax.ppermute(far, "leaf", partner_pairs(group_count, bit))
         total = near.astype(jnp.float32) + arrived.astype(jnp.float32)
+        total = total.astype(jnp.bfloat16)
         half = near.shape[0] // 2
-        total = total.astype(jnp.bfloat16)
-        near, far = total[:half], total[half:]
-    return near, far
+        near, far = (total[:half], total[half:]) if half >= ring else (total, None)
+    total = near[0].astype(jnp.float32)
+    for shift in range(1, ring):
+        arrived = lax.ppermute(near[shift], "leaf", ring_pairs(group_count, shift))
+        total = total + arrived.astype(jnp.float32)
+    return total
 
 
 def pair_of(arrays, columns):
@@ -306,24 +348,15 @@
     my_group = lax.axis_index("leaf").astype(jnp.int32)
     width = output_gradient.shape[1]
     swap = [(0, 1), (1, 0)]
-    bits = exchange_bits(group_count)
-    far_bit = bits[0]
-    both = ("leaf", "head")
-    straight = [(2 * g, 2 * (g ^ far_bit)) for g in range(group_count)]
-    across = [(2 * g, 2 * (g ^ far_bit) + 1) for g in range(group_count)]
-    gathered = [(2 * g + 1, 2 * (g ^ far_bit)) for g in range(group_count)]
     first = my_head == 0
     other = 1 - my_head
     pair0 = pair_of((keys, values), slice(0, HEAD_SIZE))
     pair1 = pair_of((keys, values), slice(HEAD_SIZE, 2 * HEAD_SIZE))
     kept = jnp.where(first, pair0, pair1)
     came = lax.ppermute(jnp.where(first, pair1, pair0), "head", swap)
-    far0 = lax.ppermute(pair0, both, straight)
-    far1 = lax.ppermute(pair1, both, across)
     query_send = lax.dynamic_slice_in_dim(queries, other * width, width, 1)
     query_came = lax.ppermute(query_send, "head", swap)
-    held = jnp.stack([jnp.where(first, kept, came), jnp.where(first, far0, far1)])
-    trunks = widen_trunks(held, bits[1:], group_count)
+    trunks = gather_trunks(jnp.where(first, kept, came), group_count)
     place = jnp.stack([my_group, my_head, my_head * width, other, other * 0]).astype(jnp.int32)
     attended, query_grads, own_grads, (near, far) = attention(
         parents,
@@ -335,19 +368,14 @@
         per_key,
         scaling,
     )
-    near, far = narrow_parts(near, far, bits[:0:-1], group_count)
     query_back = lax.ppermute(query_grads[1], "head", swap)
-    near, far = near[0].astype(jnp.float32), far[0]
-    nothing = jnp.zeros_like(near)
-    theirs = (own_grads[1] + jnp.where(first, nothing, near)).astype(jnp.bfloat16)
-    far1 = lax.ppermute(far, both, gathered)
+    total = return_parts(near, far, group_count)
+    nothing = jnp.zeros_like(total)
+    mine = (own_grads[0] + jnp.where(first, total, nothing)).astype(jnp.bfloat16)
+    theirs = (own_grads[1] + jnp.where(first, nothing, total)).astype(jnp.bfloat16)
     came_back = lax.ppermute(theirs, "head", swap)
-    far0 = lax.ppermute(far, both, straight)
-    f32 = jnp.float32
-    mine = own_grads[0] + jnp.where(first, near + far0.astype(f32), nothing)
-    cross = came_back.astype(f32) + jnp.where(first, far1.astype(f32), nothing)
-    left = jnp.where(first, mine, cross).astype(jnp.bfloat16)
-    right = jnp.where(first, cross, mine).astype(jnp.bfloat16)
+    left = jnp.where(first, mine, came_back)
+    right = jnp.where(first, came_back, mine)
     key_home = jnp.concatenate([left[:NODE_TOKENS], right[:NODE_TOKENS]], axis=1)
     value_home = jnp.concatenate([left[NODE_TOKENS:], right[NODE_TOKENS:]], axis=1)
     query_home = jnp.concatenate(
@@ -364,14 +392,13 @@
     group_count = lax.axis_size("leaf")
     my_group = lax.axis_index("leaf").astype(jnp.int32)
     node_count = output_gradient.shape[0] // NODE_TOKENS
-    bits = exchange_bits(group_count)
     query_all, key_all, value_all = [
         lax.all_to_all(a, "head", split_axis=1, concat_axis=0, tiled=True)
         for a in (queries, keys, values)
     ]
     spans = [slice(n * NODE_TOKENS, (n + 1) * NODE_TOKENS) for n in range(node_count)]
     owns = [jnp.concatenate([key_all[s], value_all[s]], axis=0) for s in spans]
-    trunks = widen_trunks(owns[0][None], bits, group_count)
+    trunks = gather_trunks(owns[0], group_count)
     zero = my_group * 0
     place = [my_group]
     for node in range(node_count):
@@ -386,9 +413,7 @@
         per_key,
         scaling,
     )
-    near, far = narrow_parts(near, far, bits[:0:-1], group_count)
-    arrived = lax.ppermute(far, "leaf", partner_pairs(group_count, bits[0]))
-    total = near[0].astype(jnp.float32) + arrived[0].astype(jnp.float32)
+    total = return_parts(near, far, group_count)
     grads = [own_grads[0] + total] + [own_grads[node] for node in range(1, node_count)]
     key_grad = jnp.concatenate([g[:NODE_TOKENS] for g in grads], axis=0).astype(jnp.bfloat16)
     value_grad = jnp.concatenate([g[NODE_TOKENS:] for g in grads], axis=0).astype(jnp.bfloat16)

time: 74.6 us -> 62.9 us (0.84)
  waiting for transfers between devices: 35.2 us -> 29.8 us
  Pallas kernels: 9.1 us -> 6.57 us
  other arithmetic: 4.35 us -> 2.57 us
  starting transfers between devices: 22.2 us -> 21 us
    ppermute x10, waiting for transfers between devices: 25.8 us -> 18.8 us  [the longest x2 6.43 us: return_parts(): arrived = lax.ppermute(far, 'leaf', partner_pairs(group_count, bit))]
    ppermute x10, starting transfers between devices: 17.9 us -> 13.2 us  [the longest x3 6.07 us: gather_trunks(): pieces.append(lax.ppermute(trunk, 'leaf', ring_pairs(group_count, shift)))]
    pallas_call x1, Pallas kernels: 9.1 us -> 6.57 us  [attention(): pl.pallas_call(functools.partial(attention_kernel, group_count, node_coun...]
    ppermute x1, waiting for transfers between devices: 0.01 us -> 2.25 us  [paired_device(): came = lax.ppermute(jnp.where(first, pair1, pair0), 'head', swap)]
    ppermute x1, starting transfers between devices: 0.07 us -> 1.58 us  [paired_device(): query_came = lax.ppermute(query_send, 'head', swap)]
    ppermute x1, starting transfers between devices: 0.29 us -> 1.52 us  [paired_device(): query_back = lax.ppermute(query_grads[1], 'head', swap)]
    convert_element_type x5 -> x3, other arithmetic: 1.37 us -> 0.26 us  [the longest x2 0.21 us: return_parts(): total = total.astype(jnp.bfloat16)]
  transfers between devices with their start and end apart: 14 -> 14, of which waited for: 9 -> 13; matrix products, arithmetic and copies ran while one was open for 3% -> 3% of each run, Pallas kernels for 0% -> 0%
where the time goes in v3:
time: 62.9 us; the launch traced here: 62.7 us
  waiting for transfers between devices  29.8 us (47%)
  starting transfers between devices  21 us (33%)
  Pallas kernels  6.57 us (10%)
  other arithmetic  2.57 us (4%)
  local copies, waits for them, and re-layouts  2.03 us (3%)
  between operations  0.81 us (1%)
    ppermute x1, waiting for transfers between devices, paired_device(): query_came = lax.ppermute(query_send, 'head', swap)  6.81 us
    pallas_call x1, Pallas kernels, attention(): pl.pallas_call(functools.partial(attention_kernel, group_count, node_coun...  6.57 us
    ppermute x2, waiting for transfers between devices, return_parts(): arrived = lax.ppermute(far, 'leaf', partner_pairs(group_count, bit))  6.43 us
    ppermute x3, starting transfers between devices, gather_trunks(): pieces.append(lax.ppermute(trunk, 'leaf', ring_pairs(group_count, shift)))  6.07 us
    ppermute x2, waiting for transfers between devices, gather_trunks(): arrived = lax.ppermute(held, 'leaf', partner_pairs(group_count, bit))  4.97 us
    ppermute x3, waiting for transfers between devices, return_parts(): arrived = lax.ppermute(near[shift], 'leaf', ring_pairs(group_count, shift))  4.28 us
    ppermute x3, starting transfers between devices, return_parts(): arrived = lax.ppermute(near[shift], 'leaf', ring_pairs(group_count, shift))  3.88 us
    ppermute x3, waiting for transfers between devices, gather_trunks(): pieces.append(lax.ppermute(trunk, 'leaf', ring_pairs(group_count, shift)))  3.11 us
  transfers between devices with their start and end apart: 14, of which 13 were waited for; matrix products, arithmetic and copies ran while one was open for 3% of the time, Pallas kernels for 0%

profile of v3, /device:TPU:0, one launch (start us, length us, event | category | flops | bytes accessed | tf_op | source)
XLA Modules:
  0.0 62.7 jit_solution(12457546610992969050)
XLA Ops:
  0.6 0.8 %fusion.7 = (bf16[128,128]{1,0:T(8,128)(2,1)S(1)}, bf16[128,128]{1,0:T(8,128)(2,1)S(1)}, bf16[128,128]{1,0:T(8,128)(2,1)S(1)}, bf16[128,128]{1,0:T(8,128)(2,1)S(1)}) fusion(bf16[128,256]{1,0:T(8,128)(2,1)} %param.6, bf16[128,256]{1,0:T(8,128)(2,1)} %param.7), kind=kLoop, calls=%fused_computation.40 | loop fusion | bytes 262144 | tf_op jit(solution)/shard_map/slice | solution.py:342
  1.5 3.1 %collective-permute-start.1 = (bf16[256,128]{1,0:T(8,128)(2,1)S(1)}, bf16[256,128]{1,0:T(8,128)(2,1)S(1)}, u32[]{:S(2)}, u32[]{:S(2)}) collective-permute-start(bf16[256,128]{1,0:T(8,128)(2,1)S(1)} %broadcast_select_fusion.5), channel_id=1, source_target_pairs={{0,1},{1,0},{2,3},{3,2},{4,5},{5,4},{6,7},{7,6},{8,9},{9,8},{10,11... | collective-permute-start | bytes 196616 | tf_op jit(solution)/shard_map/ppermute | solution.py:356
  4.6 2.2 %collective-permute-done.1.refs_3_ = bf16[256,128]{1,0:T(8,128)(2,1)S(1)} collective-permute-done((bf16[256,128]{1,0:T(8,128)(2,1)S(1)}, bf16[256,128]{1,0:T(8,128)(2,1)S(1)}, u32[]{:S(2)}, u32[]{:S(2)}) %collective-permute-start.1) | collective-permute-done | bytes 65568 | tf_op jit(solution)/shard_map/ppermute | solution.py:356
  6.8 2.1 %collective-permute-start.2 = (bf16[256,128]{1,0:T(8,128)(2,1)S(1)}, bf16[256,128]{1,0:T(8,128)(2,1)S(1)}, u32[]{:S(2)}, u32[]{:S(2)}) collective-permute-start(bf16[256,128]{1,0:T(8,128)(2,1)S(1)} %get-tuple-element.19), channel_id=1, source_target_pairs={{0,8},{2,10},{4,12},{6,14},{8,16},{10,18},{12,20},{14,22},{16,24},... | collective-permute-start | bytes 196616 | tf_op jit(solution)/shard_map/ppermute | solution.py:318
  9.0 2.6 %collective-permute-start.3 = (bf16[256,128]{1,0:T(8,128)(2,1)S(1)}, bf16[256,128]{1,0:T(8,128)(2,1)S(1)}, u32[]{:S(2)}, u32[]{:S(2)}) collective-permute-start(bf16[256,128]{1,0:T(8,128)(2,1)S(1)} %get-tuple-element.19), channel_id=1, source_target_pairs={{0,16},{2,18},{4,20},{6,22},{8,24},{10,26},{12,28},{14,30},{16,0},... | collective-permute-start | bytes 196616 | tf_op jit(solution)/shard_map/ppermute | solution.py:318
  11.6 1.3 %collective-permute-start.4 = (bf16[256,128]{1,0:T(8,128)(2,1)S(1)}, bf16[256,128]{1,0:T(8,128)(2,1)S(1)}, u32[]{:S(2)}, u32[]{:S(2)}) collective-permute-start(bf16[256,128]{1,0:T(8,128)(2,1)S(1)} %get-tuple-element.19), channel_id=1, source_target_pairs={{0,24},{2,26},{4,28},{6,30},{8,0},{10,2},{12,4},{14,6},{16,8},{18,... | collective-permute-start | bytes 196616 | tf_op jit(solution)/shard_map/ppermute | solution.py:318
  12.9 1.0 %collective-permute-done.2 = bf16[256,128]{1,0:T(8,128)(2,1)S(1)} collective-permute-done((bf16[256,128]{1,0:T(8,128)(2,1)S(1)}, bf16[256,128]{1,0:T(8,128)(2,1)S(1)}, u32[]{:S(2)}, u32[]{:S(2)}) %collective-permute-start.2) | collective-permute-done | bytes 65568 | tf_op jit(solution)/shard_map/ppermute | solution.py:318
  13.9 1.6 %collective-permute-done.3 = bf16[256,128]{1,0:T(8,128)(2,1)S(1)} collective-permute-done((bf16[256,128]{1,0:T(8,128)(2,1)S(1)}, bf16[256,128]{1,0:T(8,128)(2,1)S(1)}, u32[]{:S(2)}, u32[]{:S(2)}) %collective-permute-start.3) | collective-permute-done | bytes 65568 | tf_op jit(solution)/shard_map/ppermute | solution.py:318
  15.5 0.5 collective-permute-done.4
  16.1 1.6 %collective-permute-start.5 = (bf16[4,256,128]{2,1,0:T(8,128)(2,1)S(1)}, bf16[4,256,128]{2,1,0:T(8,128)(2,1)S(1)}, u32[]{:S(2)}, u32[]{:S(2)}) collective-permute-start(bf16[4,256,128]{2,1,0:T(8,128)(2,1)S(1)} %pad_maximum_fusion.1), channel_id=1, source_target_pairs={{0,4},{2,6},{4,0},{6,2},{8,12},{10,14},{12,8},{14,10},{16,20},{18,... | collective-permute-start | bytes 786440 | tf_op jit(solution)/shard_map/ppermute | solution.py:321
  17.7 4.8 %collective-permute-done.5 = bf16[4,256,128]{2,1,0:T(8,128)(2,1)S(1)} collective-permute-done((bf16[4,256,128]{2,1,0:T(8,128)(2,1)S(1)}, bf16[4,256,128]{2,1,0:T(8,128)(2,1)S(1)}, u32[]{:S(2)}, u32[]{:S(2)}) %collective-permute-start.5) | collective-permute-done | bytes 262176 | tf_op jit(solution)/shard_map/ppermute | solution.py:321
  22.7 1.6 %collective-permute-start = (bf16[128,1024]{1,0:T(8,128)(2,1)S(1)}, bf16[128,1024]{1,0:T(8,128)(2,1)S(1)}, u32[]{:S(2)}, u32[]{:S(2)}) collective-permute-start(bf16[128,1024]{1,0:T(8,128)(2,1)S(1)} %constant_dynamic-slice_fusion), channel_id=1, source_target_pairs={{0,1},{1,0},{2,3},{3,2},{4,5},{5,4},{6,7},{7,6},{8,9},{9,8},{10,11... | collective-permute-start | bytes 786440 | tf_op jit(solution)/shard_map/ppermute | solution.py:358
  24.4 0.2 collective-permute-done.6
  24.7 6.8 %collective-permute-done.refs_1_ = bf16[128,1024]{1,0:T(8,128)(2,1)S(1)} collective-permute-done((bf16[128,1024]{1,0:T(8,128)(2,1)S(1)}, bf16[128,1024]{1,0:T(8,128)(2,1)S(1)}, u32[]{:S(2)}, u32[]{:S(2)}) %collective-permute-start) | collective-permute-done | bytes 262176 | tf_op jit(solution)/shard_map/ppermute | solution.py:358
  31.5 6.6 %shard_map.84 = (bf16[256,1024]{1,0:T(8,128)(2,1)S(1)}, bf16[128,1024]{1,0:T(8,128)(2,1)S(1)}, bf16[128,1024]{1,0:T(8,128)(2,1)S(1)}, f32[2,256,128]{2,1,0:T(8,1...) custom-call(s32[16]{0:T(128)S(1)} %copy-done.2, s32[5]{0:T(128)S(1)} %stack.34.place_ref, ...), custom_call_target="tpu_custom_call" | custom-call | flops 2818572288 | bytes 8388608 | tf_op jit(solution)/shard_map/pallas_call | solution.py:272
  38.1 1.9 %collective-permute-done.8 = bf16[8,256,128]{2,1,0:T(8,128)(2,1)S(1)} collective-permute-done((bf16[8,256,128]{2,1,0:T(8,128)(2,1)S(1)}, bf16[8,256,128]{2,1,0:T(8,128)(2,1)S(1)}, u32[]{:S(2)}, u32[]{:S(2)}) %collective-permute-start.8) | collective-permute-done | bytes 524320 | tf_op jit(solution)/shard_map/ppermute | solution.py:329
  40.0 0.1 add_convert_fusion
  40.2 1.6 %collective-permute-start.9 = (bf16[4,256,128]{2,1,0:T(8,128)(2,1)S(1)}, bf16[4,256,128]{2,1,0:T(8,128)(2,1)S(1)}, u32[]{:S(2)}, u32[]{:S(2)}) collective-permute-start(bf16[4,256,128]{2,1,0:T(8,128)(2,1)S(1)} %slice.65), channel_id=1, source_target_pairs={{0,4},{2,6},{4,0},{6,2},{8,12},{10,14},{12,8},{14,10},{16,20},{18,... | collective-permute-start | bytes 786440 | tf_op jit(solution)/shard_map/ppermute | solution.py:329
  41.8 1.5 %collective-permute-start.7 = (bf16[128,1024]{1,0:T(8,128)(2,1)S(1)}, bf16[128,1024]{1,0:T(8,128)(2,1)S(1)}, u32[]{:S(2)}, u32[]{:S(2)}) collective-permute-start(bf16[128,1024]{1,0:T(8,128)(2,1)S(1)} %get-tuple-element.12), channel_id=1, source_target_pairs={{0,1},{1,0},{2,3},{3,2},{4,5},{5,4},{6,7},{7,6},{8,9},{9,8},{10,11... | collective-permute-start | bytes 786440 | tf_op jit(solution)/shard_map/ppermute | solution.py:371
  43.3 0.8 %copy.18 = bf16[256,1024]{1,0:T(8,128)(2,1)} copy(bf16[256,1024]{1,0:T(8,128)(2,1)S(1)} %get-tuple-element.44) | data formatting | bytes 1048576
  44.1 4.5 %collective-permute-done.9 = bf16[4,256,128]{2,1,0:T(8,128)(2,1)S(1)} collective-permute-done((bf16[4,256,128]{2,1,0:T(8,128)(2,1)S(1)}, bf16[4,256,128]{2,1,0:T(8,128)(2,1)S(1)}, u32[]{:S(2)}, u32[]{:S(2)}) %collective-permute-start.9) | collective-permute-done | bytes 262176 | tf_op jit(solution)/shard_map/ppermute | solution.py:329
  48.7 0.7 %collective-permute-start.10 = (bf16[256,128]{1,0:T(8,128)(2,1)S(1)}, bf16[256,128]{1,0:T(8,128)(2,1)S(1)}, u32[]{:S(2)}, u32[]{:S(2)}) collective-permute-start(bf16[256,128]{1,0:T(8,128)(2,1)S(1)} %get-tuple-element.23), channel_id=1, source_target_pairs={{0,8},{2,10},{4,12},{6,14},{8,16},{10,18},{12,20},{14,22},{16,24},... | collective-permute-start | bytes 196616 | tf_op jit(solution)/shard_map/ppermute | solution.py:336
  49.5 2.8 %collective-permute-start.11 = (bf16[256,128]{1,0:T(8,128)(2,1)S(1)}, bf16[256,128]{1,0:T(8,128)(2,1)S(1)}, u32[]{:S(2)}, u32[]{:S(2)}) collective-permute-start(bf16[256,128]{1,0:T(8,128)(2,1)S(1)} %get-tuple-element.25), channel_id=1, source_target_pairs={{0,16},{2,18},{4,20},{6,22},{8,24},{10,26},{12,28},{14,30},{16,0},... | collective-permute-start | bytes 196616 | tf_op jit(solution)/shard_map/ppermute | solution.py:336
  52.3 0.3 collective-permute-start.12
  52.7 2.7 %collective-permute-done.10 = bf16[256,128]{1,0:T(8,128)(2,1)S(1)} collective-permute-done((bf16[256,128]{1,0:T(8,128)(2,1)S(1)}, bf16[256,128]{1,0:T(8,128)(2,1)S(1)}, u32[]{:S(2)}, u32[]{:S(2)}) %collective-permute-start.10) | collective-permute-done | bytes 65568 | tf_op jit(solution)/shard_map/ppermute | solution.py:336
  55.4 1.4 %collective-permute-done.11 = bf16[256,128]{1,0:T(8,128)(2,1)S(1)} collective-permute-done((bf16[256,128]{1,0:T(8,128)(2,1)S(1)}, bf16[256,128]{1,0:T(8,128)(2,1)S(1)}, u32[]{:S(2)}, u32[]{:S(2)}) %collective-permute-start.11) | collective-permute-done | bytes 65568 | tf_op jit(solution)/shard_map/ppermute | solution.py:336
  56.8 0.1 collective-permute-done.12
  57.0 1.6 %collective-permute-start.13 = (bf16[256,128]{1,0:T(8,128)(2,1)S(1)}, bf16[256,128]{1,0:T(8,128)(2,1)S(1)}, u32[]{:S(2)}, u32[]{:S(2)}) collective-permute-start(bf16[256,128]{1,0:T(8,128)(2,1)S(1)} %fusion.2), channel_id=1, source_target_pairs={{0,1},{1,0},{2,3},{3,2},{4,5},{5,4},{6,7},{7,6},{8,9},{9,8},{10,11... | collective-permute-start | bytes 196616 | tf_op jit(solution)/shard_map/ppermute | solution.py:376
  58.6 0.8 %pad_maximum_fusion = bf16[128,2048]{1,0:T(8,128)(2,1)} fusion(bf16[128,1024]{1,0:T(8,128)(2,1)S(1)} %get-tuple-element.22, bf16[128,1024]{1,0:T(8,128)(2,1)S(1)} %get-tuple-element.21), kind=kLoop, calls=%fused_computation.1 | loop fusion | flops 1048576 | bytes 1048576 | tf_op jit(solution)/shard_map/concatenate | solution.py:381
  59.4 1.9 %collective-permute-done.13 = bf16[256,128]{1,0:T(8,128)(2,1)S(1)} collective-permute-done((bf16[256,128]{1,0:T(8,128)(2,1)S(1)}, bf16[256,128]{1,0:T(8,128)(2,1)S(1)}, u32[]{:S(2)}, u32[]{:S(2)}) %collective-permute-start.13) | collective-permute-done | bytes 65568 | tf_op jit(solution)/shard_map/ppermute | solution.py:376
  61.4 0.6 %pad_maximum_fusion.5 = bf16[128,256]{1,0:T(8,128)(2,1)} fusion(bf16[128,128]{1,0:T(8,128)(2,1)S(1)} %get-tuple-element.30, bf16[128,128]{1,0:T(8,128)(2,1)S(1)} %get-tuple-element.28), kind=kLoop, calls=%fused_computation.20 | loop fusion | flops 131072 | bytes 131072 | tf_op jit(solution)/shard_map/concatenate | solution.py:380
  62.1 0.6 %pad_maximum_fusion.4 = bf16[128,256]{1,0:T(8,128)(2,1)} fusion(bf16[128,128]{1,0:T(8,128)(2,1)S(1)} %get-tuple-element.31, bf16[128,128]{1,0:T(8,128)(2,1)S(1)} %get-tuple-element.29), kind=kLoop, calls=%fused_computation.19 | loop fusion | flops 131072 | bytes 131072 | tf_op jit(solution)/shard_map/concatenate | solution.py:379
  (29 shorter events, 0.9 us)
Async XLA Ops:
  1.5 5.3 %collective-permute-start.1 = (bf16[256,128]{1,0:T(8,128)(2,1)S(1)}, bf16[256,128]{1,0:T(8,128)(2,1)S(1)}, u32[]{:S(2)}, u32[]{:S(2)}) collective-permute-start(bf16[256,128]{1,0:T(8,128)(2,1)S(1)} %broadcast_select_fusion.5), channel_id=1, source_target_pairs={{0,1},{1,0},{2,3},{3,2},{4,5},{5,4},{6,7},{7,6},{8,9},{9,8},{10,11... | collective-permute-start | bytes 196616 | tf_op jit(solution)/shard_map/ppermute | solution.py:356
  6.8 7.1 %collective-permute-start.2 = (bf16[256,128]{1,0:T(8,128)(2,1)S(1)}, bf16[256,128]{1,0:T(8,128)(2,1)S(1)}, u32[]{:S(2)}, u32[]{:S(2)}) collective-permute-start(bf16[256,128]{1,0:T(8,128)(2,1)S(1)} %get-tuple-element.19), channel_id=1, source_target_pairs={{0,8},{2,10},{4,12},{6,14},{8,16},{10,18},{12,20},{14,22},{16,24},... | collective-permute-start | bytes 196616 | tf_op jit(solution)/shard_map/ppermute | solution.py:318
  9.0 6.6 %collective-permute-start.3 = (bf16[256,128]{1,0:T(8,128)(2,1)S(1)}, bf16[256,128]{1,0:T(8,128)(2,1)S(1)}, u32[]{:S(2)}, u32[]{:S(2)}) collective-permute-start(bf16[256,128]{1,0:T(8,128)(2,1)S(1)} %get-tuple-element.19), channel_id=1, source_target_pairs={{0,16},{2,18},{4,20},{6,22},{8,24},{10,26},{12,28},{14,30},{16,0},... | collective-permute-start | bytes 196616 | tf_op jit(solution)/shard_map/ppermute | solution.py:318
  11.6 4.5 %collective-permute-start.4 = (bf16[256,128]{1,0:T(8,128)(2,1)S(1)}, bf16[256,128]{1,0:T(8,128)(2,1)S(1)}, u32[]{:S(2)}, u32[]{:S(2)}) collective-permute-start(bf16[256,128]{1,0:T(8,128)(2,1)S(1)} %get-tuple-element.19), channel_id=1, source_target_pairs={{0,24},{2,26},{4,28},{6,30},{8,0},{10,2},{12,4},{14,6},{16,8},{18,... | collective-permute-start | bytes 196616 | tf_op jit(solution)/shard_map/ppermute | solution.py:318
  16.1 6.4 %collective-permute-start.5 = (bf16[4,256,128]{2,1,0:T(8,128)(2,1)S(1)}, bf16[4,256,128]{2,1,0:T(8,128)(2,1)S(1)}, u32[]{:S(2)}, u32[]{:S(2)}) collective-permute-start(bf16[4,256,128]{2,1,0:T(8,128)(2,1)S(1)} %pad_maximum_fusion.1), channel_id=1, source_target_pairs={{0,4},{2,6},{4,0},{6,2},{8,12},{10,14},{12,8},{14,10},{16,20},{18,... | collective-permute-start | bytes 786440 | tf_op jit(solution)/shard_map/ppermute | solution.py:321
  17.7 5.0 %copy-start = (bf16[128,2048]{1,0:T(8,128)(2,1)S(1)}, bf16[128,2048]{1,0:T(8,128)(2,1)}, u32[]{:S(2)}) copy-start(bf16[128,2048]{1,0:T(8,128)(2,1)} %refs_0_.1) | copy-start | bytes 1572868
  22.6 2.0 %collective-permute-start.6 = (bf16[8,256,128]{2,1,0:T(8,128)(2,1)S(1)}, bf16[8,256,128]{2,1,0:T(8,128)(2,1)S(1)}, u32[]{:S(2)}, u32[]{:S(2)}) collective-permute-start(bf16[8,256,128]{2,1,0:T(8,128)(2,1)S(1)} %get-tuple-element.26), channel_id=1, source_target_pairs={{0,2},{2,0},{4,6},{6,4},{8,10},{10,8},{12,14},{14,12},{16,18},{18,... | collective-permute-start | bytes 1572872 | tf_op jit(solution)/shard_map/ppermute | solution.py:321
  22.7 8.8 %collective-permute-start = (bf16[128,1024]{1,0:T(8,128)(2,1)S(1)}, bf16[128,1024]{1,0:T(8,128)(2,1)S(1)}, u32[]{:S(2)}, u32[]{:S(2)}) collective-permute-start(bf16[128,1024]{1,0:T(8,128)(2,1)S(1)} %constant_dynamic-slice_fusion), channel_id=1, source_target_pairs={{0,1},{1,0},{2,3},{3,2},{4,5},{5,4},{6,7},{7,6},{8,9},{9,8},{10,11... | collective-permute-start | bytes 786440 | tf_op jit(solution)/shard_map/ppermute | solution.py:358
  24.6 6.9 %copy-start.1 = (bf16[256,1024]{1,0:T(8,128)(2,1)S(1)}, bf16[256,1024]{1,0:T(8,128)(2,1)}, u32[]{:S(2)}) copy-start(bf16[256,1024]{1,0:T(8,128)(2,1)} %refs_4_.1) | copy-start | bytes 1572868
  24.7 6.8 %copy-start.2 = (s32[16]{0:T(128)S(1)}, s32[16]{0:T(128)}, u32[]{:S(2)}) copy-start(s32[16]{0:T(128)} %parents_ref.1) | copy-start | bytes 196
  38.1 2.0 %collective-permute-start.8 = (bf16[8,256,128]{2,1,0:T(8,128)(2,1)S(1)}, bf16[8,256,128]{2,1,0:T(8,128)(2,1)S(1)}, u32[]{:S(2)}, u32[]{:S(2)}) collective-permute-start(bf16[8,256,128]{2,1,0:T(8,128)(2,1)S(1)} %get-tuple-element.15), channel_id=1, source_target_pairs={{0,2},{2,0},{4,6},{6,4},{8,10},{10,8},{12,14},{14,12},{16,18},{18,... | collective-permute-start | bytes 1572872 | tf_op jit(solution)/shard_map/ppermute | solution.py:329
  40.2 8.4 %collective-permute-start.9 = (bf16[4,256,128]{2,1,0:T(8,128)(2,1)S(1)}, bf16[4,256,128]{2,1,0:T(8,128)(2,1)S(1)}, u32[]{:S(2)}, u32[]{:S(2)}) collective-permute-start(bf16[4,256,128]{2,1,0:T(8,128)(2,1)S(1)} %slice.65), channel_id=1, source_target_pairs={{0,4},{2,6},{4,0},{6,2},{8,12},{10,14},{12,8},{14,10},{16,20},{18,... | collective-permute-start | bytes 786440 | tf_op jit(solution)/shard_map/ppermute | solution.py:329
  41.8 10.8 %collective-permute-start.7 = (bf16[128,1024]{1,0:T(8,128)(2,1)S(1)}, bf16[128,1024]{1,0:T(8,128)(2,1)S(1)}, u32[]{:S(2)}, u32[]{:S(2)}) collective-permute-start(bf16[128,1024]{1,0:T(8,128)(2,1)S(1)} %get-tuple-element.12), channel_id=1, source_target_pairs={{0,1},{1,0},{2,3},{3,2},{4,5},{5,4},{6,7},{7,6},{8,9},{9,8},{10,11... | collective-permute-start | bytes 786440 | tf_op jit(solution)/shard_map/ppermute | solution.py:371
  48.7 6.6 %collective-permute-start.10 = (bf16[256,128]{1,0:T(8,128)(2,1)S(1)}, bf16[256,128]{1,0:T(8,128)(2,1)S(1)}, u32[]{:S(2)}, u32[]{:S(2)}) collective-permute-start(bf16[256,128]{1,0:T(8,128)(2,1)S(1)} %get-tuple-element.23), channel_id=1, source_target_pairs={{0,8},{2,10},{4,12},{6,14},{8,16},{10,18},{12,20},{14,22},{16,24},... | collective-permute-start | bytes 196616 | tf_op jit(solution)/shard_map/ppermute | solution.py:336
  49.5 7.3 %collective-permute-start.11 = (bf16[256,128]{1,0:T(8,128)(2,1)S(1)}, bf16[256,128]{1,0:T(8,128)(2,1)S(1)}, u32[]{:S(2)}, u32[]{:S(2)}) collective-permute-start(bf16[256,128]{1,0:T(8,128)(2,1)S(1)} %get-tuple-element.25), channel_id=1, source_target_pairs={{0,16},{2,18},{4,20},{6,22},{8,24},{10,26},{12,28},{14,30},{16,0},... | collective-permute-start | bytes 196616 | tf_op jit(solution)/shard_map/ppermute | solution.py:336
  52.3 4.7 %collective-permute-start.12 = (bf16[256,128]{1,0:T(8,128)(2,1)S(1)}, bf16[256,128]{1,0:T(8,128)(2,1)S(1)}, u32[]{:S(2)}, u32[]{:S(2)}) collective-permute-start(bf16[256,128]{1,0:T(8,128)(2,1)S(1)} %get-tuple-element.24), channel_id=1, source_target_pairs={{0,24},{2,26},{4,28},{6,30},{8,0},{10,2},{12,4},{14,6},{16,8},{18,... | collective-permute-start | bytes 196616 | tf_op jit(solution)/shard_map/ppermute | solution.py:336
  57.0 4.3 %collective-permute-start.13 = (bf16[256,128]{1,0:T(8,128)(2,1)S(1)}, bf16[256,128]{1,0:T(8,128)(2,1)S(1)}, u32[]{:S(2)}, u32[]{:S(2)}) collective-permute-start(bf16[256,128]{1,0:T(8,128)(2,1)S(1)} %fusion.2), channel_id=1, source_target_pairs={{0,1},{1,0},{2,3},{3,2},{4,5},{5,4},{6,7},{7,6},{8,9},{9,8},{10,11... | collective-permute-start | bytes 196616 | tf_op jit(solution)/shard_map/ppermute | solution.py:376

commit v4 on v3

--- a/solution.py
+++ b/solution.py
@@ -61,8 +61,9 @@
 ):
     query_refs = refs[:node_count]
     own_refs = refs[node_count : 2 * node_count]
-    grad_ref, trunk_ref = refs[2 * node_count : 2 * node_count + 2]
-    outs = refs[2 * node_count + 2 :]
+    grad_refs = refs[2 * node_count : 3 * node_count]
+    trunk_ref = refs[3 * node_count]
+    outs = refs[3 * node_count + 1 :]
     attended_ref = outs[0]
     query_grad_refs = outs[1 : 1 + node_count]
     own_grad_ref, near_ref, far_ref = outs[1 + node_count : 4 + node_count]
@@ -118,21 +119,16 @@
             self.node = node
             self.first_head = first_head
             self.blocks = list(range(MAX_DEPTH)) + [MAX_DEPTH + node]
-            self.grad_rows = pl.ds(
-                pl.multiple_of(place_ref[1 + 2 * node] * NODE_TOKENS, NODE_TOKENS), NODE_TOKENS
+            self.node_rows = pl.ds(
+                pl.multiple_of(place_ref[1 + node] * NODE_TOKENS, NODE_TOKENS), NODE_TOKENS
             )
 
-        def columns(self, offset, i):
+        def columns(self, i):
             start = (self.first_head + i) * HEAD_SIZE
-            if offset is None:
-                return slice(start, start + HEAD_SIZE)
-            return pl.ds(pl.multiple_of(offset + start, HEAD_SIZE), HEAD_SIZE)
+            return slice(start, start + HEAD_SIZE)
 
         def query(self):
-            offset = place_ref[2 + 2 * self.node]
-            pieces = [
-                query_refs[self.node][:, self.columns(offset, i)] for i in range(TILE_HEADS)
-            ]
+            pieces = [query_refs[self.node][:, self.columns(i)] for i in range(TILE_HEADS)]
             return jnp.concatenate(pieces, axis=0)
 
         def forward(self):
@@ -161,7 +157,7 @@
 
         def backward(self):
             grad_t = jnp.concatenate(
-                [grad_ref[self.grad_rows, self.columns(None, i)].T for i in range(TILE_HEADS)],
+                [grad_refs[self.node][:, self.columns(i)].T for i in range(TILE_HEADS)],
                 axis=1,
             )
             scaled_t = (grad_t.astype(jnp.float32) * self.inverse).astype(jnp.bfloat16)
@@ -180,7 +176,7 @@
                 keepdims=True,
             )
             for i in range(TILE_HEADS):
-                attended_ref[self.grad_rows, self.columns(None, i)] = attended[
+                attended_ref[self.node_rows, self.columns(i)] = attended[
                     :, block_rows(i)
                 ].T
             yield
@@ -211,7 +207,7 @@
             )
             query_grad = (query_grad * scaling).astype(jnp.bfloat16)
             for i in range(TILE_HEADS):
-                query_grad_refs[self.node][:, self.columns(None, i)] = query_grad[
+                query_grad_refs[self.node][:, self.columns(i)] = query_grad[
                     :, block_rows(i)
                 ].T
             yield
@@ -250,7 +246,7 @@
     return pltpu.with_memory_space_constraint(array, pltpu.VMEM)
 
 
-def attention(parents, place, queries, owns, grad, trunks, per_key, scaling):
+def attention(parents, place, queries, owns, grads, trunks, per_key, scaling):
     node_count = len(queries)
     group_count = trunks.shape[0]
     width = per_key * HEAD_SIZE
@@ -272,7 +268,7 @@
     results = pl.pallas_call(
         functools.partial(attention_kernel, group_count, node_count, per_key, scaling),
         out_shape=out_shape,
-        in_specs=[smem, smem] + [vmem] * (2 * node_count + 2),
+        in_specs=[smem, smem] + [vmem] * (3 * node_count + 1),
         out_specs=[vmem] * len(out_shape),
         scratch_shapes=[
             pltpu.VMEM((held_rows, HEAD_SIZE), bf16),
@@ -292,7 +288,7 @@
     )(
         parents,
         place,
-        *[on_chip(a) for a in (*queries, *owns, grad, trunks)],
+        *[on_chip(a) for a in (*queries, *owns, *grads, trunks)],
     )
     attended = results[0]
     query_grads = results[1 : 1 + node_count]
@@ -316,24 +312,44 @@
     pieces = [trunk]
     for shift in range(1, ring):
         pieces.append(lax.ppermute(trunk, "leaf", ring_pairs(group_count, shift)))
+    middle = (ring + 1) // 2
     held = jnp.stack(pieces)
-    for bit in exchange_bits(group_count // ring):
-        arrived = lax.ppermute(held, "leaf", partner_pairs(group_count, bit))
-        held = jnp.concatenate([held, arrived], axis=0)
+    for stage, bit in enumerate(exchange_bits(group_count // ring)):
+        pairs = partner_pairs(group_count, bit)
+        sent = [held]
+        if stage == 0 and ring > 1:
+            sent = [jnp.stack(pieces[:middle]), jnp.stack(pieces[middle:])]
+        arrived = []
+        for part in sent:
+            arrived.append(lax.ppermute(part, "leaf", pairs))
+        held = jnp.concatenate([held, *arrived], axis=0)
     return held
+
+
+def merged(near, arrived):
+    return (near.astype(jnp.float32) + arrived.astype(jnp.float32)).astype(jnp.bfloat16)
 
 
 def return_parts(near, far, group_count):
     ring = ring_size(group_count)
-    for bit in reversed(exchange_bits(group_count // ring)):
-        arrived = lax.ppermute(far, "leaf", partner_pairs(group_count, bit))
-        total = near.astype(jnp.float32) + arrived.astype(jnp.float32)
-        total = total.astype(jnp.bfloat16)
-        half = near.shape[0] // 2
-        near, far = (total[:half], total[half:]) if half >= ring else (total, None)
-    total = near[0].astype(jnp.float32)
+    middle = (ring + 1) // 2
+    bits = exchange_bits(group_count // ring)
+    for bit in reversed(bits):
+        pairs = partner_pairs(group_count, bit)
+        if far.shape[0] == ring and ring > 1:
+            late = lax.ppermute(far[middle:], "leaf", pairs)
+            early = lax.ppermute(far[:middle], "leaf", pairs)
+            early, late = merged(near[:middle], early), merged(near[middle:], late)
+            blocks = [early[i] for i in range(middle)] + [late[i] for i in range(ring - middle)]
+        else:
+            arrived = lax.ppermute(far, "leaf", pairs)
+            total = merged(near, arrived)
+            half = near.shape[0] // 2
+            near, far = total[:half], total[half:]
+            blocks = [total[0]]
+    total = blocks[0].astype(jnp.float32)
     for shift in range(1, ring):
-        arrived = lax.ppermute(near[shift], "leaf", ring_pairs(group_count, shift))
+        arrived = lax.ppermute(blocks[shift], "leaf", ring_pairs(group_count, shift))
         total = total + arrived.astype(jnp.float32)
     return total
 
@@ -355,15 +371,20 @@
     kept = jnp.where(first, pair0, pair1)
     came = lax.ppermute(jnp.where(first, pair1, pair0), "head", swap)
     query_send = lax.dynamic_slice_in_dim(queries, other * width, width, 1)
+    query_kept = lax.dynamic_slice_in_dim(queries, my_head * width, width, 1)
+    grads = [
+        lax.dynamic_slice_in_dim(output_gradient, node * NODE_TOKENS, NODE_TOKENS, 0)
+        for node in (my_head, other)
+    ]
     query_came = lax.ppermute(query_send, "head", swap)
     trunks = gather_trunks(jnp.where(first, kept, came), group_count)
-    place = jnp.stack([my_group, my_head, my_head * width, other, other * 0]).astype(jnp.int32)
+    place = jnp.stack([my_group, my_head, other]).astype(jnp.int32)
     attended, query_grads, own_grads, (near, far) = attention(
         parents,
         place,
-        [queries, query_came],
+        [query_kept, query_came],
         [kept, came],
-        output_gradient,
+        grads,
         trunks,
         per_key,
         scaling,
@@ -402,13 +423,13 @@
     zero = my_group * 0
     place = [my_group]
     for node in range(node_count):
-        place += [zero + node, zero]
+        place += [zero + node]
     attended, query_grads, own_grads, (near, far) = attention(
         parents,
         jnp.stack(place),
         [query_all[s] for s in spans],
         owns,
-        output_gradient,
+        [output_gradient[s] for s in spans],
         trunks,
         per_key,
         scaling,

time: 62.9 us -> 64.2 us (1.021)
  waiting for transfers between devices: 29.8 us -> 24.9 us
  local copies, waits for them, and re-layouts: 2.03 us -> 5.78 us
  starting transfers between devices: 21 us -> 22.7 us
  other arithmetic: 2.57 us -> 3.26 us
    unnamed x11 -> x12, local copies, waits for them, and re-layouts: 0.89 us -> 4.08 us
    ppermute x7 -> x9, waiting for transfers between devices: 15.7 us -> 12.6 us  [the longest x3 5.51 us: return_parts(): lax.ppermute(blocks[shift], 'leaf', ring_pairs(group_count, shift))]
    ppermute x7 -> x9, starting transfers between devices: 7.15 us -> 8.96 us  [the longest x3 3.62 us: return_parts(): lax.ppermute(blocks[shift], 'leaf', ring_pairs(group_count, shift))]
    ppermute x3, waiting for transfers between devices: 3.11 us -> 1.48 us  [gather_trunks(): pieces.append(lax.ppermute(trunk, 'leaf', ring_pairs(group_count, shift)))]
  transfers between devices with their start and end apart: 14 -> 16, of which waited for: 13 -> 12; matrix products, arithmetic and copies ran while one was open for 3% -> 7% of each run, Pallas kernels for 0% -> 0%
where the time goes in v4:
time: 64.2 us; the launch traced here: 64 us
  waiting for transfers between devices  24.9 us (39%)
  starting transfers between devices  22.7 us (35%)
  Pallas kernels  6.54 us (10%)
  local copies, waits for them, and re-layouts  5.78 us (9%)
  other arithmetic  3.26 us (5%)
  between operations  0.77 us (1%)
    ppermute x1, waiting for transfers between devices, paired_device(): query_came = lax.ppermute(query_send, 'head', swap)  6.64 us
    pallas_call x1, Pallas kernels, attention(): pl.pallas_call(functools.partial(attention_kernel, group_count, node_coun...  6.54 us
    ppermute x3, starting transfers between devices, gather_trunks(): pieces.append(lax.ppermute(trunk, 'leaf', ring_pairs(group_count, shift)))  6.01 us
    ppermute x3, waiting for transfers between devices, return_parts(): lax.ppermute(blocks[shift], 'leaf', ring_pairs(group_count, shift))  5.51 us
    unnamed x12, local copies, waits for them, and re-layouts  4.08 us
    ppermute x3, starting transfers between devices, return_parts(): lax.ppermute(blocks[shift], 'leaf', ring_pairs(group_count, shift))  3.62 us
    ppermute x3, starting transfers between devices, gather_trunks(): arrived.append(lax.ppermute(part, 'leaf', pairs))  3.17 us
    ppermute x1, starting transfers between devices, paired_device(): came = lax.ppermute(jnp.where(first, pair1, pair0), 'head', swap)  3.06 us
  transfers between devices with their start and end apart: 16, of which 12 were waited for; matrix products, arithmetic and copies ran while one was open for 7% of the time, Pallas kernels for 0%

profile of v4, /device:TPU:0, one launch (start us, length us, event | category | flops | bytes accessed | tf_op | source)
XLA Modules:
  0.0 64.0 jit_solution(9267815734931411000)
XLA Ops:
  0.6 0.8 %fusion.8 = (bf16[128,128]{1,0:T(8,128)(2,1)S(1)}, bf16[128,128]{1,0:T(8,128)(2,1)S(1)}, bf16[128,128]{1,0:T(8,128)(2,1)S(1)}, bf16[128,128]{1,0:T(8,128)(2,1)S(1)}) fusion(bf16[128,256]{1,0:T(8,128)(2,1)} %param.6, bf16[128,256]{1,0:T(8,128)(2,1)} %param.7), kind=kLoop, calls=%fused_computation.49 | loop fusion | bytes 262144 | tf_op jit(solution)/shard_map/slice | solution.py:358
  1.5 3.1 %collective-permute-start.1 = (bf16[256,128]{1,0:T(8,128)(2,1)S(1)}, bf16[256,128]{1,0:T(8,128)(2,1)S(1)}, u32[]{:S(2)}, u32[]{:S(2)}) collective-permute-start(bf16[256,128]{1,0:T(8,128)(2,1)S(1)} %broadcast_select_fusion.5), channel_id=1, source_target_pairs={{0,1},{1,0},{2,3},{3,2},{4,5},{5,4},{6,7},{7,6},{8,9},{9,8},{10,11... | collective-permute-start | bytes 196616 | tf_op jit(solution)/shard_map/ppermute | solution.py:372
  4.6 2.2 %collective-permute-done.1.refs_3_ = bf16[256,128]{1,0:T(8,128)(2,1)S(1)} collective-permute-done((bf16[256,128]{1,0:T(8,128)(2,1)S(1)}, bf16[256,128]{1,0:T(8,128)(2,1)S(1)}, u32[]{:S(2)}, u32[]{:S(2)}) %collective-permute-start.1) | collective-permute-done | bytes 65568 | tf_op jit(solution)/shard_map/ppermute | solution.py:372
  6.8 0.7 %constant_dynamic-update-slice_fusion.5 = (bf16[8,256,128]{2,1,0:T(8,128)(2,1)}, bf16[256,128]{1,0:T(8,128)(2,1)S(1)}, bf16[256,128]{1,0:T(8,128)(2,1)S(1)}) fusion(bf16[256,128]{1,0:T(8,128)(2,1)S(1)} %collective-permute-done.1.refs_3_, pred[]{:T(512)S(6)} %eq.3, bf16[128,128]{1,0:T(8,128)(2,1)S(1)} %get-tuple-element.51, ...), kind=kLoop, calls=%fused_computation.33 | loop fusion | flops 327679 | bytes 393217
  7.5 2.1 %collective-permute-start.2 = (bf16[256,128]{1,0:T(8,128)(2,1)S(1)}, bf16[256,128]{1,0:T(8,128)(2,1)S(1)}, u32[]{:S(2)}, u32[]{:S(2)}) collective-permute-start(bf16[256,128]{1,0:T(8,128)(2,1)S(1)} %get-tuple-element.19), channel_id=1, source_target_pairs={{0,8},{2,10},{4,12},{6,14},{8,16},{10,18},{12,20},{14,22},{16,24},... | collective-permute-start | bytes 196616 | tf_op jit(solution)/shard_map/ppermute | solution.py:314
  9.5 2.6 %collective-permute-start.3 = (bf16[256,128]{1,0:T(8,128)(2,1)S(1)}, bf16[256,128]{1,0:T(8,128)(2,1)S(1)}, u32[]{:S(2)}, u32[]{:S(2)}) collective-permute-start(bf16[256,128]{1,0:T(8,128)(2,1)S(1)} %get-tuple-element.19), channel_id=1, source_target_pairs={{0,16},{2,18},{4,20},{6,22},{8,24},{10,26},{12,28},{14,30},{16,0},... | collective-permute-start | bytes 196616 | tf_op jit(solution)/shard_map/ppermute | solution.py:314
  12.1 1.3 %collective-permute-start.4 = (bf16[256,128]{1,0:T(8,128)(2,1)S(1)}, bf16[256,128]{1,0:T(8,128)(2,1)S(1)}, u32[]{:S(2)}, u32[]{:S(2)}) collective-permute-start(bf16[256,128]{1,0:T(8,128)(2,1)S(1)} %get-tuple-element.19), channel_id=1, source_target_pairs={{0,24},{2,26},{4,28},{6,30},{8,0},{10,2},{12,4},{14,6},{16,8},{18,... | collective-permute-start | bytes 196616 | tf_op jit(solution)/shard_map/ppermute | solution.py:314
  13.5 1.0 %collective-permute-done.2 = bf16[256,128]{1,0:T(8,128)(2,1)S(1)} collective-permute-done((bf16[256,128]{1,0:T(8,128)(2,1)S(1)}, bf16[256,128]{1,0:T(8,128)(2,1)S(1)}, u32[]{:S(2)}, u32[]{:S(2)}) %collective-permute-start.2) | collective-permute-done | bytes 65568 | tf_op jit(solution)/shard_map/ppermute | solution.py:314
  14.5 1.6 %collective-permute-start.5 = (bf16[2,256,128]{2,1,0:T(8,128)(2,1)S(1)}, bf16[2,256,128]{2,1,0:T(8,128)(2,1)S(1)}, u32[]{:S(2)}, u32[]{:S(2)}) collective-permute-start(bf16[2,256,128]{2,1,0:T(8,128)(2,1)S(1)} %pad_maximum_fusion.1), channel_id=1, source_target_pairs={{0,4},{2,6},{4,0},{6,2},{8,12},{10,14},{12,8},{14,10},{16,20},{18,... | collective-permute-start | bytes 393224 | tf_op jit(solution)/shard_map/ppermute | solution.py:324
  16.6 1.6 %collective-permute-start.6 = (bf16[2,256,128]{2,1,0:T(8,128)(2,1)S(1)}, bf16[2,256,128]{2,1,0:T(8,128)(2,1)S(1)}, u32[]{:S(2)}, u32[]{:S(2)}) collective-permute-start(bf16[2,256,128]{2,1,0:T(8,128)(2,1)S(1)} %pad_maximum_fusion.2), channel_id=1, source_target_pairs={{0,4},{2,6},{4,0},{6,2},{8,12},{10,14},{12,8},{14,10},{16,20},{18,... | collective-permute-start | bytes 393224 | tf_op jit(solution)/shard_map/ppermute | solution.py:324
  18.2 0.6 %constant_dynamic-update-slice_fusion.4 = (bf16[8,256,128]{2,1,0:T(8,128)(2,1)}, bf16[16,256,128]{2,1,0:T(8,128)(2,1)S(1)}) fusion(bf16[8,256,128]{2,1,0:T(8,128)(2,1)} %get-tuple-element.18, bf16[256,128]{1,0:T(8,128)(2,1)S(1)} %collective-permute-done.2, bf16[16,256,128]{2,1,0:T(8,128)(2,1)S(1)} %constant_dynamic-update-slice_fusion.12), kind=kLoop, calls=%fused_computation.32 | loop fusion | bytes 196608
  18.8 0.6 %constant_dynamic-update-slice_fusion.3 = (bf16[8,256,128]{2,1,0:T(8,128)(2,1)}, bf16[16,256,128]{2,1,0:T(8,128)(2,1)S(1)}) fusion(bf16[8,256,128]{2,1,0:T(8,128)(2,1)} %get-tuple-element.45, bf16[256,128]{1,0:T(8,128)(2,1)S(1)} %collective-permute-done.3, bf16[16,256,128]{2,1,0:T(8,128)(2,1)S(1)} %get-tuple-element.46), kind=kLoop, calls=%fused_computation.31 | loop fusion | bytes 196608
  20.1 0.7 %constant_dynamic-update-slice_fusion.1 = (bf16[8,256,128]{2,1,0:T(8,128)(2,1)}, bf16[16,256,128]{2,1,0:T(8,128)(2,1)S(1)}) fusion(bf16[8,256,128]{2,1,0:T(8,128)(2,1)} %get-tuple-element.41, bf16[2,256,128]{2,1,0:T(8,128)(2,1)S(1)} %collective-permute-done.5, bf16[16,256,128]{2,1,0:T(8,128)(2,1)S(1)} %get-tuple-element.42), kind=kLoop, calls=%fused_computation.29 | loop fusion | bytes 393216
  20.8 0.8 %collective-permute-done.6 = bf16[2,256,128]{2,1,0:T(8,128)(2,1)S(1)} collective-permute-done((bf16[2,256,128]{2,1,0:T(8,128)(2,1)S(1)}, bf16[2,256,128]{2,1,0:T(8,128)(2,1)S(1)}, u32[]{:S(2)}, u32[]{:S(2)}) %collective-permute-start.6) | collective-permute-done | bytes 131104 | tf_op jit(solution)/shard_map/ppermute | solution.py:324
  21.6 0.7 %constant_dynamic-update-slice_fusion = (bf16[8,256,128]{2,1,0:T(8,128)(2,1)}, bf16[16,256,128]{2,1,0:T(8,128)(2,1)S(1)}) fusion(bf16[8,256,128]{2,1,0:T(8,128)(2,1)} %get-tuple-element.35, bf16[2,256,128]{2,1,0:T(8,128)(2,1)S(1)} %collective-permute-done.6, bf16[16,256,128]{2,1,0:T(8,128)(2,1)S(1)} %get-tuple-element.36), kind=kLoop, calls=%fused_computation.28 | loop fusion | bytes 393216 | tf_op jit(solution)/shard_map/concatenate | solution.py:325
  22.4 1.6 %collective-permute-start = (bf16[128,1024]{1,0:T(8,128)(2,1)S(1)}, bf16[128,1024]{1,0:T(8,128)(2,1)S(1)}, u32[]{:S(2)}, u32[]{:S(2)}) collective-permute-start(bf16[128,1024]{1,0:T(8,128)(2,1)S(1)} %get-tuple-element.29), channel_id=1, source_target_pairs={{0,1},{1,0},{2,3},{3,2},{4,5},{5,4},{6,7},{7,6},{8,9},{9,8},{10,11... | collective-permute-start | bytes 786440 | tf_op jit(solution)/shard_map/ppermute | solution.py:379
  24.5 6.6 %collective-permute-done.refs_1_ = bf16[128,1024]{1,0:T(8,128)(2,1)S(1)} collective-permute-done((bf16[128,1024]{1,0:T(8,128)(2,1)S(1)}, bf16[128,1024]{1,0:T(8,128)(2,1)S(1)}, u32[]{:S(2)}, u32[]{:S(2)}) %collective-permute-start) | collective-permute-done | bytes 262176 | tf_op jit(solution)/shard_map/ppermute | solution.py:379
  31.2 0.7 %copy-done = s32[16]{0:T(128)S(1)} copy-done((s32[16]{0:T(128)S(1)}, s32[16]{0:T(128)}, u32[]{:S(2)}) %copy-start) | copy-done | bytes 88
  31.8 6.5 %shard_map.84 = (bf16[256,1024]{1,0:T(8,128)(2,1)S(1)}, bf16[128,1024]{1,0:T(8,128)(2,1)S(1)}, bf16[128,1024]{1,0:T(8,128)(2,1)S(1)}, f32[2,256,128]{2,1,0:T(8,1...) custom-call(s32[16]{0:T(128)S(1)} %copy-done, s32[3]{0:T(128)S(1)} %pad_add_fusion.place_ref, ...), custom_call_target="tpu_custom_call" | custom-call | flops 2818572288 | bytes 8388608 | tf_op jit(solution)/shard_map/pallas_call | solution.py:268
  38.5 1.9 %collective-permute-done.9 = bf16[8,256,128]{2,1,0:T(8,128)(2,1)S(1)} collective-permute-done((bf16[8,256,128]{2,1,0:T(8,128)(2,1)S(1)}, bf16[8,256,128]{2,1,0:T(8,128)(2,1)S(1)}, u32[]{:S(2)}, u32[]{:S(2)}) %collective-permute-start.9) | collective-permute-done | bytes 524320 | tf_op jit(solution)/shard_map/ppermute | solution.py:345
  40.5 1.6 %collective-permute-start.10 = (bf16[2,256,128]{2,1,0:T(8,128)(2,1)S(1)}, bf16[2,256,128]{2,1,0:T(8,128)(2,1)S(1)}, u32[]{:S(2)}, u32[]{:S(2)}) collective-permute-start(bf16[2,256,128]{2,1,0:T(8,128)(2,1)S(1)} %get-tuple-element.23), channel_id=1, source_target_pairs={{0,4},{2,6},{4,0},{6,2},{8,12},{10,14},{12,8},{14,10},{16,20},{18,... | collective-permute-start | bytes 393224 | tf_op jit(solution)/shard_map/ppermute | solution.py:341
  42.6 1.5 %collective-permute-start.8 = (bf16[128,1024]{1,0:T(8,128)(2,1)S(1)}, bf16[128,1024]{1,0:T(8,128)(2,1)S(1)}, u32[]{:S(2)}, u32[]{:S(2)}) collective-permute-start(bf16[128,1024]{1,0:T(8,128)(2,1)S(1)} %get-tuple-element.12), channel_id=1, source_target_pairs={{0,1},{1,0},{2,3},{3,2},{4,5},{5,4},{6,7},{7,6},{8,9},{9,8},{10,11... | collective-permute-start | bytes 786440 | tf_op jit(solution)/shard_map/ppermute | solution.py:392
  44.1 0.8 %copy.20 = bf16[256,1024]{1,0:T(8,128)(2,1)} copy(bf16[256,1024]{1,0:T(8,128)(2,1)S(1)} %get-tuple-element.53) | data formatting | bytes 1048576
  44.9 2.0 %collective-permute-done.10 = bf16[2,256,128]{2,1,0:T(8,128)(2,1)S(1)} collective-permute-done((bf16[2,256,128]{2,1,0:T(8,128)(2,1)S(1)}, bf16[2,256,128]{2,1,0:T(8,128)(2,1)S(1)}, u32[]{:S(2)}, u32[]{:S(2)}) %collective-permute-start.10) | collective-permute-done | bytes 131104 | tf_op jit(solution)/shard_map/ppermute | solution.py:341
  47.0 2.0 %collective-permute-done.12 = bf16[2,256,128]{2,1,0:T(8,128)(2,1)S(1)} collective-permute-done((bf16[2,256,128]{2,1,0:T(8,128)(2,1)S(1)}, bf16[2,256,128]{2,1,0:T(8,128)(2,1)S(1)}, u32[]{:S(2)}, u32[]{:S(2)}) %collective-permute-start.12) | collective-permute-done | bytes 131104 | tf_op jit(solution)/shard_map/ppermute | solution.py:340
  49.0 0.8 %collective-permute-start.13 = (bf16[256,128]{1,0:T(8,128)(2,1)S(1)}, bf16[256,128]{1,0:T(8,128)(2,1)S(1)}, u32[]{:S(2)}, u32[]{:S(2)}) collective-permute-start(bf16[256,128]{1,0:T(8,128)(2,1)S(1)} %get-tuple-element.31), channel_id=1, source_target_pairs={{0,16},{2,18},{4,20},{6,22},{8,24},{10,26},{12,28},{14,30},{16,0},... | collective-permute-start | bytes 196616 | tf_op jit(solution)/shard_map/ppermute | solution.py:352
  49.8 2.3 %collective-permute-start.14 = (bf16[256,128]{1,0:T(8,128)(2,1)S(1)}, bf16[256,128]{1,0:T(8,128)(2,1)S(1)}, u32[]{:S(2)}, u32[]{:S(2)}) collective-permute-start(bf16[256,128]{1,0:T(8,128)(2,1)S(1)} %get-tuple-element.32), channel_id=1, source_target_pairs={{0,24},{2,26},{4,28},{6,30},{8,0},{10,2},{12,4},{14,6},{16,8},{18,... | collective-permute-start | bytes 196616 | tf_op jit(solution)/shard_map/ppermute | solution.py:352
  52.7 3.0 %collective-permute-done.13 = bf16[256,128]{1,0:T(8,128)(2,1)S(1)} collective-permute-done((bf16[256,128]{1,0:T(8,128)(2,1)S(1)}, bf16[256,128]{1,0:T(8,128)(2,1)S(1)}, u32[]{:S(2)}, u32[]{:S(2)}) %collective-permute-start.13) | collective-permute-done | bytes 65568 | tf_op jit(solution)/shard_map/ppermute | solution.py:352
  55.7 2.5 %collective-permute-done.11 = bf16[256,128]{1,0:T(8,128)(2,1)S(1)} collective-permute-done((bf16[256,128]{1,0:T(8,128)(2,1)S(1)}, bf16[256,128]{1,0:T(8,128)(2,1)S(1)}, u32[]{:S(2)}, u32[]{:S(2)}) %collective-permute-start.11) | collective-permute-done | bytes 65568 | tf_op jit(solution)/shard_map/ppermute | solution.py:352
  58.3 1.6 %collective-permute-start.15 = (bf16[256,128]{1,0:T(8,128)(2,1)S(1)}, bf16[256,128]{1,0:T(8,128)(2,1)S(1)}, u32[]{:S(2)}, u32[]{:S(2)}) collective-permute-start(bf16[256,128]{1,0:T(8,128)(2,1)S(1)} %fusion.2), channel_id=1, source_target_pairs={{0,1},{1,0},{2,3},{3,2},{4,5},{5,4},{6,7},{7,6},{8,9},{9,8},{10,11... | collective-permute-start | bytes 196616 | tf_op jit(solution)/shard_map/ppermute | solution.py:397
  59.9 0.8 %pad_maximum_fusion = bf16[128,2048]{1,0:T(8,128)(2,1)} fusion(bf16[128,1024]{1,0:T(8,128)(2,1)S(1)} %get-tuple-element.26, bf16[128,1024]{1,0:T(8,128)(2,1)S(1)} %get-tuple-element.25), kind=kLoop, calls=%fused_computation.1 | loop fusion | flops 1048576 | bytes 1048576 | tf_op jit(solution)/shard_map/concatenate | solution.py:402
  60.7 1.9 %collective-permute-done.15 = bf16[256,128]{1,0:T(8,128)(2,1)S(1)} collective-permute-done((bf16[256,128]{1,0:T(8,128)(2,1)S(1)}, bf16[256,128]{1,0:T(8,128)(2,1)S(1)}, u32[]{:S(2)}, u32[]{:S(2)}) %collective-permute-start.15) | collective-permute-done | bytes 65568 | tf_op jit(solution)/shard_map/ppermute | solution.py:397
  (37 shorter events, 4.5 us)
Async XLA Ops:
  1.5 5.3 %collective-permute-start.1 = (bf16[256,128]{1,0:T(8,128)(2,1)S(1)}, bf16[256,128]{1,0:T(8,128)(2,1)S(1)}, u32[]{:S(2)}, u32[]{:S(2)}) collective-permute-start(bf16[256,128]{1,0:T(8,128)(2,1)S(1)} %broadcast_select_fusion.5), channel_id=1, source_target_pairs={{0,1},{1,0},{2,3},{3,2},{4,5},{5,4},{6,7},{7,6},{8,9},{9,8},{10,11... | collective-permute-start | bytes 196616 | tf_op jit(solution)/shard_map/ppermute | solution.py:372
  7.5 7.0 %collective-permute-start.2 = (bf16[256,128]{1,0:T(8,128)(2,1)S(1)}, bf16[256,128]{1,0:T(8,128)(2,1)S(1)}, u32[]{:S(2)}, u32[]{:S(2)}) collective-permute-start(bf16[256,128]{1,0:T(8,128)(2,1)S(1)} %get-tuple-element.19), channel_id=1, source_target_pairs={{0,8},{2,10},{4,12},{6,14},{8,16},{10,18},{12,20},{14,22},{16,24},... | collective-permute-start | bytes 196616 | tf_op jit(solution)/shard_map/ppermute | solution.py:314
  9.5 6.6 %collective-permute-start.3 = (bf16[256,128]{1,0:T(8,128)(2,1)S(1)}, bf16[256,128]{1,0:T(8,128)(2,1)S(1)}, u32[]{:S(2)}, u32[]{:S(2)}) collective-permute-start(bf16[256,128]{1,0:T(8,128)(2,1)S(1)} %get-tuple-element.19), channel_id=1, source_target_pairs={{0,16},{2,18},{4,20},{6,22},{8,24},{10,26},{12,28},{14,30},{16,0},... | collective-permute-start | bytes 196616 | tf_op jit(solution)/shard_map/ppermute | solution.py:314
  12.1 4.5 %collective-permute-start.4 = (bf16[256,128]{1,0:T(8,128)(2,1)S(1)}, bf16[256,128]{1,0:T(8,128)(2,1)S(1)}, u32[]{:S(2)}, u32[]{:S(2)}) collective-permute-start(bf16[256,128]{1,0:T(8,128)(2,1)S(1)} %get-tuple-element.19), channel_id=1, source_target_pairs={{0,24},{2,26},{4,28},{6,30},{8,0},{10,2},{12,4},{14,6},{16,8},{18,... | collective-permute-start | bytes 196616 | tf_op jit(solution)/shard_map/ppermute | solution.py:314
  14.5 5.6 %collective-permute-start.5 = (bf16[2,256,128]{2,1,0:T(8,128)(2,1)S(1)}, bf16[2,256,128]{2,1,0:T(8,128)(2,1)S(1)}, u32[]{:S(2)}, u32[]{:S(2)}) collective-permute-start(bf16[2,256,128]{2,1,0:T(8,128)(2,1)S(1)} %pad_maximum_fusion.1), channel_id=1, source_target_pairs={{0,4},{2,6},{4,0},{6,2},{8,12},{10,14},{12,8},{14,10},{16,20},{18,... | collective-permute-start | bytes 393224 | tf_op jit(solution)/shard_map/ppermute | solution.py:324
  16.6 5.0 %collective-permute-start.6 = (bf16[2,256,128]{2,1,0:T(8,128)(2,1)S(1)}, bf16[2,256,128]{2,1,0:T(8,128)(2,1)S(1)}, u32[]{:S(2)}, u32[]{:S(2)}) collective-permute-start(bf16[2,256,128]{2,1,0:T(8,128)(2,1)S(1)} %pad_maximum_fusion.2), channel_id=1, source_target_pairs={{0,4},{2,6},{4,0},{6,2},{8,12},{10,14},{12,8},{14,10},{16,20},{18,... | collective-permute-start | bytes 393224 | tf_op jit(solution)/shard_map/ppermute | solution.py:324
  19.5 2.9 %copy-start.1 = (bf16[128,2048]{1,0:T(8,128)(2,1)S(1)}, bf16[128,2048]{1,0:T(8,128)(2,1)}, u32[]{:S(2)}) copy-start(bf16[128,2048]{1,0:T(8,128)(2,1)} %param.5) | copy-start | bytes 1572868
  22.3 2.1 %collective-permute-start.7 = (bf16[8,256,128]{2,1,0:T(8,128)(2,1)}, bf16[8,256,128]{2,1,0:T(8,128)(2,1)S(1)}, u32[]{:S(2)}, u32[]{:S(2)}) collective-permute-start(bf16[8,256,128]{2,1,0:T(8,128)(2,1)} %get-tuple-element.33), channel_id=1, source_target_pairs={{0,2},{2,0},{4,6},{6,4},{8,10},{10,8},{12,14},{14,12},{16,18},{18,... | collective-permute-start | bytes 1572872 | tf_op jit(solution)/shard_map/ppermute | solution.py:324
  22.3 1.7 %copy-start.2 = (bf16[256,1024]{1,0:T(8,128)(2,1)S(1)}, bf16[256,1024]{1,0:T(8,128)(2,1)}, u32[]{:S(2)}) copy-start(bf16[256,1024]{1,0:T(8,128)(2,1)} %param.8) | copy-start | bytes 1572868
  22.4 8.8 %collective-permute-start = (bf16[128,1024]{1,0:T(8,128)(2,1)S(1)}, bf16[128,1024]{1,0:T(8,128)(2,1)S(1)}, u32[]{:S(2)}, u32[]{:S(2)}) collective-permute-start(bf16[128,1024]{1,0:T(8,128)(2,1)S(1)} %get-tuple-element.29), channel_id=1, source_target_pairs={{0,1},{1,0},{2,3},{3,2},{4,5},{5,4},{6,7},{7,6},{8,9},{9,8},{10,11... | collective-permute-start | bytes 786440 | tf_op jit(solution)/shard_map/ppermute | solution.py:379
  31.2 0.7 %copy-start = (s32[16]{0:T(128)S(1)}, s32[16]{0:T(128)}, u32[]{:S(2)}) copy-start(s32[16]{0:T(128)} %parents_ref.1) | copy-start | bytes 196
  38.4 2.0 %collective-permute-start.9 = (bf16[8,256,128]{2,1,0:T(8,128)(2,1)S(1)}, bf16[8,256,128]{2,1,0:T(8,128)(2,1)S(1)}, u32[]{:S(2)}, u32[]{:S(2)}) collective-permute-start(bf16[8,256,128]{2,1,0:T(8,128)(2,1)S(1)} %get-tuple-element.15), channel_id=1, source_target_pairs={{0,2},{2,0},{4,6},{6,4},{8,10},{10,8},{12,14},{14,12},{16,18},{18,... | collective-permute-start | bytes 1572872 | tf_op jit(solution)/shard_map/ppermute | solution.py:345
  40.5 6.4 %collective-permute-start.10 = (bf16[2,256,128]{2,1,0:T(8,128)(2,1)S(1)}, bf16[2,256,128]{2,1,0:T(8,128)(2,1)S(1)}, u32[]{:S(2)}, u32[]{:S(2)}) collective-permute-start(bf16[2,256,128]{2,1,0:T(8,128)(2,1)S(1)} %get-tuple-element.23), channel_id=1, source_target_pairs={{0,4},{2,6},{4,0},{6,2},{8,12},{10,14},{12,8},{14,10},{16,20},{18,... | collective-permute-start | bytes 393224 | tf_op jit(solution)/shard_map/ppermute | solution.py:341
  42.1 6.8 %collective-permute-start.12 = (bf16[2,256,128]{2,1,0:T(8,128)(2,1)S(1)}, bf16[2,256,128]{2,1,0:T(8,128)(2,1)S(1)}, u32[]{:S(2)}, u32[]{:S(2)}) collective-permute-start(bf16[2,256,128]{2,1,0:T(8,128)(2,1)S(1)} %get-tuple-element.24), channel_id=1, source_target_pairs={{0,4},{2,6},{4,0},{6,2},{8,12},{10,14},{12,8},{14,10},{16,20},{18,... | collective-permute-start | bytes 393224 | tf_op jit(solution)/shard_map/ppermute | solution.py:340
  42.6 10.0 %collective-permute-start.8 = (bf16[128,1024]{1,0:T(8,128)(2,1)S(1)}, bf16[128,1024]{1,0:T(8,128)(2,1)S(1)}, u32[]{:S(2)}, u32[]{:S(2)}) collective-permute-start(bf16[128,1024]{1,0:T(8,128)(2,1)S(1)} %get-tuple-element.12), channel_id=1, source_target_pairs={{0,1},{1,0},{2,3},{3,2},{4,5},{5,4},{6,7},{7,6},{8,9},{9,8},{10,11... | collective-permute-start | bytes 786440 | tf_op jit(solution)/shard_map/ppermute | solution.py:392
  49.0 6.7 %collective-permute-start.13 = (bf16[256,128]{1,0:T(8,128)(2,1)S(1)}, bf16[256,128]{1,0:T(8,128)(2,1)S(1)}, u32[]{:S(2)}, u32[]{:S(2)}) collective-permute-start(bf16[256,128]{1,0:T(8,128)(2,1)S(1)} %get-tuple-element.31), channel_id=1, source_target_pairs={{0,16},{2,18},{4,20},{6,22},{8,24},{10,26},{12,28},{14,30},{16,0},... | collective-permute-start | bytes 196616 | tf_op jit(solution)/shard_map/ppermute | solution.py:352
  49.8 5.9 %collective-permute-start.14 = (bf16[256,128]{1,0:T(8,128)(2,1)S(1)}, bf16[256,128]{1,0:T(8,128)(2,1)S(1)}, u32[]{:S(2)}, u32[]{:S(2)}) collective-permute-start(bf16[256,128]{1,0:T(8,128)(2,1)S(1)} %get-tuple-element.32), channel_id=1, source_target_pairs={{0,24},{2,26},{4,28},{6,30},{8,0},{10,2},{12,4},{14,6},{16,8},{18,... | collective-permute-start | bytes 196616 | tf_op jit(solution)/shard_map/ppermute | solution.py:352
  52.2 6.1 %collective-permute-start.11 = (bf16[256,128]{1,0:T(8,128)(2,1)S(1)}, bf16[256,128]{1,0:T(8,128)(2,1)S(1)}, u32[]{:S(2)}, u32[]{:S(2)}) collective-permute-start(bf16[256,128]{1,0:T(8,128)(2,1)S(1)} %slice_bitcast_fusion.2), channel_id=1, source_target_pairs={{0,8},{2,10},{4,12},{6,14},{8,16},{10,18},{12,20},{14,22},{16,24},... | collective-permute-start | bytes 196616 | tf_op jit(solution)/shard_map/ppermute | solution.py:352
  58.3 4.3 %collective-permute-start.15 = (bf16[256,128]{1,0:T(8,128)(2,1)S(1)}, bf16[256,128]{1,0:T(8,128)(2,1)S(1)}, u32[]{:S(2)}, u32[]{:S(2)}) collective-permute-start(bf16[256,128]{1,0:T(8,128)(2,1)S(1)} %fusion.2), channel_id=1, source_target_pairs={{0,1},{1,0},{2,3},{3,2},{4,5},{5,4},{6,7},{7,6},{8,9},{9,8},{10,11... | collective-permute-start | bytes 196616 | tf_op jit(solution)/shard_map/ppermute | solution.py:397

commit v5 on v4

--- a/solution.py
+++ b/solution.py
@@ -64,12 +64,11 @@
     grad_refs = refs[2 * node_count : 3 * node_count]
     trunk_ref = refs[3 * node_count]
     outs = refs[3 * node_count + 1 :]
-    attended_ref = outs[0]
-    query_grad_refs = outs[1 : 1 + node_count]
-    own_grad_ref, near_ref, far_ref = outs[1 + node_count : 4 + node_count]
-    keys_s, values_s, keys_t, values_t, weight_f, weight_b, score_b, key_acc, value_acc = outs[
-        4 + node_count :
+    attended_ref, near_ref, far_ref, keys_s = outs[:4]
+    score_refs, weight_refs, scaled_refs = [
+        outs[4 + i * node_count : 4 + (i + 1) * node_count] for i in range(3)
     ]
+    values_s, values_t, weight_f, weight_b, key_acc, value_acc = outs[4 + 3 * node_count :]
     factor = scaling * math.log2(math.e)
     trunk_rows = MAX_DEPTH * NODE_TOKENS
     half = group_count // 2
@@ -96,7 +95,6 @@
         rows = slice(block * NODE_TOKENS, (block + 1) * NODE_TOKENS)
         keys_s[rows, :] = key
         values_s[rows, :] = value
-        keys_t[:, rows] = key.T
         values_t[:, rows] = value.T
 
     for level in range(MAX_DEPTH):
@@ -118,6 +116,7 @@
             self.slot = index % 2
             self.node = node
             self.first_head = first_head
+            self.number = first_head // TILE_HEADS
             self.blocks = list(range(MAX_DEPTH)) + [MAX_DEPTH + node]
             self.node_rows = pl.ds(
                 pl.multiple_of(place_ref[1 + node] * NODE_TOKENS, NODE_TOKENS), NODE_TOKENS
@@ -161,6 +160,9 @@
                 axis=1,
             )
             scaled_t = (grad_t.astype(jnp.float32) * self.inverse).astype(jnp.bfloat16)
+            score_b = score_refs[self.node]
+            scaled_refs[self.node][self.number] = scaled_t
+            weight_refs[self.node][self.number] = weight_b[self.slot, block_rows(MAX_DEPTH), :]
             trunk = slice(0, trunk_rows)
             own_block = self.blocks[-1]
             attended = dot(values_t[:, trunk], weight_b[self.slot, trunk, :], plain)
@@ -183,13 +185,13 @@
             for b, block in enumerate(self.blocks):
                 prob_grad = dot(values_s[block_rows(block), :], scaled_t, plain)
                 weight = weight_f[self.slot, block_rows(b), :]
-                score_b[self.slot, block_rows(b), :] = (weight * (prob_grad - delta)).astype(
+                score_b[self.number, block_rows(b), :] = (weight * (prob_grad - delta)).astype(
                     jnp.bfloat16
                 )
                 yield
             query = self.query()
-            for b, block in enumerate(self.blocks):
-                key_part = dot(score_b[self.slot, block_rows(b), :], query, plain)
+            for b, block in enumerate(self.blocks[:-1]):
+                key_part = dot(score_b[self.number, block_rows(b), :], query, plain)
                 value_part = dot(weight_b[self.slot, block_rows(b), :], scaled_t, contract_minor)
                 if block in started:
                     key_acc[block_rows(block), :] += key_part
@@ -199,18 +201,6 @@
                     value_acc[block_rows(block), :] = value_part
                     started.add(block)
                 yield
-            query_grad = dot(keys_t[:, trunk], score_b[self.slot, trunk, :], plain)
-            query_grad += dot(
-                keys_t[:, block_rows(own_block)],
-                score_b[self.slot, block_rows(MAX_DEPTH), :],
-                plain,
-            )
-            query_grad = (query_grad * scaling).astype(jnp.bfloat16)
-            for i in range(TILE_HEADS):
-                query_grad_refs[self.node][:, self.columns(i)] = query_grad[
-                    :, block_rows(i)
-                ].T
-            yield
 
     tiles = []
     for node in range(node_count):
@@ -225,10 +215,6 @@
                     running.remove(stream)
         before = tile.backward() if tile is not None else iter(())
 
-    for node in range(node_count):
-        rows = block_rows(MAX_DEPTH + node)
-        own_grad_ref[node, :NODE_TOKENS, :] = key_acc[rows, :] * scaling
-        own_grad_ref[node, NODE_TOKENS:, :] = value_acc[rows, :]
     near_ref[...] = jnp.zeros(near_ref.shape, near_ref.dtype)
     far_ref[...] = jnp.zeros(far_ref.shape, far_ref.dtype)
     for level in range(MAX_DEPTH):
@@ -240,6 +226,71 @@
         spot = back_spots[level]
         pl.when(valids[level] & (spot < half))(functools.partial(store, near_ref, spot))
         pl.when(valids[level] & (spot >= half))(functools.partial(store, far_ref, spot - half))
+
+
+def finish_kernel(
+    node,
+    per_key,
+    scaling,
+    query_ref,
+    keys_ref,
+    score_ref,
+    weight_ref,
+    scaled_ref,
+    query_grad_ref,
+    own_grad_ref,
+    keys_t,
+):
+    contract_minor = (((1,), (1,)), ((), ()))
+    plain = (((1,), (0,)), ((), ()))
+
+    def dot(left, right, dims):
+        return lax.dot_general(left, right, dims, preferred_element_type=jnp.float32)
+
+    def block_rows(block):
+        return slice(block * NODE_TOKENS, (block + 1) * NODE_TOKENS)
+
+    for b, block in enumerate([*range(MAX_DEPTH), MAX_DEPTH + node]):
+        keys_t[:, block_rows(b)] = keys_ref[block_rows(block), :].T
+    key_total = value_total = None
+    for number in range(per_key // TILE_HEADS):
+        columns = [
+            slice((number * TILE_HEADS + i) * HEAD_SIZE, (number * TILE_HEADS + i + 1) * HEAD_SIZE)
+            for i in range(TILE_HEADS)
+        ]
+        query = jnp.concatenate([query_ref[:, c] for c in columns], axis=0)
+        key_part = dot(score_ref[number, block_rows(MAX_DEPTH), :], query, plain)
+        value_part = dot(weight_ref[number], scaled_ref[number], contract_minor)
+        key_total = key_part if key_total is None else key_total + key_part
+        value_total = value_part if value_total is None else value_total + value_part
+        query_grad = (dot(keys_t[...], score_ref[number], plain) * scaling).astype(jnp.bfloat16)
+        for i, c in enumerate(columns):
+            query_grad_ref[:, c] = query_grad[:, block_rows(i)].T
+    own_grad_ref[:NODE_TOKENS, :] = key_total * scaling
+    own_grad_ref[NODE_TOKENS:, :] = value_total
+
+
+def finish(node, query, held, per_key, scaling):
+    keys_s, scores, weights, scaled = held
+    width = per_key * HEAD_SIZE
+    seen_rows = (MAX_DEPTH + 1) * NODE_TOKENS
+    vmem = pl.BlockSpec(memory_space=pltpu.VMEM)
+    operands = (query, keys_s, scores[node], weights[node], scaled[node])
+    pairs = per_key * NODE_TOKENS * seen_rows
+    return pl.pallas_call(
+        functools.partial(finish_kernel, node, per_key, scaling),
+        out_shape=[
+            pltpu.VMEM((NODE_TOKENS, width), jnp.bfloat16),
+            pltpu.VMEM((2 * NODE_TOKENS, HEAD_SIZE), jnp.float32),
+        ],
+        in_specs=[vmem] * len(operands),
+        out_specs=[vmem] * 2,
+        scratch_shapes=[pltpu.VMEM((HEAD_SIZE, seen_rows), jnp.bfloat16)],
+        compiler_params=pltpu.CompilerParams(vmem_limit_bytes=KERNEL_BYTES // 2),
+        cost_estimate=pl.CostEstimate(
+            flops=2 * pairs * HEAD_SIZE, transcendentals=0, bytes_accessed=2**20
+        ),
+    )(*[on_chip(a) for a in operands])
 
 
 def on_chip(array):
@@ -250,8 +301,8 @@
     node_count = len(queries)
     group_count = trunks.shape[0]
     width = per_key * HEAD_SIZE
-    block_count = MAX_DEPTH + node_count
-    held_rows = block_count * NODE_TOKENS
+    tile_count = per_key // TILE_HEADS
+    held_rows = (MAX_DEPTH + node_count) * NODE_TOKENS
     seen_rows = (MAX_DEPTH + 1) * NODE_TOKENS
     tile_rows = TILE_HEADS * NODE_TOKENS
     bf16, f32 = jnp.bfloat16, jnp.float32
@@ -259,10 +310,11 @@
     vmem = pl.BlockSpec(memory_space=pltpu.VMEM)
     half_shape = pltpu.VMEM((group_count // 2, 2 * NODE_TOKENS, HEAD_SIZE), bf16)
     out_shape = (
-        [pltpu.VMEM((node_count * NODE_TOKENS, width), bf16)]
-        + [pltpu.VMEM((NODE_TOKENS, width), bf16)] * node_count
-        + [pltpu.VMEM((node_count, 2 * NODE_TOKENS, HEAD_SIZE), f32)]
-        + [half_shape, half_shape]
+        [pltpu.VMEM((node_count * NODE_TOKENS, width), bf16), half_shape, half_shape]
+        + [pltpu.VMEM((held_rows, HEAD_SIZE), bf16)]
+        + [pltpu.VMEM((tile_count, seen_rows, tile_rows), bf16)] * node_count
+        + [pltpu.VMEM((tile_count, NODE_TOKENS, tile_rows), bf16)] * node_count
+        + [pltpu.VMEM((tile_count, HEAD_SIZE, tile_rows), bf16)] * node_count
     )
     pairs = node_count * per_key * NODE_TOKENS * seen_rows
     results = pl.pallas_call(
@@ -272,29 +324,26 @@
         out_specs=[vmem] * len(out_shape),
         scratch_shapes=[
             pltpu.VMEM((held_rows, HEAD_SIZE), bf16),
-            pltpu.VMEM((held_rows, HEAD_SIZE), bf16),
-            pltpu.VMEM((HEAD_SIZE, held_rows), bf16),
             pltpu.VMEM((HEAD_SIZE, held_rows), bf16),
             pltpu.VMEM((2, seen_rows, tile_rows), f32),
             pltpu.VMEM((2, seen_rows, tile_rows), bf16),
-            pltpu.VMEM((2, seen_rows, tile_rows), bf16),
-            pltpu.VMEM((held_rows, HEAD_SIZE), f32),
-            pltpu.VMEM((held_rows, HEAD_SIZE), f32),
+            pltpu.VMEM((MAX_DEPTH * NODE_TOKENS, HEAD_SIZE), f32),
+            pltpu.VMEM((MAX_DEPTH * NODE_TOKENS, HEAD_SIZE), f32),
         ],
         compiler_params=pltpu.CompilerParams(vmem_limit_bytes=KERNEL_BYTES),
         cost_estimate=pl.CostEstimate(
-            flops=12 * pairs * HEAD_SIZE, transcendentals=pairs, bytes_accessed=8 * 2**20
+            flops=10 * pairs * HEAD_SIZE, transcendentals=pairs, bytes_accessed=8 * 2**20
         ),
     )(
         parents,
         place,
         *[on_chip(a) for a in (*queries, *owns, *grads, trunks)],
     )
-    attended = results[0]
-    query_grads = results[1 : 1 + node_count]
-    own_grads = results[1 + node_count]
-    parts = results[2 + node_count :]
-    return attended, query_grads, own_grads, parts
+    attended, near, far, keys_s = results[:4]
+    scores, weights, scaled = [
+        results[4 + i * node_count : 4 + (i + 1) * node_count] for i in range(3)
+    ]
+    return attended, (near, far), (keys_s, scores, weights, scaled)
 
 
 def partner_pairs(count, bit):
@@ -339,7 +388,9 @@
         if far.shape[0] == ring and ring > 1:
             late = lax.ppermute(far[middle:], "leaf", pairs)
             early = lax.ppermute(far[:middle], "leaf", pairs)
-            early, late = merged(near[:middle], early), merged(near[middle:], late)
+            late = merged(near[middle:], late)
+            early, _ = lax.optimization_barrier((early, late))
+            early = merged(near[:middle], early)
             blocks = [early[i] for i in range(middle)] + [late[i] for i in range(ring - middle)]
         else:
             arrived = lax.ppermute(far, "leaf", pairs)
@@ -379,21 +430,24 @@
     query_came = lax.ppermute(query_send, "head", swap)
     trunks = gather_trunks(jnp.where(first, kept, came), group_count)
     place = jnp.stack([my_group, my_head, other]).astype(jnp.int32)
-    attended, query_grads, own_grads, (near, far) = attention(
+    query_nodes = [query_kept, query_came]
+    attended, (near, far), held = attention(
         parents,
         place,
-        [query_kept, query_came],
+        query_nodes,
         [kept, came],
         grads,
         trunks,
         per_key,
         scaling,
     )
-    query_back = lax.ppermute(query_grads[1], "head", swap)
+    query_away, own_away = finish(1, query_nodes[1], held, per_key, scaling)
+    query_here, own_here = finish(0, query_nodes[0], held, per_key, scaling)
+    query_back = lax.ppermute(query_away, "head", swap)
     total = return_parts(near, far, group_count)
     nothing = jnp.zeros_like(total)
-    mine = (own_grads[0] + jnp.where(first, total, nothing)).astype(jnp.bfloat16)
-    theirs = (own_grads[1] + jnp.where(first, nothing, total)).astype(jnp.bfloat16)
+    mine = (own_here + jnp.where(first, total, nothing)).astype(jnp.bfloat16)
+    theirs = (own_away + jnp.where(first, nothing, total)).astype(jnp.bfloat16)
     came_back = lax.ppermute(theirs, "head", swap)
     left = jnp.where(first, mine, came_back)
     right = jnp.where(first, came_back, mine)
@@ -401,8 +455,8 @@
     value_home = jnp.concatenate([left[NODE_TOKENS:], right[NODE_TOKENS:]], axis=1)
     query_home = jnp.concatenate(
         [
-            jnp.where(first, query_grads[0], query_back),
-            jnp.where(first, query_back, query_grads[0]),
+            jnp.where(first, query_here, query_back),
+            jnp.where(first, query_back, query_here),
         ],
         axis=1,
     )
@@ -424,16 +478,22 @@
     place = [my_group]
     for node in range(node_count):
         place += [zero + node]
-    attended, query_grads, own_grads, (near, far) = attention(
+    query_nodes = [query_all[s] for s in spans]
+    attended, (near, far), held = attention(
         parents,
         jnp.stack(place),
-        [query_all[s] for s in spans],
+        query_nodes,
         owns,
         [output_gradient[s] for s in spans],
         trunks,
         per_key,
         scaling,
     )
+    finished = [
+        finish(node, query, held, per_key, scaling) for node, query in enumerate(query_nodes)
+    ]
+    query_grads = [query_grad for query_grad, _ in finished]
+    own_grads = [own_grad for _, own_grad in finished]
     total = return_parts(near, far, group_count)
     grads = [own_grads[0] + total] + [own_grads[node] for node in range(1, node_count)]
     key_grad = jnp.concatenate([g[:NODE_TOKENS] for g in grads], axis=0).astype(jnp.bfloat16)

time: 64.2 us -> 65.9 us (1.026)
  waiting for transfers between devices: 24.9 us -> 27.6 us
  starting transfers between devices: 22.7 us -> 20.9 us
  Pallas kernels: 6.54 us -> 7.91 us
    ppermute x3, waiting for transfers between devices: 1.48 us -> 4.15 us  [gather_trunks(): pieces.append(lax.ppermute(trunk, 'leaf', ring_pairs(group_count, shift)))]
    ppermute x3, waiting for transfers between devices: 5.51 us -> 2.95 us  [return_parts(): lax.ppermute(blocks[shift], 'leaf', ring_pairs(group_count, shift))]
    ppermute x1, waiting for transfers between devices: 2.02 us -> 4.23 us  [return_parts(): early = lax.ppermute(far[:middle], 'leaf', pairs)]
    ppermute x1, waiting for transfers between devices: 1.98 us -> 0.01 us  [return_parts(): late = lax.ppermute(far[middle:], 'leaf', pairs)]
    ppermute x3, waiting for transfers between devices: 1.22 us -> 2.6 us  [gather_trunks(): arrived.append(lax.ppermute(part, 'leaf', pairs))]
    pallas_call x0 -> x2, Pallas kernels: none -> 1.36 us  [finish(): pl.pallas_call(functools.partial(finish_kernel, node, per_key, scaling),...]
    ppermute x1, starting transfers between devices: 1.59 us -> 0.57 us  [paired_device(): came_back = lax.ppermute(theirs, 'head', swap)]
    ppermute x1, waiting for transfers between devices: 1.92 us -> 2.93 us  [paired_device(): came_back = lax.ppermute(theirs, 'head', swap)]
  transfers between devices with their start and end apart: 16 -> 16, of which waited for: 12 -> 11; matrix products, arithmetic and copies ran while one was open for 7% -> 7% of each run, Pallas kernels for 0% -> 2%
where the time goes in v5:
time: 65.9 us; the launch traced here: 65.7 us
  waiting for transfers between devices  27.6 us (42%)
  starting transfers between devices  20.9 us (32%)
  Pallas kernels  7.91 us (12%)
  local copies, waits for them, and re-layouts  5.18 us (8%)
  other arithmetic  3.27 us (5%)
  between operations  0.82 us (1%)
    ppermute x1, waiting for transfers between devices, paired_device(): query_came = lax.ppermute(query_send, 'head', swap)  6.63 us
    pallas_call x1, Pallas kernels, attention(): pl.pallas_call(functools.partial(attention_kernel, group_count, node_coun...  6.55 us
    ppermute x3, starting transfers between devices, gather_trunks(): pieces.append(lax.ppermute(trunk, 'leaf', ring_pairs(group_count, shift)))  5.12 us
    ppermute x3, starting transfers between devices, return_parts(): lax.ppermute(blocks[shift], 'leaf', ring_pairs(group_count, shift))  4.32 us
    ppermute x1, waiting for transfers between devices, return_parts(): early = lax.ppermute(far[:middle], 'leaf', pairs)  4.23 us
    ppermute x3, waiting for transfers between devices, gather_trunks(): pieces.append(lax.ppermute(trunk, 'leaf', ring_pairs(group_count, shift)))  4.15 us
    unnamed x12, local copies, waits for them, and re-layouts  3.43 us
    ppermute x1, starting transfers between devices, paired_device(): came = lax.ppermute(jnp.where(first, pair1, pair0), 'head', swap)  3.06 us
  transfers between devices with their start and end apart: 16, of which 11 were waited for; matrix products, arithmetic and copies ran while one was open for 7% of the time, Pallas kernels for 2%

profile of v5, /device:TPU:0, one launch (start us, length us, event | category | flops | bytes accessed | tf_op | source)
XLA Modules:
  0.0 65.7 jit_solution(12909010042211798654)
XLA Ops:
  0.6 0.9 %fusion.5 = (bf16[128,128]{1,0:T(8,128)(2,1)S(1)}, bf16[128,128]{1,0:T(8,128)(2,1)S(1)}, bf16[128,128]{1,0:T(8,128)(2,1)S(1)}, bf16[128,128]{1,0:T(8,128)(2,1)S(1)}) fusion(bf16[128,256]{1,0:T(8,128)(2,1)} %param.6, bf16[128,256]{1,0:T(8,128)(2,1)} %param.7), kind=kLoop, calls=%fused_computation.47 | loop fusion | bytes 262144 | tf_op jit(solution)/shard_map/slice | solution.py:409
  1.6 3.1 %collective-permute-start.1 = (bf16[256,128]{1,0:T(8,128)(2,1)S(1)}, bf16[256,128]{1,0:T(8,128)(2,1)S(1)}, u32[]{:S(2)}, u32[]{:S(2)}) collective-permute-start(bf16[256,128]{1,0:T(8,128)(2,1)S(1)} %broadcast_select_fusion.5), channel_id=1, source_target_pairs={{0,1},{1,0},{2,3},{3,2},{4,5},{5,4},{6,7},{7,6},{8,9},{9,8},{10,11... | collective-permute-start | bytes 196616 | tf_op jit(solution)/shard_map/ppermute | solution.py:423
  4.6 2.2 %collective-permute-done.1.refs_3_ = bf16[256,128]{1,0:T(8,128)(2,1)S(1)} collective-permute-done((bf16[256,128]{1,0:T(8,128)(2,1)S(1)}, bf16[256,128]{1,0:T(8,128)(2,1)S(1)}, u32[]{:S(2)}, u32[]{:S(2)}) %collective-permute-start.1) | collective-permute-done | bytes 65568 | tf_op jit(solution)/shard_map/ppermute | solution.py:423
  6.9 0.7 %constant_dynamic-update-slice_fusion.5 = (bf16[8,256,128]{2,1,0:T(8,128)(2,1)}, bf16[256,128]{1,0:T(8,128)(2,1)S(1)}, bf16[256,128]{1,0:T(8,128)(2,1)S(1)}) fusion(bf16[256,128]{1,0:T(8,128)(2,1)S(1)} %collective-permute-done.1.refs_3_, pred[]{:T(512)S(6)} %eq.3, bf16[128,128]{1,0:T(8,128)(2,1)S(1)} %get-tuple-element.67, ...), kind=kLoop, calls=%fused_computation.31 | loop fusion | flops 327679 | bytes 393217
  7.5 4.1 %collective-permute-start.4 = (bf16[256,128]{1,0:T(8,128)(2,1)S(1)}, bf16[256,128]{1,0:T(8,128)(2,1)S(1)}, u32[]{:S(2)}, u32[]{:S(2)}) collective-permute-start(bf16[256,128]{1,0:T(8,128)(2,1)S(1)} %get-tuple-element.37), channel_id=1, source_target_pairs={{0,24},{2,26},{4,28},{6,30},{8,0},{10,2},{12,4},{14,6},{16,8},{18,... | collective-permute-start | bytes 196616 | tf_op jit(solution)/shard_map/ppermute | solution.py:363
  11.6 1.0 %collective-permute-start.2 = (bf16[256,128]{1,0:T(8,128)(2,1)S(1)}, bf16[256,128]{1,0:T(8,128)(2,1)S(1)}, u32[]{:S(2)}, u32[]{:S(2)}) collective-permute-start(bf16[256,128]{1,0:T(8,128)(2,1)S(1)} %get-tuple-element.37), channel_id=1, source_target_pairs={{0,8},{2,10},{4,12},{6,14},{8,16},{10,18},{12,20},{14,22},{16,24},... | collective-permute-start | bytes 196616 | tf_op jit(solution)/shard_map/ppermute | solution.py:363
  12.7 0.9 %collective-permute-done.4 = bf16[256,128]{1,0:T(8,128)(2,1)S(1)} collective-permute-done((bf16[256,128]{1,0:T(8,128)(2,1)S(1)}, bf16[256,128]{1,0:T(8,128)(2,1)S(1)}, u32[]{:S(2)}, u32[]{:S(2)}) %collective-permute-start.4) | collective-permute-done | bytes 65568 | tf_op jit(solution)/shard_map/ppermute | solution.py:363
  13.5 3.3 %collective-permute-done.3 = bf16[256,128]{1,0:T(8,128)(2,1)S(1)} collective-permute-done((bf16[256,128]{1,0:T(8,128)(2,1)S(1)}, bf16[256,128]{1,0:T(8,128)(2,1)S(1)}, u32[]{:S(2)}, u32[]{:S(2)}) %collective-permute-start.3) | collective-permute-done | bytes 65568 | tf_op jit(solution)/shard_map/ppermute | solution.py:363
  16.8 1.6 %collective-permute-start.6 = (bf16[2,256,128]{2,1,0:T(8,128)(2,1)S(1)}, bf16[2,256,128]{2,1,0:T(8,128)(2,1)S(1)}, u32[]{:S(2)}, u32[]{:S(2)}) collective-permute-start(bf16[2,256,128]{2,1,0:T(8,128)(2,1)S(1)} %pad_maximum_fusion.2), channel_id=1, source_target_pairs={{0,4},{2,6},{4,0},{6,2},{8,12},{10,14},{12,8},{14,10},{16,20},{18,... | collective-permute-start | bytes 393224 | tf_op jit(solution)/shard_map/ppermute | solution.py:373
  18.4 0.9 %collective-permute-start.5 = (bf16[2,256,128]{2,1,0:T(8,128)(2,1)S(1)}, bf16[2,256,128]{2,1,0:T(8,128)(2,1)S(1)}, u32[]{:S(2)}, u32[]{:S(2)}) collective-permute-start(bf16[2,256,128]{2,1,0:T(8,128)(2,1)S(1)} %pad_maximum_fusion.1), channel_id=1, source_target_pairs={{0,4},{2,6},{4,0},{6,2},{8,12},{10,14},{12,8},{14,10},{16,20},{18,... | collective-permute-start | bytes 393224 | tf_op jit(solution)/shard_map/ppermute | solution.py:373
  19.3 0.6 constant_dynamic-update-slice_fusion.4
  19.9 0.6 constant_dynamic-update-slice_fusion.3
  21.2 2.2 %collective-permute-done.5 = bf16[2,256,128]{2,1,0:T(8,128)(2,1)S(1)} collective-permute-done((bf16[2,256,128]{2,1,0:T(8,128)(2,1)S(1)}, bf16[2,256,128]{2,1,0:T(8,128)(2,1)S(1)}, u32[]{:S(2)}, u32[]{:S(2)}) %collective-permute-start.5) | collective-permute-done | bytes 131104 | tf_op jit(solution)/shard_map/ppermute | solution.py:373
  23.4 0.7 %constant_dynamic-update-slice_fusion.1 = (bf16[8,256,128]{2,1,0:T(8,128)(2,1)}, bf16[16,256,128]{2,1,0:T(8,128)(2,1)S(1)}) fusion(bf16[8,256,128]{2,1,0:T(8,128)(2,1)} %get-tuple-element.57, bf16[2,256,128]{2,1,0:T(8,128)(2,1)S(1)} %collective-permute-done.5, bf16[16,256,128]{2,1,0:T(8,128)(2,1)S(1)} %get-tuple-element.58), kind=kLoop, calls=%fused_computation.27 | loop fusion | bytes 393216
  24.1 0.7 %constant_dynamic-update-slice_fusion = (bf16[8,256,128]{2,1,0:T(8,128)(2,1)}, bf16[16,256,128]{2,1,0:T(8,128)(2,1)S(1)}) fusion(bf16[8,256,128]{2,1,0:T(8,128)(2,1)} %get-tuple-element.51, bf16[2,256,128]{2,1,0:T(8,128)(2,1)S(1)} %collective-permute-done.6, bf16[16,256,128]{2,1,0:T(8,128)(2,1)S(1)} %get-tuple-element.52), kind=kLoop, calls=%fused_computation.26 | loop fusion | bytes 393216 | tf_op jit(solution)/shard_map/concatenate | solution.py:374
  24.9 1.6 %collective-permute-start = (bf16[128,1024]{1,0:T(8,128)(2,1)S(1)}, bf16[128,1024]{1,0:T(8,128)(2,1)S(1)}, u32[]{:S(2)}, u32[]{:S(2)}) collective-permute-start(bf16[128,1024]{1,0:T(8,128)(2,1)S(1)} %get-tuple-element.45), channel_id=1, source_target_pairs={{0,1},{1,0},{2,3},{3,2},{4,5},{5,4},{6,7},{7,6},{8,9},{9,8},{10,11... | collective-permute-start | bytes 786440 | tf_op jit(solution)/shard_map/ppermute | solution.py:430
  27.0 6.6 %collective-permute-done.refs_1_.query_ref = bf16[128,1024]{1,0:T(8,128)(2,1)S(1)} collective-permute-done((bf16[128,1024]{1,0:T(8,128)(2,1)S(1)}, bf16[128,1024]{1,0:T(8,128)(2,1)S(1)}, u32[]{:S(2)}, u32[]{:S(2)}) %collective-permute-start) | collective-permute-done | bytes 262176 | tf_op jit(solution)/shard_map/ppermute | solution.py:430
  33.7 6.5 %shard_map.84 = (bf16[256,1024]{1,0:T(8,128)(2,1)S(1)}, bf16[8,256,128]{2,1,0:T(8,128)(2,1)S(1)}, bf16[8,256,128]{2,1,0:T(8,128)(2,1)S(1)}, bf16[1024,128]{1,0:T...) custom-call(s32[16]{0:T(128)S(1)} %copy-done, ...), custom_call_target="tpu_custom_call" | custom-call | flops 2348810240 | bytes 8388608 | tf_op jit(solution)/shard_map/pallas_call | solution.py:320
  40.3 1.9 %collective-permute-done.9 = bf16[8,256,128]{2,1,0:T(8,128)(2,1)S(1)} collective-permute-done((bf16[8,256,128]{2,1,0:T(8,128)(2,1)S(1)}, bf16[8,256,128]{2,1,0:T(8,128)(2,1)S(1)}, u32[]{:S(2)}, u32[]{:S(2)}) %collective-permute-start.9) | collective-permute-done | bytes 524320 | tf_op jit(solution)/shard_map/ppermute | solution.py:396
  42.4 1.4 %collective-permute-start.11 = (bf16[2,256,128]{2,1,0:T(8,128)(2,1)S(1)}, bf16[2,256,128]{2,1,0:T(8,128)(2,1)S(1)}, u32[]{:S(2)}, u32[]{:S(2)}) collective-permute-start(bf16[2,256,128]{2,1,0:T(8,128)(2,1)S(1)} %get-tuple-element.40), channel_id=1, source_target_pairs={{0,4},{2,6},{4,0},{6,2},{8,12},{10,14},{12,8},{14,10},{16,20},{18,... | collective-permute-start | bytes 393224 | tf_op jit(solution)/shard_map/ppermute | solution.py:389
  43.8 0.8 %copy.20 = bf16[256,1024]{1,0:T(8,128)(2,1)} copy(bf16[256,1024]{1,0:T(8,128)(2,1)S(1)} %get-tuple-element.69) | data formatting | bytes 1048576
  44.5 0.7 %shard_map.86 = (bf16[128,1024]{1,0:T(8,128)(2,1)S(1)}, f32[256,128]{1,0:T(8,128)S(1)}) custom-call(bf16[128,1024]{1,0:T(8,128)(2,1)S(1)} %collective-permute-done.refs_1_.query_ref, bf16[1024,128]{1,0:T(8,128)(2,1)S(1)} %get-tuple-element.20.keys_ref, bf16[4,896,256]{2,1,0:T(8,128)(2,1)S(1)} %get-tuple-element.25.score_ref, ...), custom_call_target="tpu_custom_call" | custom-call | flops 234881024 | bytes 1048576 | tf_op jit(solution)/shard_map/pallas_call | solution.py:280
  45.2 1.6 %collective-permute-start.8 = (bf16[128,1024]{1,0:T(8,128)(2,1)S(1)}, bf16[128,1024]{1,0:T(8,128)(2,1)S(1)}, u32[]{:S(2)}, u32[]{:S(2)}) collective-permute-start(bf16[128,1024]{1,0:T(8,128)(2,1)S(1)} %get-tuple-element.28), channel_id=1, source_target_pairs={{0,1},{1,0},{2,3},{3,2},{4,5},{5,4},{6,7},{7,6},{8,9},{9,8},{10,11... | collective-permute-start | bytes 786440 | tf_op jit(solution)/shard_map/ppermute | solution.py:446
  46.8 0.7 %shard_map.85 = (bf16[128,1024]{1,0:T(8,128)(2,1)S(1)}, f32[256,128]{1,0:T(8,128)S(1)}) custom-call(bf16[128,1024]{1,0:T(8,128)(2,1)S(1)} %get-tuple-element.46.refs_0_.query_ref, bf16[1024,128]{1,0:T(8,128)(2,1)S(1)} %get-tuple-element.20.keys_ref, bf16[4,896,256]{2,1,0:T(8,128)(2,1)S(1)} %get-tuple-element.21.score_ref, ...), custom_call_target="tpu_custom_call" | custom-call | flops 234881024 | bytes 1048576 | tf_op jit(solution)/shard_map/pallas_call | solution.py:280
  47.5 0.8 %collective-permute-start.10 = (bf16[2,256,128]{2,1,0:T(8,128)(2,1)S(1)}, bf16[2,256,128]{2,1,0:T(8,128)(2,1)S(1)}, u32[]{:S(2)}, u32[]{:S(2)}) collective-permute-start(bf16[2,256,128]{2,1,0:T(8,128)(2,1)S(1)} %get-tuple-element.39), channel_id=1, source_target_pairs={{0,4},{2,6},{4,0},{6,2},{8,12},{10,14},{12,8},{14,10},{16,20},{18,... | collective-permute-start | bytes 393224 | tf_op jit(solution)/shard_map/ppermute | solution.py:390
  48.3 4.2 %collective-permute-done.10 = bf16[2,256,128]{2,1,0:T(8,128)(2,1)S(1)} collective-permute-done((bf16[2,256,128]{2,1,0:T(8,128)(2,1)S(1)}, bf16[2,256,128]{2,1,0:T(8,128)(2,1)S(1)}, u32[]{:S(2)}, u32[]{:S(2)}) %collective-permute-start.10) | collective-permute-done | bytes 131104 | tf_op jit(solution)/shard_map/ppermute | solution.py:390
  52.7 2.8 %collective-permute-start.13 = (bf16[256,128]{1,0:T(8,128)(2,1)S(1)}, bf16[256,128]{1,0:T(8,128)(2,1)S(1)}, u32[]{:S(2)}, u32[]{:S(2)}) collective-permute-start(bf16[256,128]{1,0:T(8,128)(2,1)S(1)} %get-tuple-element.47), channel_id=1, source_target_pairs={{0,16},{2,18},{4,20},{6,22},{8,24},{10,26},{12,28},{14,30},{16,0},... | collective-permute-start | bytes 196616 | tf_op jit(solution)/shard_map/ppermute | solution.py:403
  55.5 1.5 %collective-permute-start.14 = (bf16[256,128]{1,0:T(8,128)(2,1)S(1)}, bf16[256,128]{1,0:T(8,128)(2,1)S(1)}, u32[]{:S(2)}, u32[]{:S(2)}) collective-permute-start(bf16[256,128]{1,0:T(8,128)(2,1)S(1)} %get-tuple-element.48), channel_id=1, source_target_pairs={{0,24},{2,26},{4,28},{6,30},{8,0},{10,2},{12,4},{14,6},{16,8},{18,... | collective-permute-start | bytes 196616 | tf_op jit(solution)/shard_map/ppermute | solution.py:403
  57.0 1.8 %collective-permute-done.12 = bf16[256,128]{1,0:T(8,128)(2,1)S(1)} collective-permute-done((bf16[256,128]{1,0:T(8,128)(2,1)S(1)}, bf16[256,128]{1,0:T(8,128)(2,1)S(1)}, u32[]{:S(2)}, u32[]{:S(2)}) %collective-permute-start.12) | collective-permute-done | bytes 65568 | tf_op jit(solution)/shard_map/ppermute | solution.py:403
  58.8 1.1 %collective-permute-done.13 = bf16[256,128]{1,0:T(8,128)(2,1)S(1)} collective-permute-done((bf16[256,128]{1,0:T(8,128)(2,1)S(1)}, bf16[256,128]{1,0:T(8,128)(2,1)S(1)}, u32[]{:S(2)}, u32[]{:S(2)}) %collective-permute-start.13) | collective-permute-done | bytes 65568 | tf_op jit(solution)/shard_map/ppermute | solution.py:403
  60.6 0.8 %pad_maximum_fusion = bf16[128,2048]{1,0:T(8,128)(2,1)} fusion(bf16[128,1024]{1,0:T(8,128)(2,1)S(1)} %get-tuple-element.42, bf16[128,1024]{1,0:T(8,128)(2,1)S(1)} %get-tuple-element.41), kind=kLoop, calls=%fused_computation.1 | loop fusion | flops 1048576 | bytes 1048576 | tf_op jit(solution)/shard_map/concatenate | solution.py:456
  61.4 2.9 %collective-permute-done.15 = bf16[256,128]{1,0:T(8,128)(2,1)S(1)} collective-permute-done((bf16[256,128]{1,0:T(8,128)(2,1)S(1)}, bf16[256,128]{1,0:T(8,128)(2,1)S(1)}, u32[]{:S(2)}, u32[]{:S(2)}) %collective-permute-start.15) | collective-permute-done | bytes 65568 | tf_op jit(solution)/shard_map/ppermute | solution.py:451
  (40 shorter events, 3.7 us)
Async XLA Ops:
  0.6 24.2 %copy-start.1 = (bf16[128,2048]{1,0:T(8,128)(2,1)S(1)}, bf16[128,2048]{1,0:T(8,128)(2,1)}, u32[]{:S(2)}) copy-start(bf16[128,2048]{1,0:T(8,128)(2,1)} %param.5) | copy-start | bytes 1572868
  1.5 25.0 %copy-start.2 = (bf16[256,1024]{1,0:T(8,128)(2,1)S(1)}, bf16[256,1024]{1,0:T(8,128)(2,1)}, u32[]{:S(2)}) copy-start(bf16[256,1024]{1,0:T(8,128)(2,1)} %param.8) | copy-start | bytes 1572868
  1.6 5.3 %collective-permute-start.1 = (bf16[256,128]{1,0:T(8,128)(2,1)S(1)}, bf16[256,128]{1,0:T(8,128)(2,1)S(1)}, u32[]{:S(2)}, u32[]{:S(2)}) collective-permute-start(bf16[256,128]{1,0:T(8,128)(2,1)S(1)} %broadcast_select_fusion.5), channel_id=1, source_target_pairs={{0,1},{1,0},{2,3},{3,2},{4,5},{5,4},{6,7},{7,6},{8,9},{9,8},{10,11... | collective-permute-start | bytes 196616 | tf_op jit(solution)/shard_map/ppermute | solution.py:423
  7.5 6.0 %collective-permute-start.4 = (bf16[256,128]{1,0:T(8,128)(2,1)S(1)}, bf16[256,128]{1,0:T(8,128)(2,1)S(1)}, u32[]{:S(2)}, u32[]{:S(2)}) collective-permute-start(bf16[256,128]{1,0:T(8,128)(2,1)S(1)} %get-tuple-element.37), channel_id=1, source_target_pairs={{0,24},{2,26},{4,28},{6,30},{8,0},{10,2},{12,4},{14,6},{16,8},{18,... | collective-permute-start | bytes 196616 | tf_op jit(solution)/shard_map/ppermute | solution.py:363
  11.6 5.2 %collective-permute-start.3 = (bf16[256,128]{1,0:T(8,128)(2,1)S(1)}, bf16[256,128]{1,0:T(8,128)(2,1)S(1)}, u32[]{:S(2)}, u32[]{:S(2)}) collective-permute-start(bf16[256,128]{1,0:T(8,128)(2,1)S(1)} %get-tuple-element.37), channel_id=1, source_target_pairs={{0,16},{2,18},{4,20},{6,22},{8,24},{10,26},{12,28},{14,30},{16,0},... | collective-permute-start | bytes 196616 | tf_op jit(solution)/shard_map/ppermute | solution.py:363
  11.6 6.7 %collective-permute-start.2 = (bf16[256,128]{1,0:T(8,128)(2,1)S(1)}, bf16[256,128]{1,0:T(8,128)(2,1)S(1)}, u32[]{:S(2)}, u32[]{:S(2)}) collective-permute-start(bf16[256,128]{1,0:T(8,128)(2,1)S(1)} %get-tuple-element.37), channel_id=1, source_target_pairs={{0,8},{2,10},{4,12},{6,14},{8,16},{10,18},{12,20},{14,22},{16,24},... | collective-permute-start | bytes 196616 | tf_op jit(solution)/shard_map/ppermute | solution.py:363
  16.8 7.3 %collective-permute-start.6 = (bf16[2,256,128]{2,1,0:T(8,128)(2,1)S(1)}, bf16[2,256,128]{2,1,0:T(8,128)(2,1)S(1)}, u32[]{:S(2)}, u32[]{:S(2)}) collective-permute-start(bf16[2,256,128]{2,1,0:T(8,128)(2,1)S(1)} %pad_maximum_fusion.2), channel_id=1, source_target_pairs={{0,4},{2,6},{4,0},{6,2},{8,12},{10,14},{12,8},{14,10},{16,20},{18,... | collective-permute-start | bytes 393224 | tf_op jit(solution)/shard_map/ppermute | solution.py:373
  18.4 5.0 %collective-permute-start.5 = (bf16[2,256,128]{2,1,0:T(8,128)(2,1)S(1)}, bf16[2,256,128]{2,1,0:T(8,128)(2,1)S(1)}, u32[]{:S(2)}, u32[]{:S(2)}) collective-permute-start(bf16[2,256,128]{2,1,0:T(8,128)(2,1)S(1)} %pad_maximum_fusion.1), channel_id=1, source_target_pairs={{0,4},{2,6},{4,0},{6,2},{8,12},{10,14},{12,8},{14,10},{16,20},{18,... | collective-permute-start | bytes 393224 | tf_op jit(solution)/shard_map/ppermute | solution.py:373
  24.1 9.5 %copy-start = (s32[16]{0:T(128)S(1)}, s32[16]{0:T(128)}, u32[]{:S(2)}) copy-start(s32[16]{0:T(128)} %parents_ref.1) | copy-start | bytes 196
  24.8 2.1 %collective-permute-start.7 = (bf16[8,256,128]{2,1,0:T(8,128)(2,1)}, bf16[8,256,128]{2,1,0:T(8,128)(2,1)S(1)}, u32[]{:S(2)}, u32[]{:S(2)}) collective-permute-start(bf16[8,256,128]{2,1,0:T(8,128)(2,1)} %get-tuple-element.49), channel_id=1, source_target_pairs={{0,2},{2,0},{4,6},{6,4},{8,10},{10,8},{12,14},{14,12},{16,18},{18,... | collective-permute-start | bytes 1572872 | tf_op jit(solution)/shard_map/ppermute | solution.py:373
  24.9 8.8 %collective-permute-start = (bf16[128,1024]{1,0:T(8,128)(2,1)S(1)}, bf16[128,1024]{1,0:T(8,128)(2,1)S(1)}, u32[]{:S(2)}, u32[]{:S(2)}) collective-permute-start(bf16[128,1024]{1,0:T(8,128)(2,1)S(1)} %get-tuple-element.45), channel_id=1, source_target_pairs={{0,1},{1,0},{2,3},{3,2},{4,5},{5,4},{6,7},{7,6},{8,9},{9,8},{10,11... | collective-permute-start | bytes 786440 | tf_op jit(solution)/shard_map/ppermute | solution.py:430
  40.2 2.0 %collective-permute-start.9 = (bf16[8,256,128]{2,1,0:T(8,128)(2,1)S(1)}, bf16[8,256,128]{2,1,0:T(8,128)(2,1)S(1)}, u32[]{:S(2)}, u32[]{:S(2)}) collective-permute-start(bf16[8,256,128]{2,1,0:T(8,128)(2,1)S(1)} %get-tuple-element.31), channel_id=1, source_target_pairs={{0,2},{2,0},{4,6},{6,4},{8,10},{10,8},{12,14},{14,12},{16,18},{18,... | collective-permute-start | bytes 1572872 | tf_op jit(solution)/shard_map/ppermute | solution.py:396
  42.4 5.9 %collective-permute-start.11 = (bf16[2,256,128]{2,1,0:T(8,128)(2,1)S(1)}, bf16[2,256,128]{2,1,0:T(8,128)(2,1)S(1)}, u32[]{:S(2)}, u32[]{:S(2)}) collective-permute-start(bf16[2,256,128]{2,1,0:T(8,128)(2,1)S(1)} %get-tuple-element.40), channel_id=1, source_target_pairs={{0,4},{2,6},{4,0},{6,2},{8,12},{10,14},{12,8},{14,10},{16,20},{18,... | collective-permute-start | bytes 393224 | tf_op jit(solution)/shard_map/ppermute | solution.py:389
  45.2 11.7 %collective-permute-start.8 = (bf16[128,1024]{1,0:T(8,128)(2,1)S(1)}, bf16[128,1024]{1,0:T(8,128)(2,1)S(1)}, u32[]{:S(2)}, u32[]{:S(2)}) collective-permute-start(bf16[128,1024]{1,0:T(8,128)(2,1)S(1)} %get-tuple-element.28), channel_id=1, source_target_pairs={{0,1},{1,0},{2,3},{3,2},{4,5},{5,4},{6,7},{7,6},{8,9},{9,8},{10,11... | collective-permute-start | bytes 786440 | tf_op jit(solution)/shard_map/ppermute | solution.py:446
  47.5 5.0 %collective-permute-start.10 = (bf16[2,256,128]{2,1,0:T(8,128)(2,1)S(1)}, bf16[2,256,128]{2,1,0:T(8,128)(2,1)S(1)}, u32[]{:S(2)}, u32[]{:S(2)}) collective-permute-start(bf16[2,256,128]{2,1,0:T(8,128)(2,1)S(1)} %get-tuple-element.39), channel_id=1, source_target_pairs={{0,4},{2,6},{4,0},{6,2},{8,12},{10,14},{12,8},{14,10},{16,20},{18,... | collective-permute-start | bytes 393224 | tf_op jit(solution)/shard_map/ppermute | solution.py:390
  52.6 6.2 %collective-permute-start.12 = (bf16[256,128]{1,0:T(8,128)(2,1)S(1)}, bf16[256,128]{1,0:T(8,128)(2,1)S(1)}, u32[]{:S(2)}, u32[]{:S(2)}) collective-permute-start(bf16[256,128]{1,0:T(8,128)(2,1)S(1)} %slice_bitcast_fusion.2), channel_id=1, source_target_pairs={{0,8},{2,10},{4,12},{6,14},{8,16},{10,18},{12,20},{14,22},{16,24},... | collective-permute-start | bytes 196616 | tf_op jit(solution)/shard_map/ppermute | solution.py:403
  52.7 7.2 %collective-permute-start.13 = (bf16[256,128]{1,0:T(8,128)(2,1)S(1)}, bf16[256,128]{1,0:T(8,128)(2,1)S(1)}, u32[]{:S(2)}, u32[]{:S(2)}) collective-permute-start(bf16[256,128]{1,0:T(8,128)(2,1)S(1)} %get-tuple-element.47), channel_id=1, source_target_pairs={{0,16},{2,18},{4,20},{6,22},{8,24},{10,26},{12,28},{14,30},{16,0},... | collective-permute-start | bytes 196616 | tf_op jit(solution)/shard_map/ppermute | solution.py:403
  55.5 4.5 %collective-permute-start.14 = (bf16[256,128]{1,0:T(8,128)(2,1)S(1)}, bf16[256,128]{1,0:T(8,128)(2,1)S(1)}, u32[]{:S(2)}, u32[]{:S(2)}) collective-permute-start(bf16[256,128]{1,0:T(8,128)(2,1)S(1)} %get-tuple-element.48), channel_id=1, source_target_pairs={{0,24},{2,26},{4,28},{6,30},{8,0},{10,2},{12,4},{14,6},{16,8},{18,... | collective-permute-start | bytes 196616 | tf_op jit(solution)/shard_map/ppermute | solution.py:403
  60.0 4.3 %collective-permute-start.15 = (bf16[256,128]{1,0:T(8,128)(2,1)S(1)}, bf16[256,128]{1,0:T(8,128)(2,1)S(1)}, u32[]{:S(2)}, u32[]{:S(2)}) collective-permute-start(bf16[256,128]{1,0:T(8,128)(2,1)S(1)} %add_convert_fusion.3), channel_id=1, source_target_pairs={{0,1},{1,0},{2,3},{3,2},{4,5},{5,4},{6,7},{7,6},{8,9},{9,8},{10,11... | collective-permute-start | bytes 196616 | tf_op jit(solution)/shard_map/ppermute | solution.py:451

commit v6 on v5

--- a/solution.py
+++ b/solution.py
@@ -14,7 +14,7 @@
 MAX_DEPTH = 6
 
 masked_score = -1e30
-TILE_HEADS = 2
+TILE_HEADS = 4
 KERNEL_BYTES = 24 * 2**20
 
 
@@ -40,13 +40,17 @@
     return 4 if group_count % 4 == 0 else 1
 
 
+def ring_order(shift):
+    return shift % 2 * 2 + shift // 2
+
+
 def relative_spots(me, target, group_count):
     ring = ring_size(group_count)
     inner = group_count // ring
     me_ring, target_ring = me // inner, target // inner
     block = ring * reverse_bits((me % inner) ^ (target % inner), inner)
     gathered = block + (me_ring - target_ring + ring) % ring
-    returned = block + (target_ring - me_ring + ring) % ring
+    returned = block + ring_order((target_ring - me_ring + ring) % ring)
     return gathered, returned
 
 
@@ -363,15 +367,16 @@
         pieces.append(lax.ppermute(trunk, "leaf", ring_pairs(group_count, shift)))
     middle = (ring + 1) // 2
     held = jnp.stack(pieces)
+    parts = [jnp.stack(pieces[:middle]), jnp.stack(pieces[middle:])] if ring > 1 else [held]
     for stage, bit in enumerate(exchange_bits(group_count // ring)):
         pairs = partner_pairs(group_count, bit)
-        sent = [held]
-        if stage == 0 and ring > 1:
-            sent = [jnp.stack(pieces[:middle]), jnp.stack(pieces[middle:])]
         arrived = []
-        for part in sent:
+        for part in parts:
             arrived.append(lax.ppermute(part, "leaf", pairs))
+        parts = [held, jnp.concatenate(arrived, axis=0)] if stage == 0 else [held]
         held = jnp.concatenate([held, *arrived], axis=0)
+        if stage > 0:
+            parts = [held]
     return held
 
 
@@ -383,7 +388,7 @@
     ring = ring_size(group_count)
     middle = (ring + 1) // 2
     bits = exchange_bits(group_count // ring)
-    for bit in reversed(bits):
+    for stage, bit in enumerate(reversed(bits)):
         pairs = partner_pairs(group_count, bit)
         if far.shape[0] == ring and ring > 1:
             late = lax.ppermute(far[middle:], "leaf", pairs)
@@ -392,6 +397,13 @@
             early, _ = lax.optimization_barrier((early, late))
             early = merged(near[:middle], early)
             blocks = [early[i] for i in range(middle)] + [late[i] for i in range(ring - middle)]
+        elif stage == 0 and near.shape[0] > 1:
+            half = near.shape[0] // 2
+            early = lax.ppermute(far[half:], "leaf", pairs)
+            late = lax.ppermute(far[:half], "leaf", pairs)
+            far = merged(near[half:], early)
+            late, _ = lax.optimization_barrier((late, far))
+            near = merged(near[:half], late)
         else:
             arrived = lax.ppermute(far, "leaf", pairs)
             total = merged(near, arrived)
@@ -400,9 +412,36 @@
             blocks = [total[0]]
     total = blocks[0].astype(jnp.float32)
     for shift in range(1, ring):
-        arrived = lax.ppermute(blocks[shift], "leaf", ring_pairs(group_count, shift))
+        block = blocks[ring_order(shift)]
+        arrived = lax.ppermute(block, "leaf", ring_pairs(group_count, shift))
         total = total + arrived.astype(jnp.float32)
     return total
+
+
+def side_by_side_kernel(place_ref, mine_ref, came_ref, key_ref, value_ref):
+    def write(left_ref, right_ref):
+        for out_ref, rows in (
+            (key_ref, slice(0, NODE_TOKENS)),
+            (value_ref, slice(NODE_TOKENS, 2 * NODE_TOKENS)),
+        ):
+            out_ref[:, :HEAD_SIZE] = left_ref[rows, :]
+            out_ref[:, HEAD_SIZE:] = right_ref[rows, :]
+
+    first = place_ref[1] == 0
+    pl.when(first)(lambda: write(mine_ref, came_ref))
+    pl.when(jnp.logical_not(first))(lambda: write(came_ref, mine_ref))
+
+
+def side_by_side(place, mine, came):
+    vmem = pl.BlockSpec(memory_space=pltpu.VMEM)
+    shape = jax.ShapeDtypeStruct((NODE_TOKENS, 2 * HEAD_SIZE), mine.dtype)
+    return pl.pallas_call(
+        side_by_side_kernel,
+        out_shape=[shape, shape],
+        in_specs=[pl.BlockSpec(memory_space=pltpu.SMEM), vmem, vmem],
+        out_specs=[vmem, vmem],
+        compiler_params=pltpu.CompilerParams(vmem_limit_bytes=KERNEL_BYTES // 8),
+    )(place, on_chip(mine), on_chip(came))
 
 
 def pair_of(arrays, columns):
@@ -449,10 +488,7 @@
     mine = (own_here + jnp.where(first, total, nothing)).astype(jnp.bfloat16)
     theirs = (own_away + jnp.where(first, nothing, total)).astype(jnp.bfloat16)
     came_back = lax.ppermute(theirs, "head", swap)
-    left = jnp.where(first, mine, came_back)
-    right = jnp.where(first, came_back, mine)
-    key_home = jnp.concatenate([left[:NODE_TOKENS], right[:NODE_TOKENS]], axis=1)
-    value_home = jnp.concatenate([left[NODE_TOKENS:], right[NODE_TOKENS:]], axis=1)
+    key_home, value_home = side_by_side(place, mine, came_back)
     query_home = jnp.concatenate(
         [
             jnp.where(first, query_here, query_back),

time: 65.9 us -> 58.4 us (0.89)
  waiting for transfers between devices: 27.6 us -> 25.1 us
  local copies, waits for them, and re-layouts: 5.18 us -> 3.01 us
  other arithmetic: 3.27 us -> 1.37 us
  starting transfers between devices: 20.9 us -> 19.4 us
    ppermute x1, waiting for transfers between devices: 6.63 us -> 0.01 us  [paired_device(): query_came = lax.ppermute(query_send, 'head', swap)]
    ppermute x1, waiting for transfers between devices: 0.01 us -> 6.25 us  [return_parts(): late = lax.ppermute(far[middle:], 'leaf', pairs)]
    ppermute x1, waiting for transfers between devices: 4.23 us -> 0.01 us  [return_parts(): early = lax.ppermute(far[:middle], 'leaf', pairs)]
    ppermute x3 -> x4, waiting for transfers between devices: 2.6 us -> 6.55 us  [gather_trunks(): arrived.append(lax.ppermute(part, 'leaf', pairs))]
    unnamed x12 -> x11, local copies, waits for them, and re-layouts: 3.43 us -> 0.92 us
    ppermute x1, starting transfers between devices: 1.58 us -> 0.09 us  [paired_device(): query_came = lax.ppermute(query_send, 'head', swap)]
    concatenate x2 -> x1, other arithmetic: 1.28 us -> 0.02 us  [gather_trunks(): parts = [held, jnp.concatenate(arrived, axis=0)] if stage == 0 else [held]]
    pallas_call x0 -> x1, Pallas kernels: none -> 1.22 us  [side_by_side(): pl.pallas_call(side_by_side_kernel, out_shape=[shape, shape], in_specs=[p...]
  transfers between devices with their start and end apart: 16 -> 18, of which waited for: 11 -> 11; matrix products, arithmetic and copies ran while one was open for 7% -> 6% of each run, Pallas kernels for 2% -> 2%
where the time goes in v6:
time: 58.4 us; the launch traced here: 58.3 us
  waiting for transfers between devices  25.1 us (43%)
  starting transfers between devices  19.4 us (33%)
  Pallas kernels  8.46 us (14%)
  local copies, waits for them, and re-layouts  3.01 us (5%)
  other arithmetic  1.37 us (2%)
  between operations  0.88 us (2%)
    ppermute x4, waiting for transfers between devices, gather_trunks(): arrived.append(lax.ppermute(part, 'leaf', pairs))  6.55 us
    ppermute x1, waiting for transfers between devices, return_parts(): late = lax.ppermute(far[middle:], 'leaf', pairs)  6.25 us
    pallas_call x1, Pallas kernels, attention(): pl.pallas_call(functools.partial(attention_kernel, group_count, node_coun...  5.91 us
    ppermute x3, starting transfers between devices, gather_trunks(): pieces.append(lax.ppermute(trunk, 'leaf', ring_pairs(group_count, shift)))  4.96 us
    ppermute x3, waiting for transfers between devices, gather_trunks(): pieces.append(lax.ppermute(trunk, 'leaf', ring_pairs(group_count, shift)))  4.87 us
    ppermute x3, starting transfers between devices, return_parts(): arrived = lax.ppermute(block, 'leaf', ring_pairs(group_count, shift))  4.54 us
    ppermute x3, waiting for transfers between devices, return_parts(): arrived = lax.ppermute(block, 'leaf', ring_pairs(group_count, shift))  3.23 us
    ppermute x1, starting transfers between devices, paired_device(): came = lax.ppermute(jnp.where(first, pair1, pair0), 'head', swap)  3.06 us
  transfers between devices with their start and end apart: 18, of which 11 were waited for; matrix products, arithmetic and copies ran while one was open for 6% of the time, Pallas kernels for 2%

profile of v6, /device:TPU:0, one launch (start us, length us, event | category | flops | bytes accessed | tf_op | source)
XLA Modules:
  0.0 58.3 jit_solution(15139520953458161479)
XLA Ops:
  0.6 0.9 %fusion.4 = (bf16[128,128]{1,0:T(8,128)(2,1)S(1)}, bf16[128,128]{1,0:T(8,128)(2,1)S(1)}, bf16[128,128]{1,0:T(8,128)(2,1)S(1)}, bf16[128,128]{1,0:T(8,128)(2,1)S(1)}) fusion(bf16[128,256]{1,0:T(8,128)(2,1)} %param.6, bf16[128,256]{1,0:T(8,128)(2,1)} %param.7), kind=kLoop, calls=%fused_computation.40 | loop fusion | bytes 262144 | tf_op jit(solution)/shard_map/slice | solution.py:448
  1.6 3.1 %collective-permute-start.1 = (bf16[256,128]{1,0:T(8,128)(2,1)S(1)}, bf16[256,128]{1,0:T(8,128)(2,1)S(1)}, u32[]{:S(2)}, u32[]{:S(2)}) collective-permute-start(bf16[256,128]{1,0:T(8,128)(2,1)S(1)} %broadcast_select_fusion.3), channel_id=1, source_target_pairs={{0,1},{1,0},{2,3},{3,2},{4,5},{5,4},{6,7},{7,6},{8,9},{9,8},{10,11... | collective-permute-start | bytes 196616 | tf_op jit(solution)/shard_map/ppermute | solution.py:462
  4.6 1.1 %constant_dynamic-slice_fusion.2 = (bf16[128,1024]{1,0:T(8,128)(2,1)S(1)}, bf16[128,1024]{1,0:T(8,128)(2,1)S(1)}) fusion(bf16[128,2048]{1,0:T(8,128)(2,1)} %param.5, s32[]{:T(128)S(6)} %select_n.51, s32[]{:T(128)S(6)} %select_n.50), kind=kLoop, calls=%fused_computation.35 | loop fusion | bytes 1048584 | tf_op jit(solution)/shard_map/dynamic_slice | solution.py:463
  5.8 1.2 %collective-permute-done.1.refs_3_ = bf16[256,128]{1,0:T(8,128)(2,1)S(1)} collective-permute-done((bf16[256,128]{1,0:T(8,128)(2,1)S(1)}, bf16[256,128]{1,0:T(8,128)(2,1)S(1)}, u32[]{:S(2)}, u32[]{:S(2)}) %collective-permute-start.1) | collective-permute-done | bytes 65568 | tf_op jit(solution)/shard_map/ppermute | solution.py:462
  7.1 1.9 %collective-permute-start.2 = (bf16[256,128]{1,0:T(8,128)(2,1)S(1)}, bf16[256,128]{1,0:T(8,128)(2,1)S(1)}, u32[]{:S(2)}, u32[]{:S(2)}) collective-permute-start(bf16[256,128]{1,0:T(8,128)(2,1)S(1)} %get-tuple-element.41), channel_id=1, source_target_pairs={{0,8},{2,10},{4,12},{6,14},{8,16},{10,18},{12,20},{14,22},{16,24},... | collective-permute-start | bytes 196616 | tf_op jit(solution)/shard_map/ppermute | solution.py:367
  9.1 2.0 %collective-permute-start.4 = (bf16[256,128]{1,0:T(8,128)(2,1)S(1)}, bf16[256,128]{1,0:T(8,128)(2,1)S(1)}, u32[]{:S(2)}, u32[]{:S(2)}) collective-permute-start(bf16[256,128]{1,0:T(8,128)(2,1)S(1)} %get-tuple-element.41), channel_id=1, source_target_pairs={{0,24},{2,26},{4,28},{6,30},{8,0},{10,2},{12,4},{14,6},{16,8},{18,... | collective-permute-start | bytes 196616 | tf_op jit(solution)/shard_map/ppermute | solution.py:367
  11.2 1.0 %collective-permute-start.3 = (bf16[256,128]{1,0:T(8,128)(2,1)S(1)}, bf16[256,128]{1,0:T(8,128)(2,1)S(1)}, u32[]{:S(2)}, u32[]{:S(2)}) collective-permute-start(bf16[256,128]{1,0:T(8,128)(2,1)S(1)} %get-tuple-element.41), channel_id=1, source_target_pairs={{0,16},{2,18},{4,20},{6,22},{8,24},{10,26},{12,28},{14,30},{16,0},... | collective-permute-start | bytes 196616 | tf_op jit(solution)/shard_map/ppermute | solution.py:367
  12.2 2.0 %collective-permute-done.2 = bf16[256,128]{1,0:T(8,128)(2,1)S(1)} collective-permute-done((bf16[256,128]{1,0:T(8,128)(2,1)S(1)}, bf16[256,128]{1,0:T(8,128)(2,1)S(1)}, u32[]{:S(2)}, u32[]{:S(2)}) %collective-permute-start.2) | collective-permute-done | bytes 65568 | tf_op jit(solution)/shard_map/ppermute | solution.py:367
  14.2 2.9 %collective-permute-done.3 = bf16[256,128]{1,0:T(8,128)(2,1)S(1)} collective-permute-done((bf16[256,128]{1,0:T(8,128)(2,1)S(1)}, bf16[256,128]{1,0:T(8,128)(2,1)S(1)}, u32[]{:S(2)}, u32[]{:S(2)}) %collective-permute-start.3) | collective-permute-done | bytes 65568 | tf_op jit(solution)/shard_map/ppermute | solution.py:367
  17.1 1.6 %collective-permute-start.6 = (bf16[2,256,128]{2,1,0:T(8,128)(2,1)S(1)}, bf16[2,256,128]{2,1,0:T(8,128)(2,1)S(1)}, u32[]{:S(2)}, u32[]{:S(2)}) collective-permute-start(bf16[2,256,128]{2,1,0:T(8,128)(2,1)S(1)} %pad_maximum_fusion.4), channel_id=1, source_target_pairs={{0,4},{2,6},{4,0},{6,2},{8,12},{10,14},{12,8},{14,10},{16,20},{18,... | collective-permute-start | bytes 393224 | tf_op jit(solution)/shard_map/ppermute | solution.py:375
  18.7 0.5 collective-permute-start.5
  19.3 3.7 %collective-permute-done.6 = bf16[2,256,128]{2,1,0:T(8,128)(2,1)S(1)} collective-permute-done((bf16[2,256,128]{2,1,0:T(8,128)(2,1)S(1)}, bf16[2,256,128]{2,1,0:T(8,128)(2,1)S(1)}, u32[]{:S(2)}, u32[]{:S(2)}) %collective-permute-start.6) | collective-permute-done | bytes 131104 | tf_op jit(solution)/shard_map/ppermute | solution.py:375
  23.0 1.4 %collective-permute-done.5 = bf16[2,256,128]{2,1,0:T(8,128)(2,1)S(1)} collective-permute-done((bf16[2,256,128]{2,1,0:T(8,128)(2,1)S(1)}, bf16[2,256,128]{2,1,0:T(8,128)(2,1)S(1)}, u32[]{:S(2)}, u32[]{:S(2)}) %collective-permute-start.5) | collective-permute-done | bytes 131104 | tf_op jit(solution)/shard_map/ppermute | solution.py:375
  24.6 1.4 %collective-permute-done.8 = bf16[4,256,128]{2,1,0:T(8,128)(2,1)S(1)} collective-permute-done((bf16[4,256,128]{2,1,0:T(8,128)(2,1)S(1)}, bf16[4,256,128]{2,1,0:T(8,128)(2,1)S(1)}, u32[]{:S(2)}, u32[]{:S(2)}) %collective-permute-start.8) | collective-permute-done | bytes 262176 | tf_op jit(solution)/shard_map/ppermute | solution.py:375
  26.1 5.9 %shard_map.84 = (bf16[256,1024]{1,0:T(8,128)(2,1)S(1)}, bf16[8,256,128]{2,1,0:T(8,128)(2,1)S(1)}, bf16[8,256,128]{2,1,0:T(8,128)(2,1)S(1)}, bf16[1024,128]{1,0:T...) custom-call(s32[16]{0:T(128)S(1)} %copy-done, ...), custom_call_target="tpu_custom_call" | custom-call | flops 2348810240 | bytes 8388608 | tf_op jit(solution)/shard_map/pallas_call | solution.py:324
  32.3 0.8 %copy.16 = bf16[256,1024]{1,0:T(8,128)(2,1)} copy(bf16[256,1024]{1,0:T(8,128)(2,1)S(1)} %get-tuple-element.63) | data formatting | bytes 1048576
  33.1 0.7 %shard_map.86 = (bf16[128,1024]{1,0:T(8,128)(2,1)S(1)}, f32[256,128]{1,0:T(8,128)S(1)}) custom-call(bf16[128,1024]{1,0:T(8,128)(2,1)S(1)} %collective-permute-done.refs_1_.query_ref, bf16[1024,128]{1,0:T(8,128)(2,1)S(1)} %get-tuple-element.23.keys_ref, bf16[2,896,512]{2,1,0:T(8,128)(2,1)S(1)} %get-tuple-element.28.score_ref, ...), custom_call_target="tpu_custom_call" | custom-call | flops 234881024 | bytes 1048576 | tf_op jit(solution)/shard_map/pallas_call | solution.py:284
  33.7 1.1 %collective-permute-start.9 = (bf16[128,1024]{1,0:T(8,128)(2,1)S(1)}, bf16[128,1024]{1,0:T(8,128)(2,1)S(1)}, u32[]{:S(2)}, u32[]{:S(2)}) collective-permute-start(bf16[128,1024]{1,0:T(8,128)(2,1)S(1)} %get-tuple-element.31), channel_id=1, source_target_pairs={{0,1},{1,0},{2,3},{3,2},{4,5},{5,4},{6,7},{7,6},{8,9},{9,8},{10,11... | collective-permute-start | bytes 786440 | tf_op jit(solution)/shard_map/ppermute | solution.py:485
  34.9 0.7 %shard_map.85 = (bf16[128,1024]{1,0:T(8,128)(2,1)S(1)}, f32[256,128]{1,0:T(8,128)S(1)}) custom-call(bf16[128,1024]{1,0:T(8,128)(2,1)S(1)} %get-tuple-element.50.refs_0_.query_ref, bf16[1024,128]{1,0:T(8,128)(2,1)S(1)} %get-tuple-element.23.keys_ref, bf16[2,896,512]{2,1,0:T(8,128)(2,1)S(1)} %get-tuple-element.24.score_ref, ...), custom_call_target="tpu_custom_call" | custom-call | flops 234881024 | bytes 1048576 | tf_op jit(solution)/shard_map/pallas_call | solution.py:284
  35.7 0.7 %collective-permute-done.10 = bf16[4,256,128]{2,1,0:T(8,128)(2,1)S(1)} collective-permute-done((bf16[4,256,128]{2,1,0:T(8,128)(2,1)S(1)}, bf16[4,256,128]{2,1,0:T(8,128)(2,1)S(1)}, u32[]{:S(2)}, u32[]{:S(2)}) %collective-permute-start.10) | collective-permute-done | bytes 262176 | tf_op jit(solution)/shard_map/ppermute | solution.py:403
  36.3 1.4 %collective-permute-start.12 = (bf16[2,256,128]{2,1,0:T(8,128)(2,1)S(1)}, bf16[2,256,128]{2,1,0:T(8,128)(2,1)S(1)}, u32[]{:S(2)}, u32[]{:S(2)}) collective-permute-start(bf16[2,256,128]{2,1,0:T(8,128)(2,1)S(1)} %get-tuple-element.53), channel_id=1, source_target_pairs={{0,4},{2,6},{4,0},{6,2},{8,12},{10,14},{12,8},{14,10},{16,20},{18,... | collective-permute-start | bytes 393224 | tf_op jit(solution)/shard_map/ppermute | solution.py:395
  37.7 0.6 %collective-permute-start.13 = (bf16[2,256,128]{2,1,0:T(8,128)(2,1)S(1)}, bf16[2,256,128]{2,1,0:T(8,128)(2,1)S(1)}, u32[]{:S(2)}, u32[]{:S(2)}) collective-permute-start(bf16[2,256,128]{2,1,0:T(8,128)(2,1)S(1)} %get-tuple-element.54), channel_id=1, source_target_pairs={{0,4},{2,6},{4,0},{6,2},{8,12},{10,14},{12,8},{14,10},{16,20},{18,... | collective-permute-start | bytes 393224 | tf_op jit(solution)/shard_map/ppermute | solution.py:394
  38.4 6.2 %collective-permute-done.13 = bf16[2,256,128]{2,1,0:T(8,128)(2,1)S(1)} collective-permute-done((bf16[2,256,128]{2,1,0:T(8,128)(2,1)S(1)}, bf16[2,256,128]{2,1,0:T(8,128)(2,1)S(1)}, u32[]{:S(2)}, u32[]{:S(2)}) %collective-permute-start.13) | collective-permute-done | bytes 131104 | tf_op jit(solution)/shard_map/ppermute | solution.py:394
  44.8 0.7 %collective-permute-start.15 = (bf16[256,128]{1,0:T(8,128)(2,1)S(1)}, bf16[256,128]{1,0:T(8,128)(2,1)S(1)}, u32[]{:S(2)}, u32[]{:S(2)}) collective-permute-start(bf16[256,128]{1,0:T(8,128)(2,1)S(1)} %slice_bitcast_fusion.1), channel_id=1, source_target_pairs={{0,16},{2,18},{4,20},{6,22},{8,24},{10,26},{12,28},{14,30},{16,0},... | collective-permute-start | bytes 196616 | tf_op jit(solution)/shard_map/ppermute | solution.py:416
  45.5 2.2 %collective-permute-start.14 = (bf16[256,128]{1,0:T(8,128)(2,1)S(1)}, bf16[256,128]{1,0:T(8,128)(2,1)S(1)}, u32[]{:S(2)}, u32[]{:S(2)}) collective-permute-start(bf16[256,128]{1,0:T(8,128)(2,1)S(1)} %get-tuple-element.55), channel_id=1, source_target_pairs={{0,8},{2,10},{4,12},{6,14},{8,16},{10,18},{12,20},{14,22},{16,24},... | collective-permute-start | bytes 196616 | tf_op jit(solution)/shard_map/ppermute | solution.py:416
  47.6 1.7 %collective-permute-start.16 = (bf16[256,128]{1,0:T(8,128)(2,1)S(1)}, bf16[256,128]{1,0:T(8,128)(2,1)S(1)}, u32[]{:S(2)}, u32[]{:S(2)}) collective-permute-start(bf16[256,128]{1,0:T(8,128)(2,1)S(1)} %get-tuple-element.56), channel_id=1, source_target_pairs={{0,24},{2,26},{4,28},{6,30},{8,0},{10,2},{12,4},{14,6},{16,8},{18,... | collective-permute-start | bytes 196616 | tf_op jit(solution)/shard_map/ppermute | solution.py:416
  49.4 2.8 %collective-permute-done.15 = bf16[256,128]{1,0:T(8,128)(2,1)S(1)} collective-permute-done((bf16[256,128]{1,0:T(8,128)(2,1)S(1)}, bf16[256,128]{1,0:T(8,128)(2,1)S(1)}, u32[]{:S(2)}, u32[]{:S(2)}) %collective-permute-start.15) | collective-permute-done | bytes 65568 | tf_op jit(solution)/shard_map/ppermute | solution.py:416
  52.2 0.5 collective-permute-done.16
  52.7 1.2 %collective-permute-start.17 = (bf16[256,128]{1,0:T(8,128)(2,1)S(1)}, bf16[256,128]{1,0:T(8,128)(2,1)S(1)}, u32[]{:S(2)}, u32[]{:S(2)}) collective-permute-start(bf16[256,128]{1,0:T(8,128)(2,1)S(1)} %get-tuple-element.51), channel_id=1, source_target_pairs={{0,1},{1,0},{2,3},{3,2},{4,5},{5,4},{6,7},{7,6},{8,9},{9,8},{10,11... | collective-permute-start | bytes 196616 | tf_op jit(solution)/shard_map/ppermute | solution.py:490
  53.9 0.8 %pad_maximum_fusion = bf16[128,2048]{1,0:T(8,128)(2,1)} fusion(bf16[128,1024]{1,0:T(8,128)(2,1)S(1)} %get-tuple-element.46, bf16[128,1024]{1,0:T(8,128)(2,1)S(1)} %get-tuple-element.45), kind=kLoop, calls=%fused_computation | loop fusion | flops 1048576 | bytes 1048576 | tf_op jit(solution)/shard_map/concatenate | solution.py:492
  54.7 2.3 %collective-permute-done.17.came_ref = bf16[256,128]{1,0:T(8,128)(2,1)S(1)} collective-permute-done((bf16[256,128]{1,0:T(8,128)(2,1)S(1)}, bf16[256,128]{1,0:T(8,128)(2,1)S(1)}, u32[]{:S(2)}, u32[]{:S(2)}) %collective-permute-start.17) | collective-permute-done | bytes 65568 | tf_op jit(solution)/shard_map/ppermute | solution.py:490
  57.0 1.2 %shard_map.87 = (bf16[128,256]{1,0:T(8,128)(2,1)}, bf16[128,256]{1,0:T(8,128)(2,1)}) custom-call(s32[3]{0:T(128)S(1)} %pad_add_fusion.place_ref, bf16[256,128]{1,0:T(8,128)(2,1)S(1)} %get-tuple-element.52.mine_ref, bf16[256,128]{1,0:T(8,128)(2,1)S(1)} %collective-permute-done.17.came_ref), custom_call_target="tpu_custom_call" | custom-call | tf_op jit(solution)/shard_map/pallas_call | solution.py:438
  (41 shorter events, 1.3 us)
Async XLA Ops:
  0.6 5.1 %copy-start.1 = (bf16[256,1024]{1,0:T(8,128)(2,1)S(1)}, bf16[256,1024]{1,0:T(8,128)(2,1)}, u32[]{:S(2)}) copy-start(bf16[256,1024]{1,0:T(8,128)(2,1)} %param.8) | copy-start | bytes 1572868
  1.6 5.5 %collective-permute-start.1 = (bf16[256,128]{1,0:T(8,128)(2,1)S(1)}, bf16[256,128]{1,0:T(8,128)(2,1)S(1)}, u32[]{:S(2)}, u32[]{:S(2)}) collective-permute-start(bf16[256,128]{1,0:T(8,128)(2,1)S(1)} %broadcast_select_fusion.3), channel_id=1, source_target_pairs={{0,1},{1,0},{2,3},{3,2},{4,5},{5,4},{6,7},{7,6},{8,9},{9,8},{10,11... | collective-permute-start | bytes 196616 | tf_op jit(solution)/shard_map/ppermute | solution.py:462
  5.7 20.4 %collective-permute-start = (bf16[128,1024]{1,0:T(8,128)(2,1)S(1)}, bf16[128,1024]{1,0:T(8,128)(2,1)S(1)}, u32[]{:S(2)}, u32[]{:S(2)}) collective-permute-start(bf16[128,1024]{1,0:T(8,128)(2,1)S(1)} %get-tuple-element.49), channel_id=1, source_target_pairs={{0,1},{1,0},{2,3},{3,2},{4,5},{5,4},{6,7},{7,6},{8,9},{9,8},{10,11... | collective-permute-start | bytes 786440 | tf_op jit(solution)/shard_map/ppermute | solution.py:469
  7.1 19.0 %copy-start = (s32[16]{0:T(128)S(1)}, s32[16]{0:T(128)}, u32[]{:S(2)}) copy-start(s32[16]{0:T(128)} %parents_ref.1) | copy-start | bytes 196
  7.1 7.0 %collective-permute-start.2 = (bf16[256,128]{1,0:T(8,128)(2,1)S(1)}, bf16[256,128]{1,0:T(8,128)(2,1)S(1)}, u32[]{:S(2)}, u32[]{:S(2)}) collective-permute-start(bf16[256,128]{1,0:T(8,128)(2,1)S(1)} %get-tuple-element.41), channel_id=1, source_target_pairs={{0,8},{2,10},{4,12},{6,14},{8,16},{10,18},{12,20},{14,22},{16,24},... | collective-permute-start | bytes 196616 | tf_op jit(solution)/shard_map/ppermute | solution.py:367
  9.1 5.0 %collective-permute-start.4 = (bf16[256,128]{1,0:T(8,128)(2,1)S(1)}, bf16[256,128]{1,0:T(8,128)(2,1)S(1)}, u32[]{:S(2)}, u32[]{:S(2)}) collective-permute-start(bf16[256,128]{1,0:T(8,128)(2,1)S(1)} %get-tuple-element.41), channel_id=1, source_target_pairs={{0,24},{2,26},{4,28},{6,30},{8,0},{10,2},{12,4},{14,6},{16,8},{18,... | collective-permute-start | bytes 196616 | tf_op jit(solution)/shard_map/ppermute | solution.py:367
  11.2 5.9 %collective-permute-start.3 = (bf16[256,128]{1,0:T(8,128)(2,1)S(1)}, bf16[256,128]{1,0:T(8,128)(2,1)S(1)}, u32[]{:S(2)}, u32[]{:S(2)}) collective-permute-start(bf16[256,128]{1,0:T(8,128)(2,1)S(1)} %get-tuple-element.41), channel_id=1, source_target_pairs={{0,16},{2,18},{4,20},{6,22},{8,24},{10,26},{12,28},{14,30},{16,0},... | collective-permute-start | bytes 196616 | tf_op jit(solution)/shard_map/ppermute | solution.py:367
  17.1 5.9 %collective-permute-start.6 = (bf16[2,256,128]{2,1,0:T(8,128)(2,1)S(1)}, bf16[2,256,128]{2,1,0:T(8,128)(2,1)S(1)}, u32[]{:S(2)}, u32[]{:S(2)}) collective-permute-start(bf16[2,256,128]{2,1,0:T(8,128)(2,1)S(1)} %pad_maximum_fusion.4), channel_id=1, source_target_pairs={{0,4},{2,6},{4,0},{6,2},{8,12},{10,14},{12,8},{14,10},{16,20},{18,... | collective-permute-start | bytes 393224 | tf_op jit(solution)/shard_map/ppermute | solution.py:375
  18.7 5.7 %collective-permute-start.5 = (bf16[2,256,128]{2,1,0:T(8,128)(2,1)S(1)}, bf16[2,256,128]{2,1,0:T(8,128)(2,1)S(1)}, u32[]{:S(2)}, u32[]{:S(2)}) collective-permute-start(bf16[2,256,128]{2,1,0:T(8,128)(2,1)S(1)} %pad_maximum_fusion.3), channel_id=1, source_target_pairs={{0,4},{2,6},{4,0},{6,2},{8,12},{10,14},{12,8},{14,10},{16,20},{18,... | collective-permute-start | bytes 393224 | tf_op jit(solution)/shard_map/ppermute | solution.py:375
  19.2 5.4 %collective-permute-start.7 = (bf16[4,256,128]{2,1,0:T(8,128)(2,1)S(1)}, bf16[4,256,128]{2,1,0:T(8,128)(2,1)S(1)}, u32[]{:S(2)}, u32[]{:S(2)}) collective-permute-start(bf16[4,256,128]{2,1,0:T(8,128)(2,1)S(1)} %pad_maximum_fusion.1), channel_id=1, source_target_pairs={{0,2},{2,0},{4,6},{6,4},{8,10},{10,8},{12,14},{14,12},{16,18},{18,... | collective-permute-start | bytes 786440 | tf_op jit(solution)/shard_map/ppermute | solution.py:375
  24.4 1.6 %collective-permute-start.8 = (bf16[4,256,128]{2,1,0:T(8,128)(2,1)S(1)}, bf16[4,256,128]{2,1,0:T(8,128)(2,1)S(1)}, u32[]{:S(2)}, u32[]{:S(2)}) collective-permute-start(bf16[4,256,128]{2,1,0:T(8,128)(2,1)S(1)} %pad_maximum_fusion.2), channel_id=1, source_target_pairs={{0,2},{2,0},{4,6},{6,4},{8,10},{10,8},{12,14},{14,12},{16,18},{18,... | collective-permute-start | bytes 786440 | tf_op jit(solution)/shard_map/ppermute | solution.py:375
  32.0 3.5 %collective-permute-start.11 = (bf16[4,256,128]{2,1,0:T(8,128)(2,1)S(1)}, bf16[4,256,128]{2,1,0:T(8,128)(2,1)S(1)}, u32[]{:S(2)}, u32[]{:S(2)}) collective-permute-start(bf16[4,256,128]{2,1,0:T(8,128)(2,1)S(1)} %get-tuple-element.44), channel_id=1, source_target_pairs={{0,2},{2,0},{4,6},{6,4},{8,10},{10,8},{12,14},{14,12},{16,18},{18,... | collective-permute-start | bytes 786440 | tf_op jit(solution)/shard_map/ppermute | solution.py:402
  33.7 15.6 %collective-permute-start.9 = (bf16[128,1024]{1,0:T(8,128)(2,1)S(1)}, bf16[128,1024]{1,0:T(8,128)(2,1)S(1)}, u32[]{:S(2)}, u32[]{:S(2)}) collective-permute-start(bf16[128,1024]{1,0:T(8,128)(2,1)S(1)} %get-tuple-element.31), channel_id=1, source_target_pairs={{0,1},{1,0},{2,3},{3,2},{4,5},{5,4},{6,7},{7,6},{8,9},{9,8},{10,11... | collective-permute-start | bytes 786440 | tf_op jit(solution)/shard_map/ppermute | solution.py:485
  34.8 1.5 %collective-permute-start.10 = (bf16[4,256,128]{2,1,0:T(8,128)(2,1)S(1)}, bf16[4,256,128]{2,1,0:T(8,128)(2,1)S(1)}, u32[]{:S(2)}, u32[]{:S(2)}) collective-permute-start(bf16[4,256,128]{2,1,0:T(8,128)(2,1)S(1)} %get-tuple-element.43), channel_id=1, source_target_pairs={{0,2},{2,0},{4,6},{6,4},{8,10},{10,8},{12,14},{14,12},{16,18},{18,... | collective-permute-start | bytes 786440 | tf_op jit(solution)/shard_map/ppermute | solution.py:403
  36.3 8.4 %collective-permute-start.12 = (bf16[2,256,128]{2,1,0:T(8,128)(2,1)S(1)}, bf16[2,256,128]{2,1,0:T(8,128)(2,1)S(1)}, u32[]{:S(2)}, u32[]{:S(2)}) collective-permute-start(bf16[2,256,128]{2,1,0:T(8,128)(2,1)S(1)} %get-tuple-element.53), channel_id=1, source_target_pairs={{0,4},{2,6},{4,0},{6,2},{8,12},{10,14},{12,8},{14,10},{16,20},{18,... | collective-permute-start | bytes 393224 | tf_op jit(solution)/shard_map/ppermute | solution.py:395
  37.7 7.0 %collective-permute-start.13 = (bf16[2,256,128]{2,1,0:T(8,128)(2,1)S(1)}, bf16[2,256,128]{2,1,0:T(8,128)(2,1)S(1)}, u32[]{:S(2)}, u32[]{:S(2)}) collective-permute-start(bf16[2,256,128]{2,1,0:T(8,128)(2,1)S(1)} %get-tuple-element.54), channel_id=1, source_target_pairs={{0,4},{2,6},{4,0},{6,2},{8,12},{10,14},{12,8},{14,10},{16,20},{18,... | collective-permute-start | bytes 393224 | tf_op jit(solution)/shard_map/ppermute | solution.py:394
  44.8 7.4 %collective-permute-start.15 = (bf16[256,128]{1,0:T(8,128)(2,1)S(1)}, bf16[256,128]{1,0:T(8,128)(2,1)S(1)}, u32[]{:S(2)}, u32[]{:S(2)}) collective-permute-start(bf16[256,128]{1,0:T(8,128)(2,1)S(1)} %slice_bitcast_fusion.1), channel_id=1, source_target_pairs={{0,16},{2,18},{4,20},{6,22},{8,24},{10,26},{12,28},{14,30},{16,0},... | collective-permute-start | bytes 196616 | tf_op jit(solution)/shard_map/ppermute | solution.py:416
  45.5 6.7 %collective-permute-start.14 = (bf16[256,128]{1,0:T(8,128)(2,1)S(1)}, bf16[256,128]{1,0:T(8,128)(2,1)S(1)}, u32[]{:S(2)}, u32[]{:S(2)}) collective-permute-start(bf16[256,128]{1,0:T(8,128)(2,1)S(1)} %get-tuple-element.55), channel_id=1, source_target_pairs={{0,8},{2,10},{4,12},{6,14},{8,16},{10,18},{12,20},{14,22},{16,24},... | collective-permute-start | bytes 196616 | tf_op jit(solution)/shard_map/ppermute | solution.py:416
  47.6 5.0 %collective-permute-start.16 = (bf16[256,128]{1,0:T(8,128)(2,1)S(1)}, bf16[256,128]{1,0:T(8,128)(2,1)S(1)}, u32[]{:S(2)}, u32[]{:S(2)}) collective-permute-start(bf16[256,128]{1,0:T(8,128)(2,1)S(1)} %get-tuple-element.56), channel_id=1, source_target_pairs={{0,24},{2,26},{4,28},{6,30},{8,0},{10,2},{12,4},{14,6},{16,8},{18,... | collective-permute-start | bytes 196616 | tf_op jit(solution)/shard_map/ppermute | solution.py:416
  52.7 4.3 %collective-permute-start.17 = (bf16[256,128]{1,0:T(8,128)(2,1)S(1)}, bf16[256,128]{1,0:T(8,128)(2,1)S(1)}, u32[]{:S(2)}, u32[]{:S(2)}) collective-permute-start(bf16[256,128]{1,0:T(8,128)(2,1)S(1)} %get-tuple-element.51), channel_id=1, source_target_pairs={{0,1},{1,0},{2,3},{3,2},{4,5},{5,4},{6,7},{7,6},{8,9},{9,8},{10,11... | collective-permute-start | bytes 196616 | tf_op jit(solution)/shard_map/ppermute | solution.py:490
